TPU v7x, 16 devices: a whole 2x2x2 slice. The times are simulated.
16 devices in a mesh: ep: 16 (over z, y, x, core).
Axes of the slice: x: 2, y: 2, z: 2, core: 2. Of those that a mesh axis runs over, the one named last changes fastest.
Arguments:
- hidden: bfloat16 [32768, 768], P('ep')
- w_router: float32 [768, 32], replicated
- expert_ids: int32 [32768, 2], P('ep')
- w_one: bfloat16 [32, 768, 3072], P('ep')
- w_three: bfloat16 [32, 768, 3072], P('ep')
- w_two: bfloat16 [32, 3072, 768], P('ep')
Outputs:
- output: bfloat16 [32768, 768], P('ep')
All inputs are finite; a program needn't handle non-finite values.
Results may differ from a plain program's by a relative error of at most 0.0086898.
Values are sent between devices in bfloat16 or wider.
A program may use at most 1 GiB of HBM per device.

v0:
```python
import functools

import jax
import jax.numpy as jnp
from jax import lax
from jax.experimental import pallas as pl
from jax.experimental.pallas import tpu as pltpu
from jax.sharding import PartitionSpec as P


F32 = jnp.float32
BF16 = jnp.bfloat16
I32 = jnp.int32
TILE = 16
CHUNKS = ((0, 176), (176, 176), (352, 160))
VMEM_BYTES = 60 * 1024 * 1024


def _dot(a, b):
    return jnp.dot(a, b, preferred_element_type=F32)


def route_kernel(local_count, row_cap, x_ref, wr_ref, ids_ref, slot_ref, cols_ref, cnt_ref):
    tok = x_ref.shape[0]
    n_exp = wr_ref.shape[0]
    w = wr_ref[...]
    w_hi = w.astype(BF16)
    rest = w - w_hi.astype(F32)
    w_mid = rest.astype(BF16)
    w_lo = (rest - w_mid.astype(F32)).astype(BF16)
    x = x_ref[...]
    nt = (((1,), (1,)), ((), ()))
    w_all = jnp.concatenate([w_hi, w_mid, w_lo], axis=0)
    parts = lax.dot_general(w_all, x, nt, preferred_element_type=F32)
    logits = parts[:n_exp] + (parts[n_exp : 2 * n_exp] + parts[2 * n_exp :])
    ids = ids_ref[...]
    id_a, id_b = ids[0:1], ids[1:2]
    row = lax.broadcasted_iota(I32, (n_exp, tok), 0)
    oh_a, oh_b = row == id_a, row == id_b
    zero = jnp.zeros((), F32)
    l_a = jnp.sum(jnp.where(oh_a, logits, zero), axis=0, keepdims=True)
    l_b = jnp.sum(jnp.where(oh_b, logits, zero), axis=0, keepdims=True)
    top = jnp.maximum(l_a, l_b)
    e_a, e_b = jnp.exp(l_a - top), jnp.exp(l_b - top)
    g_a, g_b = e_a / (e_a + e_b), e_b / (e_a + e_b)
    chosen = jnp.where(oh_a | oh_b, 1.0, 0.0).astype(F32)
    width = 256
    tri = (lax.broadcasted_iota(I32, (width, width), 0) < lax.broadcasted_iota(I32, (width, width), 1))
    tri = jnp.where(tri, 1.0, 0.0).astype(BF16)
    before = jnp.zeros((n_exp, 1), F32)
    ranks = []
    for k in range(tok // width):
        blk = chosen[:, k * width : (k + 1) * width]
        ranks.append(_dot(blk.astype(BF16), tri) + before)
        before = before + jnp.sum(blk, axis=1, keepdims=True)
    rank = jnp.concatenate(ranks, axis=1)
    cnt_ref[...] = jnp.broadcast_to(before, cnt_ref.shape).astype(I32)

    def slot_of(ident, onehot):
        here = jnp.sum(jnp.where(onehot, rank, zero), axis=0, keepdims=True)
        dev = ident // local_count
        lower = (row < ident) & (row >= dev * local_count)
        base = jnp.sum(jnp.where(lower, jnp.broadcast_to(before, (n_exp, tok)), zero), axis=0, keepdims=True)
        return dev.astype(F32) * row_cap + here + base

    s_a, s_b = slot_of(id_a, oh_a), slot_of(id_b, oh_b)
    both = jnp.concatenate([s_a, s_b, g_a, g_b, s_a, s_b, g_a, g_b], axis=0)
    slot_ref[...] = both.astype(I32)
    cols_ref[...] = both.T


def pack_kernel(row_cap, chunks, counts_ref, slot_ref, x_ref, *refs):
    out_refs, list_ref = refs[:-1], refs[-1]
    tok = x_ref.shape[0]
    n_dev = out_refs[0].shape[0]
    for (start, size), out_ref in zip(chunks, out_refs):

        def collect(d, cnt):
            list_ref[cnt] = d
            return cnt + (counts_ref[d] > start).astype(I32)

        list_ref[n_dev] = 0
        cnt = lax.fori_loop(0, n_dev, collect, jnp.int32(0))
        last = jnp.maximum(cnt - 1, 0)

        def pair(i, _):
            d0, d1 = list_ref[2 * i], list_ref[jnp.minimum(2 * i + 1, last)]
            pos = lax.broadcasted_iota(I32, (size, tok), 0) + start
            want = jnp.concatenate([pos + d0 * row_cap, pos + d1 * row_cap], axis=0)
            hit = (want == slot_ref[0:1, :]) | (want == slot_ref[1:2, :])
            pick = jnp.where(hit, 1.0, 0.0).astype(BF16)
            rows = _dot(pick, x_ref[...]).astype(BF16)
            out_ref[d0] = rows[:size]
            out_ref[d1] = rows[size:]
            return 0

        lax.fori_loop(0, (cnt + 1) // 2, pair, 0)


WIDE = 512
STEP = 256


def ffn_kernel(start, size, n_src, bound_ref, x_ref, w1_hbm, w3_hbm, w2_hbm, out_ref, w1, w3, w2, xbuf, hbuf, ybuf, list_ref, sems):
    n_loc, _, ff = w1.shape
    n_f = ff // WIDE
    per = size // TILE

    def copy(e, which, f):
        cut = pl.ds(f * WIDE, WIDE)
        at = (e, cut) if which == 2 else (e, slice(None), cut)
        src, dst = ((w1_hbm, w1), (w3_hbm, w3), (w2_hbm, w2))[which]
        return pltpu.make_async_copy(src.at[at], dst.at[at], sems.at[e, which, f])

    counts = []
    for e in range(n_loc):

        def need(s, any_):
            lo, hi = bound_ref[e, s], bound_ref[e + 1, s]
            return any_ | ((lo < start + size) & (hi > start) & (hi > lo)).astype(I32)

        used = lax.fori_loop(0, n_src, need, jnp.int32(0))
        counts.append(used)

        @pl.when(used > 0)
        def _():
            for f in range(n_f):
                copy(e, 0, f).start()
                copy(e, 1, f).start()
            for f in range(n_f):
                copy(e, 2, f).start()

    out_ref[...] = jnp.zeros_like(out_ref)
    for e in range(n_loc):

        @pl.when(counts[e] > 0)
        def _():
            def collect(i, cnt):
                s = i // per
                t0 = start + (i % per) * TILE
                lo = bound_ref[e, s]
                hi = bound_ref[e + 1, s]
                hit = (lo < t0 + TILE) & (hi > t0) & (hi > lo)

                @pl.when(hit)
                def _():
                    list_ref[cnt] = i
                    here = pl.ds(pl.multiple_of(i * TILE, TILE), TILE)
                    xbuf[pl.ds(pl.multiple_of(cnt * TILE, TILE), TILE), :] = x_ref[here, :]

                return cnt + hit.astype(I32)

            cnt = lax.fori_loop(0, n_src * per, collect, jnp.int32(0))

            def block(g, _):
                at = pl.ds(pl.multiple_of(g * STEP, STEP), STEP)
                xb = xbuf[at, :]
                for f in range(n_f):

                    @pl.when(g == 0)
                    def _():
                        copy(e, 0, f).wait()
                        copy(e, 1, f).wait()

                    cut = slice(f * WIDE, (f + 1) * WIDE)
                    u = _dot(xb, w1[e, :, cut])
                    v = _dot(xb, w3[e, :, cut])
                    hbuf[:, cut] = (u * jax.nn.sigmoid(u) * v).astype(BF16)

                @pl.when(g == 0)
                def _():
                    for f in range(n_f):
                        copy(e, 2, f).wait()

                ybuf[at, :] = _dot(hbuf[...], w2[e]).astype(BF16)
                return 0

            lax.fori_loop(0, (cnt * TILE + STEP - 1) // STEP, block, 0)

            def put(k, _):
                i = list_ref[k]
                s = i // per
                t0 = start + (i % per) * TILE
                pos = t0 + lax.broadcasted_iota(I32, (TILE, 1), 0)
                own = (pos >= bound_ref[e, s]) & (pos < bound_ref[e + 1, s])
                at = pl.ds(pl.multiple_of(i * TILE, TILE), TILE)
                y = ybuf[pl.ds(pl.multiple_of(k * TILE, TILE), TILE), :]
                out_ref[at, :] = jnp.where(own, y, out_ref[at, :])
                return 0

            lax.fori_loop(0, cnt, put, 0)


def combine_kernel(row_cap, start, size, n_dev, has_acc, counts_ref, cols_ref, back_ref, *refs):
    if has_acc:
        acc_ref, out_ref, rows_ref, slot_ref, cnt_ref = refs
    else:
        out_ref, rows_ref, slot_ref, cnt_ref = refs

    @pl.when(pl.program_id(0) == 0)
    def _():
        slot_ref[...] = jnp.full_like(slot_ref, -1.0)

        def collect(d, cnt):
            @pl.when(counts_ref[d] > start)
            def _():
                pos = lax.broadcasted_iota(I32, (1, size), 1) + (d * row_cap + start)
                rows_ref[pl.ds(pl.multiple_of(cnt * size, TILE), size), :] = back_ref[d]
                slot_ref[cnt] = jnp.broadcast_to(pos.astype(F32), (8, size))

            return cnt + (counts_ref[d] > start).astype(I32)

        cnt = lax.fori_loop(0, n_dev, collect, jnp.int32(0))
        cnt_ref[0] = cnt

        @pl.when(cnt % 2 == 1)
        def _():
            rows_ref[pl.ds(pl.multiple_of(cnt * size, TILE), size), :] = jnp.zeros((size, rows_ref.shape[1]), BF16)

    c = cols_ref[...]
    toks, dim = out_ref.shape

    def pair(i, total):
        rows = rows_ref[pl.ds(pl.multiple_of(i * 2 * size, TILE), 2 * size), :]
        ids = jnp.concatenate([slot_ref[2 * i, 0:1], slot_ref[2 * i + 1, 0:1]], axis=1)
        for k in range(2):
            pick = jnp.where(ids == c[:, k : k + 1], 1.0, 0.0).astype(BF16)
            total = total + c[:, 2 + k : 3 + k] * _dot(pick, rows)
        return total

    first = acc_ref[...] if has_acc else jnp.zeros((toks, dim), F32)
    total = lax.fori_loop(0, (cnt_ref[0] + 1) // 2, pair, first)
    out_ref[...] = total.astype(out_ref.dtype)


def _params(**kw):
    return pltpu.CompilerParams(vmem_limit_bytes=VMEM_BYTES, **kw)


def solution(mesh):
    n = mesh.shape["ep"]

    def body(x, w_router, ids, w1, w3, w2):
        tok, dim = x.shape
        local = w1.shape[0]
        ff = w1.shape[2]
        n_exp = n * local
        cap = 4 * tok // n
        slots, cols, counts = pl.pallas_call(
            functools.partial(route_kernel, local, cap),
            out_shape=(
                jax.ShapeDtypeStruct((8, tok), I32),
                jax.ShapeDtypeStruct((tok, 8), F32),
                jax.ShapeDtypeStruct((n_exp, 128), I32),
            ),
            compiler_params=_params(),
            name="route",
        )(x, w_router.T, ids.T)
        per_exp = lax.all_to_all(counts[:, 0].reshape(n, local), "ep", 0, 0, tiled=True)
        ends = jnp.cumsum(per_exp, axis=1).T
        bounds = jnp.concatenate([jnp.zeros((1, n), I32), ends], axis=0)
        dev_counts = jnp.sum(counts[:, 0].reshape(n, local), axis=1)
        smem = pl.BlockSpec(memory_space=pltpu.SMEM)
        vmem = pl.BlockSpec(memory_space=pltpu.VMEM)
        hbm = pl.BlockSpec(memory_space=pl.ANY)
        sends = []
        for part in (CHUNKS[:1], CHUNKS[1:]):
            total = sum(size for _, size in part)
            pack = pl.pallas_call(
                functools.partial(pack_kernel, cap, part),
                in_specs=[smem, vmem, vmem],
                out_specs=[vmem] * len(part),
                out_shape=[jax.ShapeDtypeStruct((n, size, dim), BF16) for _, size in part],
                scratch_shapes=[pltpu.SMEM((n + 1,), I32)],
                compiler_params=_params(),
                cost_estimate=pl.CostEstimate(flops=2 * n * total * tok * dim, bytes_accessed=1, transcendentals=0),
            )
            sends += pack(dev_counts, slots, x)
        acc = None
        for index, (start, size) in enumerate(CHUNKS):
            got = lax.all_to_all(sends[index], "ep", 0, 0, tiled=True)
            rows = n * size
            made = pl.pallas_call(
                functools.partial(ffn_kernel, start, size, n),
                in_specs=[smem, vmem, hbm, hbm, hbm],
                out_specs=vmem,
                scratch_shapes=[
                    pltpu.VMEM((local, dim, ff), BF16),
                    pltpu.VMEM((local, dim, ff), BF16),
                    pltpu.VMEM((local, ff, dim), BF16),
                    pltpu.VMEM((rows, dim), BF16),
                    pltpu.VMEM((STEP, ff), BF16),
                    pltpu.VMEM((rows, dim), BF16),
                    pltpu.SMEM((rows // TILE,), I32),
                    pltpu.SemaphoreType.DMA((local, 3, ff // WIDE)),
                ],
                out_shape=jax.ShapeDtypeStruct((rows, dim), BF16),
                compiler_params=_params(),
                cost_estimate=pl.CostEstimate(flops=6 * rows * dim * ff, bytes_accessed=1, transcendentals=0),
            )
            made = made(bounds, got.reshape(rows, dim), w1, w3, w2)
            back = lax.all_to_all(made.reshape(n, size, dim), "ep", 0, 0, tiled=True)
            last = index == len(CHUNKS) - 1
            tb = 512
            tile_spec = pl.BlockSpec((tb, dim), lambda i, c: (i, 0))
            ins = [cols, back] + ([] if acc is None else [acc])
            specs = [pl.BlockSpec((tb, 8), lambda i, c: (i, 0)), pl.BlockSpec((n, size, dim), lambda i, c: (0, 0, 0))]
            combine = pl.pallas_call(
                functools.partial(combine_kernel, cap, start, size, n, acc is not None),
                grid_spec=pltpu.PrefetchScalarGridSpec(
                    num_scalar_prefetch=1,
                    grid=(tok // tb,),
                    in_specs=specs + ([] if acc is None else [tile_spec]),
                    out_specs=tile_spec,
                    scratch_shapes=[
                        pltpu.VMEM((rows + size, dim), BF16),
                        pltpu.VMEM((n + 1, 8, size), F32),
                        pltpu.SMEM((1,), I32),
                    ],
                ),
                out_shape=jax.ShapeDtypeStruct((tok, dim), BF16 if last else F32),
                compiler_params=_params(),
                cost_estimate=pl.CostEstimate(flops=4 * rows * tok * dim, bytes_accessed=1, transcendentals=0),
            )
            acc = combine(dev_counts, *ins)
        return acc

    return jax.shard_map(
        body,
        mesh=mesh,
        in_specs=(P("ep", None), P(None, None), P("ep", None), P("ep", None, None), P("ep", None, None), P("ep", None, None)),
        out_specs=P("ep", None),
        check_vma=False,
    )
```

profile of v0, /device:TPU:11, one launch (start us, length us, event | category | flops | bytes accessed | tf_op | source)
XLA Modules:
  0.0 490.2 jit_solution(4831431202129554842)
XLA Ops:
  0.0 4.6 route.1
  4.6 0.8 slice_reduce_fusion
  5.4 0.7 all_to_all.26
  6.1 4.2 all-to-all-start
  10.3 0.1 reshape_squeeze.4
  10.4 0.6 reduce_sum.9.counts_ref
  11.0 11.0 %shard_map.64 = (bf16[16,176,768]{2,1,0:T(8,128)(2,1)}, bf16[16,160,768]{2,1,0:T(8,128)(2,1)}) custom-call(s32[16]{0:T(128)} %reduce_sum.9.counts_ref, s32[8,2048]{1,0:T(8,128)} %get-tuple-element.12.slot_ref, bf16[2048,768]{1,0:T(8,128)(2,1)} %x_ref.5), custom_call_target="tpu_custom_call" | custom-call | flops 16911433728 | bytes 1 | tf_op jit(solution)/shard_map/pallas_call | solution.py:278
  22.0 0.0 all-to-all-done
  22.0 3.8 all-to-all-start.1
  25.9 15.8 %shard_map.67 = bf16[16,176,768]{2,1,0:T(8,128)(2,1)} custom-call(s32[16]{0:T(128)} %reduce_sum.9.counts_ref, s32[8,2048]{1,0:T(8,128)} %get-tuple-element.12.slot_ref, bf16[2048,768]{1,0:T(8,128)(2,1)} %x_ref.5), custom_call_target="tpu_custom_call" | custom-call | flops 8858370048 | bytes 1 | tf_op jit(solution)/shard_map/pallas_call | solution.py:278
  41.6 33.3 %all-to-all-done.1 = bf16[16,160,768]{2,1,0:T(8,128)(2,1)} async-done(((bf16[16,160,768]{2,1,0:T(8,128)(2,1)}), bf16[16,160,768]{2,1,0:T(8,128)(2,1)}, u32[]{:S(2)}, u32[]{:S(2)}) %all-to-all-start.1) | async-done | bytes 3932192 | tf_op jit(solution)/shard_map/all_to_all | solution.py:281
  74.9 53.3 %all_to_all.42 = bf16[16,176,768]{2,1,0:T(8,128)(2,1)} all-to-all(bf16[16,176,768]{2,1,0:T(8,128)(2,1)} %shard_map.67), channel_id=1, replica_groups=mesh['ep'=16] {'ep'}, dimensions={0} | all-to-all | bytes 8650752 | tf_op jit(solution)/shard_map/all_to_all | solution.py:281
  128.2 5.7 %all-to-all-start.3 = ((bf16[16,176,768]{2,1,0:T(8,128)(2,1)}), bf16[16,176,768]{2,1,0:T(8,128)(2,1)}, u32[]{:S(2)}, u32[]{:S(2)}) async-start(bf16[16,176,768]{2,1,0:T(8,128)(2,1)} %get-tuple-element.14), calls=%async_computation.3 | async-start | bytes 8650752 | tf_op jit(solution)/shard_map/all_to_all | solution.py:281
  133.9 0.1 copy.10
  134.0 0.6 concatenate.3.bound_ref
  134.6 84.0 %shard_map.68 = bf16[2816,768]{1,0:T(8,128)(2,1)} custom-call(s32[3,16]{1,0:T(4,128)} %concatenate.3.bound_ref, bf16[2816,768]{1,0:T(8,128)(2,1)} %bitcast.11, bf16[2,768,3072]{2,1,0:T(8,128)(2,1)} %w1_hbm.5, bf16[2,768,3072]{2,1,0:T(8,128)(2,1)} %w3_hbm.5, bf16[2,3072,768]{2,1,0:T(8,128)(2,1)} %w2_hbm.5), custom_call_target="tpu_custom_call" | custom-call | flops 39862665216 | bytes 1 | tf_op jit(solution)/shard_map/pallas_call | solution.py:301
  218.6 0.0 all-to-all-done.3
  218.6 14.4 %all-to-all-start.6 = ((bf16[16,176,768]{2,1,0:T(8,128)(2,1)}), bf16[16,176,768]{2,1,0:T(8,128)(2,1)}, u32[]{:S(2)}, u32[]{:S(2)}) async-start(bf16[16,176,768]{2,1,0:T(8,128)(2,1)} %bitcast.13), calls=%async_computation.6 | async-start | bytes 8650752 | tf_op jit(solution)/shard_map/all_to_all | solution.py:302
  233.0 93.6 %shard_map.66 = bf16[2816,768]{1,0:T(8,128)(2,1)} custom-call(s32[3,16]{1,0:T(4,128)} %concatenate.3.bound_ref, bf16[2816,768]{1,0:T(8,128)(2,1)} %bitcast.7.x_ref, bf16[2,768,3072]{2,1,0:T(8,128)(2,1)} %w1_hbm.5, bf16[2,768,3072]{2,1,0:T(8,128)(2,1)} %w3_hbm.5, bf16[2,3072,768]{2,1,0:T(8,128)(2,1)} %w2_hbm.5), custom_call_target="tpu_custom_call" | custom-call | flops 39862665216 | bytes 1 | tf_op jit(solution)/shard_map/pallas_call | solution.py:301
  326.7 0.0 all-to-all-done.6.back_ref
  326.7 3.2 all-to-all-start.4
  329.9 77.3 %shard_map.65 = bf16[2560,768]{1,0:T(8,128)(2,1)} custom-call(s32[3,16]{1,0:T(4,128)} %concatenate.3.bound_ref, bf16[2560,768]{1,0:T(8,128)(2,1)} %bitcast.5.x_ref, bf16[2,768,3072]{2,1,0:T(8,128)(2,1)} %w1_hbm.5, bf16[2,768,3072]{2,1,0:T(8,128)(2,1)} %w3_hbm.5, bf16[2,3072,768]{2,1,0:T(8,128)(2,1)} %w2_hbm.5), custom_call_target="tpu_custom_call" | custom-call | flops 36238786560 | bytes 1 | tf_op jit(solution)/shard_map/pallas_call | solution.py:301
  407.1 0.0 all-to-all-done.4.back_ref
  407.1 3.3 all-to-all-start.2
  410.4 45.7 %shard_map.69.refs_0_ = f32[2048,768]{1,0:T(8,128)} custom-call(s32[16]{0:T(128)} %reduce_sum.9.counts_ref, f32[2048,8]{1,0:T(8,128)} %get-tuple-element.11.cols_ref, bf16[16,176,768]{2,1,0:T(8,128)(2,1)} %all-to-all-done.6.back_ref), custom_call_target="tpu_custom_call" | custom-call | flops 17716740096 | bytes 1 | tf_op jit(solution)/shard_map/pallas_call | solution.py:325
  456.2 17.1 %shard_map.70.refs_0_ = f32[2048,768]{1,0:T(8,128)} custom-call(s32[16]{0:T(128)} %reduce_sum.9.counts_ref, f32[2048,8]{1,0:T(8,128)} %get-tuple-element.11.cols_ref, bf16[16,176,768]{2,1,0:T(8,128)(2,1)} %all-to-all-done.4.back_ref, f32[2048,768]{1,0:T(8,128)} %shard_map.69.refs_0_), custom_call_target="tpu_custom_call" | custom-call | flops 17716740096 | bytes 1 | tf_op jit(solution)/shard_map/pallas_call | solution.py:325
  473.3 0.0 all-to-all-done.2.back_ref
  473.3 16.7 %shard_map.71 = bf16[2048,768]{1,0:T(8,128)(2,1)} custom-call(s32[16]{0:T(128)} %reduce_sum.9.counts_ref, f32[2048,8]{1,0:T(8,128)} %get-tuple-element.11.cols_ref, bf16[16,160,768]{2,1,0:T(8,128)(2,1)} %all-to-all-done.2.back_ref, f32[2048,768]{1,0:T(8,128)} %shard_map.70.refs_0_), custom_call_target="tpu_custom_call" | custom-call | flops 16106127360 | bytes 1 | tf_op jit(solution)/shard_map/pallas_call | solution.py:325
  (1 shorter events, 0.0 us)
Async XLA Ops:
  6.1 15.9 %all-to-all-start = ((s32[16,1,2]{2,1,0:T(1,128)}), s32[16,1,2]{2,1,0:T(1,128)S(1)}, u32[]{:S(2)}, u32[]{:S(2)}) async-start(s32[16,1,2]{2,1,0:T(1,128)} %bitcast.2), calls=%async_computation | async-start | bytes 16384 | tf_op jit(solution)/shard_map/all_to_all | solution.py:259
  22.0 52.9 %all-to-all-start.1 = ((bf16[16,160,768]{2,1,0:T(8,128)(2,1)}), bf16[16,160,768]{2,1,0:T(8,128)(2,1)}, u32[]{:S(2)}, u32[]{:S(2)}) async-start(bf16[16,160,768]{2,1,0:T(8,128)(2,1)} %get-tuple-element.13), calls=%async_computation.1 | async-start | bytes 7864320 | tf_op jit(solution)/shard_map/all_to_all | solution.py:281
  128.2 90.4 %all-to-all-start.3 = ((bf16[16,176,768]{2,1,0:T(8,128)(2,1)}), bf16[16,176,768]{2,1,0:T(8,128)(2,1)}, u32[]{:S(2)}, u32[]{:S(2)}) async-start(bf16[16,176,768]{2,1,0:T(8,128)(2,1)} %get-tuple-element.14), calls=%async_computation.3 | async-start | bytes 8650752 | tf_op jit(solution)/shard_map/all_to_all | solution.py:281
  218.6 108.0 %all-to-all-start.6 = ((bf16[16,176,768]{2,1,0:T(8,128)(2,1)}), bf16[16,176,768]{2,1,0:T(8,128)(2,1)}, u32[]{:S(2)}, u32[]{:S(2)}) async-start(bf16[16,176,768]{2,1,0:T(8,128)(2,1)} %bitcast.13), calls=%async_computation.6 | async-start | bytes 8650752 | tf_op jit(solution)/shard_map/all_to_all | solution.py:302
  326.7 80.5 %all-to-all-start.4 = ((bf16[16,176,768]{2,1,0:T(8,128)(2,1)}), bf16[16,176,768]{2,1,0:T(8,128)(2,1)}, u32[]{:S(2)}, u32[]{:S(2)}) async-start(bf16[16,176,768]{2,1,0:T(8,128)(2,1)} %bitcast.12), calls=%async_computation.4 | async-start | bytes 8650752 | tf_op jit(solution)/shard_map/all_to_all | solution.py:302
  407.1 66.2 %all-to-all-start.2 = ((bf16[16,160,768]{2,1,0:T(8,128)(2,1)}), bf16[16,160,768]{2,1,0:T(8,128)(2,1)}, u32[]{:S(2)}, u32[]{:S(2)}) async-start(bf16[16,160,768]{2,1,0:T(8,128)(2,1)} %bitcast.14), calls=%async_computation.2 | async-start | bytes 7864320 | tf_op jit(solution)/shard_map/all_to_all | solution.py:302
where the time goes:
time: 499 us; the launch traced here: 490 us
  Pallas kernels  366 us (73%)
  blocking collectives  53.3 us (11%)
  starting transfers between devices  34.6 us (7%)
  waiting for transfers between devices  33.3 us (7%)
    pallas_call x3, Pallas kernels, body(): made = made(bounds, got.reshape(rows, dim), w1, w3, w2)  255 us
    pallas_call x3, Pallas kernels, body(): acc = combine(dev_counts, *ins)  79.5 us
    all_to_all x1, blocking collectives, body(): got = lax.all_to_all(sends[index], 'ep', 0, 0, tiled=True)  53.3 us
    all_to_all x2, waiting for transfers between devices, body(): got = lax.all_to_all(sends[index], 'ep', 0, 0, tiled=True)  33.3 us
    pallas_call x2, Pallas kernels, body(): sends += pack(dev_counts, slots, x)  26.8 us
    all_to_all x3, starting transfers between devices, body(): back = lax.all_to_all(made.reshape(n, size, dim), 'ep', 0, 0, tiled=True)  20.9 us
  transfers between devices with their start and end apart: 6, of which 1 were waited for; matrix products, arithmetic and copies ran while one was open for 0% of the time, Pallas kernels for 70%

commit v1 on v0

--- a/solution.py
+++ b/solution.py
@@ -12,7 +12,7 @@
 BF16 = jnp.bfloat16
 I32 = jnp.int32
 TILE = 16
-CHUNKS = ((0, 176), (176, 176), (352, 160))
+CHUNKS = ((0, 128), (128, 128), (256, 128), (384, 128))
 VMEM_BYTES = 60 * 1024 * 1024
 
 
@@ -69,32 +69,53 @@
     cols_ref[...] = both.T
 
 
+SLOT_TILE = 32
+PACK_GROUP = 8
+SUM_GROUP = 16
+
+
+def list_tiles(n_dev, size, start, counts_ref, list_ref, visit=None):
+    per = size // SLOT_TILE
+
+    def collect(i, cnt):
+        hit = counts_ref[i // per] > start + (i % per) * SLOT_TILE
+
+        @pl.when(hit)
+        def _():
+            list_ref[cnt] = i
+            if visit is not None:
+                visit(i, cnt)
+
+        return cnt + hit.astype(I32)
+
+    return lax.fori_loop(0, n_dev * per, collect, jnp.int32(0))
+
+
+def first_slot(i, size, start, row_cap):
+    per = size // SLOT_TILE
+    return (i // per) * row_cap + start + (i % per) * SLOT_TILE
+
+
 def pack_kernel(row_cap, chunks, counts_ref, slot_ref, x_ref, *refs):
     out_refs, list_ref = refs[:-1], refs[-1]
     tok = x_ref.shape[0]
-    n_dev = out_refs[0].shape[0]
     for (start, size), out_ref in zip(chunks, out_refs):
-
-        def collect(d, cnt):
-            list_ref[cnt] = d
-            return cnt + (counts_ref[d] > start).astype(I32)
-
-        list_ref[n_dev] = 0
-        cnt = lax.fori_loop(0, n_dev, collect, jnp.int32(0))
+        n_dev = out_ref.shape[0] // size
+        list_ref[0] = 0
+        cnt = list_tiles(n_dev, size, start, counts_ref, list_ref)
         last = jnp.maximum(cnt - 1, 0)
 
-        def pair(i, _):
-            d0, d1 = list_ref[2 * i], list_ref[jnp.minimum(2 * i + 1, last)]
-            pos = lax.broadcasted_iota(I32, (size, tok), 0) + start
-            want = jnp.concatenate([pos + d0 * row_cap, pos + d1 * row_cap], axis=0)
+        @pl.loop(0, (cnt + PACK_GROUP - 1) // PACK_GROUP)
+        def _(g):
+            tiles = [list_ref[jnp.minimum(g * PACK_GROUP + j, last)] for j in range(PACK_GROUP)]
+            pos = lax.broadcasted_iota(I32, (SLOT_TILE, tok), 0)
+            want = jnp.concatenate([pos + first_slot(i, size, start, row_cap) for i in tiles], axis=0)
             hit = (want == slot_ref[0:1, :]) | (want == slot_ref[1:2, :])
             pick = jnp.where(hit, 1.0, 0.0).astype(BF16)
             rows = _dot(pick, x_ref[...]).astype(BF16)
-            out_ref[d0] = rows[:size]
-            out_ref[d1] = rows[size:]
-            return 0
-
-        lax.fori_loop(0, (cnt + 1) // 2, pair, 0)
+            for j, i in enumerate(tiles):
+                at = pl.ds(pl.multiple_of(i * SLOT_TILE, SLOT_TILE), SLOT_TILE)
+                out_ref[at, :] = rows[j * SLOT_TILE : (j + 1) * SLOT_TILE]
 
 
 WIDE = 512
@@ -152,30 +173,27 @@
 
             cnt = lax.fori_loop(0, n_src * per, collect, jnp.int32(0))
 
-            def block(g, _):
+            def block(g, fresh):
                 at = pl.ds(pl.multiple_of(g * STEP, STEP), STEP)
                 xb = xbuf[at, :]
                 for f in range(n_f):
-
-                    @pl.when(g == 0)
-                    def _():
+                    if fresh:
                         copy(e, 0, f).wait()
                         copy(e, 1, f).wait()
-
                     cut = slice(f * WIDE, (f + 1) * WIDE)
                     u = _dot(xb, w1[e, :, cut])
                     v = _dot(xb, w3[e, :, cut])
                     hbuf[:, cut] = (u * jax.nn.sigmoid(u) * v).astype(BF16)
-
-                @pl.when(g == 0)
-                def _():
+                if fresh:
                     for f in range(n_f):
                         copy(e, 2, f).wait()
-
                 ybuf[at, :] = _dot(hbuf[...], w2[e]).astype(BF16)
-                return 0
-
-            lax.fori_loop(0, (cnt * TILE + STEP - 1) // STEP, block, 0)
+
+            block(0, True)
+
+            @pl.loop(1, (cnt * TILE + STEP - 1) // STEP)
+            def _(g):
+                block(g, False)
 
             def put(k, _):
                 i = list_ref[k]
@@ -193,44 +211,47 @@
 
 def combine_kernel(row_cap, start, size, n_dev, has_acc, counts_ref, cols_ref, back_ref, *refs):
     if has_acc:
-        acc_ref, out_ref, rows_ref, slot_ref, cnt_ref = refs
+        acc_ref, out_ref, rows_ref, sum_ref, list_ref, cnt_ref = refs
     else:
-        out_ref, rows_ref, slot_ref, cnt_ref = refs
+        out_ref, rows_ref, sum_ref, list_ref, cnt_ref = refs
+    group = SUM_GROUP * SLOT_TILE
+    toks, dim = out_ref.shape
 
     @pl.when(pl.program_id(0) == 0)
     def _():
-        slot_ref[...] = jnp.full_like(slot_ref, -1.0)
-
-        def collect(d, cnt):
-            @pl.when(counts_ref[d] > start)
-            def _():
-                pos = lax.broadcasted_iota(I32, (1, size), 1) + (d * row_cap + start)
-                rows_ref[pl.ds(pl.multiple_of(cnt * size, TILE), size), :] = back_ref[d]
-                slot_ref[cnt] = jnp.broadcast_to(pos.astype(F32), (8, size))
-
-            return cnt + (counts_ref[d] > start).astype(I32)
-
-        cnt = lax.fori_loop(0, n_dev, collect, jnp.int32(0))
-        cnt_ref[0] = cnt
-
-        @pl.when(cnt % 2 == 1)
-        def _():
-            rows_ref[pl.ds(pl.multiple_of(cnt * size, TILE), size), :] = jnp.zeros((size, rows_ref.shape[1]), BF16)
+        def bring(i, k):
+            src = pl.ds(pl.multiple_of(i * SLOT_TILE, SLOT_TILE), SLOT_TILE)
+            rows_ref[pl.ds(pl.multiple_of(k * SLOT_TILE, SLOT_TILE), SLOT_TILE), :] = back_ref[src, :]
+
+        cnt = list_tiles(n_dev, size, start, counts_ref, list_ref, bring)
+        groups = (cnt + SUM_GROUP - 1) // SUM_GROUP
+        cnt_ref[0] = groups
+
+        @pl.loop(cnt, groups * SUM_GROUP)
+        def _(k):
+            list_ref[k] = -1
+            rows_ref[pl.ds(pl.multiple_of(k * SLOT_TILE, SLOT_TILE), SLOT_TILE), :] = jnp.zeros((SLOT_TILE, dim), BF16)
 
     c = cols_ref[...]
-    toks, dim = out_ref.shape
-
-    def pair(i, total):
-        rows = rows_ref[pl.ds(pl.multiple_of(i * 2 * size, TILE), 2 * size), :]
-        ids = jnp.concatenate([slot_ref[2 * i, 0:1], slot_ref[2 * i + 1, 0:1]], axis=1)
+    sum_ref[...] = acc_ref[...] if has_acc else jnp.zeros((toks, dim), F32)
+    lane = lax.broadcasted_iota(I32, (1, group), 1)
+
+    @pl.loop(0, cnt_ref[0])
+    def _(g):
+        rows = rows_ref[pl.ds(pl.multiple_of(g * group, group), group), :]
+        ids = jnp.full((1, group), -1, I32)
+        for j in range(SUM_GROUP):
+            i = list_ref[g * SUM_GROUP + j]
+            base = jnp.where(i < 0, -1 - group, first_slot(i, size, start, row_cap))
+            ids = jnp.where(lane // SLOT_TILE == j, base + lane % SLOT_TILE, ids)
+        ids = ids.astype(F32)
+        add = 0.0
         for k in range(2):
             pick = jnp.where(ids == c[:, k : k + 1], 1.0, 0.0).astype(BF16)
-            total = total + c[:, 2 + k : 3 + k] * _dot(pick, rows)
-        return total
-
-    first = acc_ref[...] if has_acc else jnp.zeros((toks, dim), F32)
-    total = lax.fori_loop(0, (cnt_ref[0] + 1) // 2, pair, first)
-    out_ref[...] = total.astype(out_ref.dtype)
+            add = add + c[:, 2 + k : 3 + k] * _dot(pick, rows)
+        sum_ref[...] += add
+
+    out_ref[...] = sum_ref[...].astype(out_ref.dtype)
 
 
 def _params(**kw):
@@ -270,15 +291,15 @@
                 functools.partial(pack_kernel, cap, part),
                 in_specs=[smem, vmem, vmem],
                 out_specs=[vmem] * len(part),
-                out_shape=[jax.ShapeDtypeStruct((n, size, dim), BF16) for _, size in part],
-                scratch_shapes=[pltpu.SMEM((n + 1,), I32)],
+                out_shape=[jax.ShapeDtypeStruct((n * size, dim), BF16) for _, size in part],
+                scratch_shapes=[pltpu.SMEM((cap * n // SLOT_TILE,), I32)],
                 compiler_params=_params(),
                 cost_estimate=pl.CostEstimate(flops=2 * n * total * tok * dim, bytes_accessed=1, transcendentals=0),
             )
             sends += pack(dev_counts, slots, x)
         acc = None
         for index, (start, size) in enumerate(CHUNKS):
-            got = lax.all_to_all(sends[index], "ep", 0, 0, tiled=True)
+            got = lax.all_to_all(sends[index].reshape(n, size, dim), "ep", 0, 0, tiled=True)
             rows = n * size
             made = pl.pallas_call(
                 functools.partial(ffn_kernel, start, size, n),
@@ -299,12 +320,12 @@
                 cost_estimate=pl.CostEstimate(flops=6 * rows * dim * ff, bytes_accessed=1, transcendentals=0),
             )
             made = made(bounds, got.reshape(rows, dim), w1, w3, w2)
-            back = lax.all_to_all(made.reshape(n, size, dim), "ep", 0, 0, tiled=True)
+            back = lax.all_to_all(made.reshape(n, size, dim), "ep", 0, 0, tiled=True).reshape(rows, dim)
             last = index == len(CHUNKS) - 1
             tb = 512
             tile_spec = pl.BlockSpec((tb, dim), lambda i, c: (i, 0))
             ins = [cols, back] + ([] if acc is None else [acc])
-            specs = [pl.BlockSpec((tb, 8), lambda i, c: (i, 0)), pl.BlockSpec((n, size, dim), lambda i, c: (0, 0, 0))]
+            specs = [pl.BlockSpec((tb, 8), lambda i, c: (i, 0)), pl.BlockSpec((rows, dim), lambda i, c: (0, 0))]
             combine = pl.pallas_call(
                 functools.partial(combine_kernel, cap, start, size, n, acc is not None),
                 grid_spec=pltpu.PrefetchScalarGridSpec(
@@ -313,8 +334,9 @@
                     in_specs=specs + ([] if acc is None else [tile_spec]),
                     out_specs=tile_spec,
                     scratch_shapes=[
-                        pltpu.VMEM((rows + size, dim), BF16),
-                        pltpu.VMEM((n + 1, 8, size), F32),
+                        pltpu.VMEM((rows, dim), BF16),
+                        pltpu.VMEM((tb, dim), F32),
+                        pltpu.SMEM((rows // SLOT_TILE,), I32),
                         pltpu.SMEM((1,), I32),
                     ],
                 ),

time: 499 us -> 471 us (0.944)
  Pallas kernels: 366 us -> 312 us
  blocking collectives: 53.3 us -> 81.9 us
  waiting for transfers between devices: 33.3 us -> 20.7 us
    pallas_call x3 -> x4, Pallas kernels: 255 us -> 208 us  [body(): made = made(bounds, got.reshape(rows, dim), w1, w3, w2)]
    all_to_all x1 -> x2, blocking collectives: 53.3 us -> 81.9 us  [body(): lax.all_to_all(sends[index].reshape(n, size, dim), 'ep', 0, 0, tiled=True)]
    pallas_call x3 -> x4, Pallas kernels: 79.5 us -> 66.6 us  [body(): acc = combine(dev_counts, *ins)]
    all_to_all x5 -> x6, waiting for transfers between devices: 33.3 us -> 20.7 us  [the longest x2 20.7 us: body(): lax.all_to_all(sends[index].reshape(n, size, dim), 'ep', 0, 0, tiled=True)]
    pallas_call x2, Pallas kernels: 26.8 us -> 32.2 us  [body(): sends += pack(dev_counts, slots, x)]
    unnamed x0 -> x10, local copies, waits for them, and re-layouts: none -> 5.02 us
    all_to_all x5 -> x6, starting transfers between devices: 30.4 us -> 35.1 us  [the longest x4 26.3 us: body(): lax.all_to_all(made.reshape(n, size, dim), 'ep', 0, 0, tiled=True)]
  transfers between devices with their start and end apart: 6 -> 7, of which waited for: 1 -> 1; matrix products, arithmetic and copies ran while one was open for 0% -> 0% of each run, Pallas kernels for 70% -> 64%
where the time goes in v1:
time: 471 us; the launch traced here: 462 us
  Pallas kernels  312 us (66%)
  blocking collectives  81.9 us (17%)
  starting transfers between devices  39.3 us (8%)
  waiting for transfers between devices  20.7 us (4%)
  local copies, waits for them, and re-layouts  7.24 us (2%)
    pallas_call x4, Pallas kernels, body(): made = made(bounds, got.reshape(rows, dim), w1, w3, w2)  208 us
    all_to_all x2, blocking collectives, body(): lax.all_to_all(sends[index].reshape(n, size, dim), 'ep', 0, 0, tiled=True)  81.9 us
    pallas_call x4, Pallas kernels, body(): acc = combine(dev_counts, *ins)  66.6 us
    pallas_call x2, Pallas kernels, body(): sends += pack(dev_counts, slots, x)  32.2 us
    all_to_all x4, starting transfers between devices, body(): lax.all_to_all(made.reshape(n, size, dim), 'ep', 0, 0, tiled=True)  26.3 us
    all_to_all x2, waiting for transfers between devices, body(): lax.all_to_all(sends[index].reshape(n, size, dim), 'ep', 0, 0, tiled=True)  20.7 us
  transfers between devices with their start and end apart: 7, of which 1 were waited for; matrix products, arithmetic and copies ran while one was open for 0% of the time, Pallas kernels for 64%

profile of v1, /device:TPU:11, one launch (start us, length us, event | category | flops | bytes accessed | tf_op | source)
XLA Modules:
  0.0 462.2 jit_solution(11452663572487766233)
XLA Ops:
  0.0 4.5 route.1
  4.5 0.8 slice_reduce_fusion
  5.4 0.7 all_to_all.32
  6.1 4.2 all-to-all-start
  10.2 0.1 reshape_squeeze.4
  10.3 0.7 reduce_sum.9.counts_ref
  11.0 13.5 %shard_map.68 = bf16[2048,768]{1,0:T(8,128)(2,1)} custom-call(s32[16]{0:T(128)} %reduce_sum.9.counts_ref, s32[8,2048]{1,0:T(8,128)} %get-tuple-element.13.slot_ref, bf16[2048,768]{1,0:T(8,128)(2,1)} %x_ref.5), custom_call_target="tpu_custom_call" | custom-call | flops 6442450944 | bytes 1 | tf_op jit(solution)/shard_map/pallas_call | solution.py:299
  24.5 0.0 all-to-all-done
  24.5 3.8 all-to-all-start.7
  28.3 18.7 %shard_map.64 = (bf16[2048,768]{1,0:T(8,128)(2,1)}, bf16[2048,768]{1,0:T(8,128)(2,1)}, bf16[2048,768]{1,0:T(8,128)(2,1)}) custom-call(s32[16]{0:T(128)} %reduce_sum.9.counts_ref, s32[8,2048]{1,0:T(8,128)} %get-tuple-element.13.slot_ref, bf16[2048,768]{1,0:T(8,128)(2,1)} %x_ref.5), custom_call_target="tpu_custom_call" | custom-call | flops 19327352832 | bytes 1 | tf_op jit(solution)/shard_map/pallas_call | solution.py:299
  47.0 20.7 %all-to-all-done.7 = bf16[16,128,768]{2,1,0:T(8,128)(2,1)S(1)} async-done(((bf16[16,128,768]{2,1,0:T(8,128)(2,1)}), bf16[16,128,768]{2,1,0:T(8,128)(2,1)S(1)}, u32[]{:S(2)}, u32[]{:S(2)}) %all-to-all-start.7) | async-done | bytes 3145760 | tf_op jit(solution)/shard_map/all_to_all | solution.py:302
  67.8 0.0 copy-start.2
  67.8 0.0 copy-start.4
  67.8 41.2 %all_to_all.52 = bf16[16,128,768]{2,1,0:T(8,128)(2,1)} all-to-all(bf16[16,128,768]{2,1,0:T(8,128)(2,1)} %bitcast.34), channel_id=1, replica_groups=mesh['ep'=16] {'ep'}, dimensions={0} | all-to-all | bytes 6291456 | tf_op jit(solution)/shard_map/all_to_all | solution.py:302
  109.0 0.0 copy-done.2
  109.0 0.0 copy-done.4
  109.0 40.7 %all_to_all.53 = bf16[16,128,768]{2,1,0:T(8,128)(2,1)} all-to-all(bf16[16,128,768]{2,1,0:T(8,128)(2,1)S(1)} %bitcast.33), channel_id=1, replica_groups=mesh['ep'=16] {'ep'}, dimensions={0} | all-to-all | bytes 6291456 | tf_op jit(solution)/shard_map/all_to_all | solution.py:302
  149.7 4.9 %all-to-all-start.5 = ((bf16[16,128,768]{2,1,0:T(8,128)(2,1)}), bf16[16,128,768]{2,1,0:T(8,128)(2,1)S(1)}, u32[]{:S(2)}, u32[]{:S(2)}) async-start(bf16[16,128,768]{2,1,0:T(8,128)(2,1)} %bitcast.26), calls=%async_computation.5 | async-start | bytes 6291456 | tf_op jit(solution)/shard_map/all_to_all | solution.py:302
  154.6 0.1 copy.10
  154.8 0.5 concatenate.3.bound_ref
  155.3 44.3 %shard_map.69 = bf16[2048,768]{1,0:T(8,128)(2,1)} custom-call(s32[3,16]{1,0:T(4,128)} %concatenate.3.bound_ref, bf16[2048,768]{1,0:T(8,128)(2,1)} %bitcast.24, bf16[2,768,3072]{2,1,0:T(8,128)(2,1)} %w1_hbm.7, bf16[2,768,3072]{2,1,0:T(8,128)(2,1)} %w3_hbm.7, bf16[2,3072,768]{2,1,0:T(8,128)(2,1)} %w2_hbm.7), custom_call_target="tpu_custom_call" | custom-call | flops 28991029248 | bytes 1 | tf_op jit(solution)/shard_map/pallas_call | solution.py:322
  199.6 0.0 all-to-all-done.5
  199.6 0.0 copy-start.1
  199.6 1.6 copy-done.1
  201.3 17.0 %all-to-all-start.8 = ((bf16[16,128,768]{2,1,0:T(8,128)(2,1)}), bf16[16,128,768]{2,1,0:T(8,128)(2,1)S(1)}, u32[]{:S(2)}, u32[]{:S(2)}) async-start(bf16[16,128,768]{2,1,0:T(8,128)(2,1)} %bitcast.31), calls=%async_computation.8 | async-start | bytes 6291456 | tf_op jit(solution)/shard_map/all_to_all | solution.py:323
  218.3 61.2 %shard_map.66 = bf16[2048,768]{1,0:T(8,128)(2,1)} custom-call(s32[3,16]{1,0:T(4,128)} %concatenate.3.bound_ref, bf16[2048,768]{1,0:T(8,128)(2,1)} %bitcast.25, bf16[2,768,3072]{2,1,0:T(8,128)(2,1)} %w1_hbm.7, bf16[2,768,3072]{2,1,0:T(8,128)(2,1)} %w3_hbm.7, bf16[2,3072,768]{2,1,0:T(8,128)(2,1)} %w2_hbm.7), custom_call_target="tpu_custom_call" | custom-call | flops 28991029248 | bytes 1 | tf_op jit(solution)/shard_map/pallas_call | solution.py:322
  279.4 0.0 all-to-all-done.8
  279.5 0.0 copy-start
  279.5 1.7 copy-done
  281.2 3.1 all-to-all-start.4
  284.3 53.3 %shard_map.67 = bf16[2048,768]{1,0:T(8,128)(2,1)} custom-call(s32[3,16]{1,0:T(4,128)} %concatenate.3.bound_ref, bf16[2048,768]{1,0:T(8,128)(2,1)} %bitcast.23, bf16[2,768,3072]{2,1,0:T(8,128)(2,1)} %w1_hbm.7, bf16[2,768,3072]{2,1,0:T(8,128)(2,1)} %w3_hbm.7, bf16[2,3072,768]{2,1,0:T(8,128)(2,1)} %w2_hbm.7), custom_call_target="tpu_custom_call" | custom-call | flops 28991029248 | bytes 1 | tf_op jit(solution)/shard_map/pallas_call | solution.py:322
  337.6 0.0 all-to-all-done.4
  337.6 2.7 all-to-all-start.6
  340.3 49.6 %shard_map.65 = bf16[2048,768]{1,0:T(8,128)(2,1)} custom-call(s32[3,16]{1,0:T(4,128)} %concatenate.3.bound_ref, bf16[2048,768]{1,0:T(8,128)(2,1)} %bitcast.21, bf16[2,768,3072]{2,1,0:T(8,128)(2,1)} %w1_hbm.7, bf16[2,768,3072]{2,1,0:T(8,128)(2,1)} %w3_hbm.7, bf16[2,3072,768]{2,1,0:T(8,128)(2,1)} %w2_hbm.7), custom_call_target="tpu_custom_call" | custom-call | flops 28991029248 | bytes 1 | tf_op jit(solution)/shard_map/pallas_call | solution.py:322
  389.8 0.0 all-to-all-done.6
  389.8 0.0 copy-start.3
  389.9 1.7 copy-done.3
  391.5 3.5 all-to-all-start.2
  395.1 23.7 %shard_map.70.refs_0_ = f32[2048,768]{1,0:T(8,128)} custom-call(s32[16]{0:T(128)} %reduce_sum.9.counts_ref, f32[2048,8]{1,0:T(8,128)} %get-tuple-element.12.cols_ref, bf16[2048,768]{1,0:T(8,128)(2,1)} %bitcast.22), custom_call_target="tpu_custom_call" | custom-call | flops 12884901888 | bytes 1 | tf_op jit(solution)/shard_map/pallas_call | solution.py:347
  418.7 19.9 %shard_map.71.refs_0_ = f32[2048,768]{1,0:T(8,128)} custom-call(s32[16]{0:T(128)} %reduce_sum.9.counts_ref, f32[2048,8]{1,0:T(8,128)} %get-tuple-element.12.cols_ref, bf16[2048,768]{1,0:T(8,128)(2,1)} %bitcast.27, f32[2048,768]{1,0:T(8,128)} %shard_map.70.refs_0_), custom_call_target="tpu_custom_call" | custom-call | flops 12884901888 | bytes 1 | tf_op jit(solution)/shard_map/pallas_call | solution.py:347
  438.7 11.8 %shard_map.72.refs_0_ = f32[2048,768]{1,0:T(8,128)} custom-call(s32[16]{0:T(128)} %reduce_sum.9.counts_ref, f32[2048,8]{1,0:T(8,128)} %get-tuple-element.12.cols_ref, bf16[2048,768]{1,0:T(8,128)(2,1)} %bitcast.12.back_ref, f32[2048,768]{1,0:T(8,128)} %shard_map.71.refs_0_), custom_call_target="tpu_custom_call" | custom-call | flops 12884901888 | bytes 1 | tf_op jit(solution)/shard_map/pallas_call | solution.py:347
  450.5 0.0 all-to-all-done.2
  450.5 11.2 %shard_map.73 = bf16[2048,768]{1,0:T(8,128)(2,1)} custom-call(s32[16]{0:T(128)} %reduce_sum.9.counts_ref, f32[2048,8]{1,0:T(8,128)} %get-tuple-element.12.cols_ref, bf16[2048,768]{1,0:T(8,128)(2,1)} %bitcast.8.back_ref, f32[2048,768]{1,0:T(8,128)} %shard_map.72.refs_0_), custom_call_target="tpu_custom_call" | custom-call | flops 12884901888 | bytes 1 | tf_op jit(solution)/shard_map/pallas_call | solution.py:347
  (1 shorter events, 0.0 us)
Async XLA Ops:
  6.1 18.4 %all-to-all-start = ((s32[16,1,2]{2,1,0:T(1,128)}), s32[16,1,2]{2,1,0:T(1,128)S(1)}, u32[]{:S(2)}, u32[]{:S(2)}) async-start(s32[16,1,2]{2,1,0:T(1,128)} %bitcast.2), calls=%async_computation | async-start | bytes 16384 | tf_op jit(solution)/shard_map/all_to_all | solution.py:280
  24.5 43.3 %all-to-all-start.7 = ((bf16[16,128,768]{2,1,0:T(8,128)(2,1)}), bf16[16,128,768]{2,1,0:T(8,128)(2,1)S(1)}, u32[]{:S(2)}, u32[]{:S(2)}) async-start(bf16[16,128,768]{2,1,0:T(8,128)(2,1)} %bitcast.29), calls=%async_computation.7 | async-start | bytes 6291456 | tf_op jit(solution)/shard_map/all_to_all | solution.py:302
  67.8 41.2 %copy-start.2 = (bf16[16,128,768]{2,1,0:T(8,128)(2,1)}, bf16[16,128,768]{2,1,0:T(8,128)(2,1)S(1)}, u32[]{:S(2)}) copy-start(bf16[16,128,768]{2,1,0:T(8,128)(2,1)S(1)} %all-to-all-done.7) | copy-start | bytes 9437188
  67.8 41.2 %copy-start.4 = (bf16[2048,768]{1,0:T(8,128)(2,1)S(1)}, bf16[2048,768]{1,0:T(8,128)(2,1)}, u32[]{:S(2)}) copy-start(bf16[2048,768]{1,0:T(8,128)(2,1)} %get-tuple-element.14) | copy-start | bytes 9437188
  149.7 49.9 %all-to-all-start.5 = ((bf16[16,128,768]{2,1,0:T(8,128)(2,1)}), bf16[16,128,768]{2,1,0:T(8,128)(2,1)S(1)}, u32[]{:S(2)}, u32[]{:S(2)}) async-start(bf16[16,128,768]{2,1,0:T(8,128)(2,1)} %bitcast.26), calls=%async_computation.5 | async-start | bytes 6291456 | tf_op jit(solution)/shard_map/all_to_all | solution.py:302
  199.6 1.6 copy-start.1
  201.3 78.2 %all-to-all-start.8 = ((bf16[16,128,768]{2,1,0:T(8,128)(2,1)}), bf16[16,128,768]{2,1,0:T(8,128)(2,1)S(1)}, u32[]{:S(2)}, u32[]{:S(2)}) async-start(bf16[16,128,768]{2,1,0:T(8,128)(2,1)} %bitcast.31), calls=%async_computation.8 | async-start | bytes 6291456 | tf_op jit(solution)/shard_map/all_to_all | solution.py:323
  279.5 1.7 copy-start
  281.2 56.4 %all-to-all-start.4 = ((bf16[16,128,768]{2,1,0:T(8,128)(2,1)}), bf16[16,128,768]{2,1,0:T(8,128)(2,1)}, u32[]{:S(2)}, u32[]{:S(2)}) async-start(bf16[16,128,768]{2,1,0:T(8,128)(2,1)} %bitcast.32), calls=%async_computation.4 | async-start | bytes 6291456 | tf_op jit(solution)/shard_map/all_to_all | solution.py:323
  337.6 52.2 %all-to-all-start.6 = ((bf16[16,128,768]{2,1,0:T(8,128)(2,1)}), bf16[16,128,768]{2,1,0:T(8,128)(2,1)S(1)}, u32[]{:S(2)}, u32[]{:S(2)}) async-start(bf16[16,128,768]{2,1,0:T(8,128)(2,1)} %bitcast.30), calls=%async_computation.6 | async-start | bytes 6291456 | tf_op jit(solution)/shard_map/all_to_all | solution.py:323
  389.8 1.7 copy-start.3
  391.5 59.0 %all-to-all-start.2 = ((bf16[16,128,768]{2,1,0:T(8,128)(2,1)}), bf16[16,128,768]{2,1,0:T(8,128)(2,1)}, u32[]{:S(2)}, u32[]{:S(2)}) async-start(bf16[16,128,768]{2,1,0:T(8,128)(2,1)} %bitcast.28), calls=%async_computation.2 | async-start | bytes 6291456 | tf_op jit(solution)/shard_map/all_to_all | solution.py:323

commit v2 on v1

--- a/solution.py
+++ b/solution.py
@@ -14,6 +14,7 @@
 TILE = 16
 CHUNKS = ((0, 128), (128, 128), (256, 128), (384, 128))
 VMEM_BYTES = 60 * 1024 * 1024
+FFN_VMEM = 44 * 1024 * 1024
 
 
 def _dot(a, b):
@@ -122,7 +123,7 @@
 STEP = 256
 
 
-def ffn_kernel(start, size, n_src, bound_ref, x_ref, w1_hbm, w3_hbm, w2_hbm, out_ref, w1, w3, w2, xbuf, hbuf, ybuf, list_ref, sems):
+def ffn_kernel(start, size, n_src, bound_ref, x_ref, w1_hbm, w3_hbm, w2_hbm, out_ref, w1, w3, w2, xbuf, hbuf, ybuf, list_ref, used_ref, sems):
     n_loc, _, ff = w1.shape
     n_f = ff // WIDE
     per = size // TILE
@@ -133,28 +134,31 @@
         src, dst = ((w1_hbm, w1), (w3_hbm, w3), (w2_hbm, w2))[which]
         return pltpu.make_async_copy(src.at[at], dst.at[at], sems.at[e, which, f])
 
-    counts = []
-    for e in range(n_loc):
-
+    @pl.loop(0, n_loc)
+    def _(e):
         def need(s, any_):
             lo, hi = bound_ref[e, s], bound_ref[e + 1, s]
             return any_ | ((lo < start + size) & (hi > start) & (hi > lo)).astype(I32)
 
         used = lax.fori_loop(0, n_src, need, jnp.int32(0))
-        counts.append(used)
+        used_ref[e] = used
 
         @pl.when(used > 0)
         def _():
-            for f in range(n_f):
+            @pl.loop(0, n_f)
+            def _(f):
                 copy(e, 0, f).start()
                 copy(e, 1, f).start()
-            for f in range(n_f):
+
+            @pl.loop(0, n_f)
+            def _(f):
                 copy(e, 2, f).start()
 
     out_ref[...] = jnp.zeros_like(out_ref)
-    for e in range(n_loc):
-
-        @pl.when(counts[e] > 0)
+
+    @pl.loop(0, n_loc)
+    def _(e):
+        @pl.when(used_ref[e] > 0)
         def _():
             def collect(i, cnt):
                 s = i // per
@@ -173,27 +177,33 @@
 
             cnt = lax.fori_loop(0, n_src * per, collect, jnp.int32(0))
 
-            def block(g, fresh):
+            def columns(at, f):
+                cut = pl.ds(f * WIDE if isinstance(f, int) else pl.multiple_of(f * WIDE, WIDE), WIDE)
+                xb = xbuf[at, :]
+                u = _dot(xb, w1[e, :, cut])
+                v = _dot(xb, w3[e, :, cut])
+                hbuf[:, cut] = (u * jax.nn.sigmoid(u) * v).astype(BF16)
+
+            @pl.loop(0, n_f)
+            def _(f):
+                copy(e, 0, f).wait()
+                copy(e, 1, f).wait()
+                columns(pl.ds(0, STEP), f)
+
+            @pl.loop(0, n_f)
+            def _(f):
+                copy(e, 2, f).wait()
+
+            @pl.loop(0, (cnt * TILE + STEP - 1) // STEP)
+            def _(g):
                 at = pl.ds(pl.multiple_of(g * STEP, STEP), STEP)
-                xb = xbuf[at, :]
-                for f in range(n_f):
-                    if fresh:
-                        copy(e, 0, f).wait()
-                        copy(e, 1, f).wait()
-                    cut = slice(f * WIDE, (f + 1) * WIDE)
-                    u = _dot(xb, w1[e, :, cut])
-                    v = _dot(xb, w3[e, :, cut])
-                    hbuf[:, cut] = (u * jax.nn.sigmoid(u) * v).astype(BF16)
-                if fresh:
+
+                @pl.when(g > 0)
+                def _():
                     for f in range(n_f):
-                        copy(e, 2, f).wait()
+                        columns(at, f)
+
                 ybuf[at, :] = _dot(hbuf[...], w2[e]).astype(BF16)
-
-            block(0, True)
-
-            @pl.loop(1, (cnt * TILE + STEP - 1) // STEP)
-            def _(g):
-                block(g, False)
 
             def put(k, _):
                 i = list_ref[k]
@@ -254,8 +264,8 @@
     out_ref[...] = sum_ref[...].astype(out_ref.dtype)
 
 
-def _params(**kw):
-    return pltpu.CompilerParams(vmem_limit_bytes=VMEM_BYTES, **kw)
+def _params(vmem_limit_bytes=VMEM_BYTES):
+    return pltpu.CompilerParams(vmem_limit_bytes=vmem_limit_bytes)
 
 
 def solution(mesh):
@@ -313,13 +323,15 @@
                     pltpu.VMEM((STEP, ff), BF16),
                     pltpu.VMEM((rows, dim), BF16),
                     pltpu.SMEM((rows // TILE,), I32),
+                    pltpu.SMEM((local,), I32),
                     pltpu.SemaphoreType.DMA((local, 3, ff // WIDE)),
                 ],
-                out_shape=jax.ShapeDtypeStruct((rows, dim), BF16),
-                compiler_params=_params(),
+                out_shape=pltpu.VMEM((rows, dim), BF16),
+                compiler_params=_params(FFN_VMEM),
                 cost_estimate=pl.CostEstimate(flops=6 * rows * dim * ff, bytes_accessed=1, transcendentals=0),
             )
-            made = made(bounds, got.reshape(rows, dim), w1, w3, w2)
+            got = pltpu.with_memory_space_constraint(got.reshape(rows, dim), pltpu.VMEM)
+            made = made(bounds, got, *[pltpu.with_memory_space_constraint(w, pltpu.HBM) for w in (w1, w3, w2)])
             back = lax.all_to_all(made.reshape(n, size, dim), "ep", 0, 0, tiled=True).reshape(rows, dim)
             last = index == len(CHUNKS) - 1
             tb = 512

time: 471 us -> 442 us (0.938); the launches traced: 462 us -> 440 us
  Pallas kernels: 312 us -> 284 us
  local copies, waits for them, and re-layouts: 7.24 us -> 13.8 us
    pallas_call x4, Pallas kernels: 208 us -> 181 us  [body(): made(bounds, got, *[pltpu.with_memory_space_constraint(w, pltpu.HBM) for...]
    unnamed x10 -> x18, local copies, waits for them, and re-layouts: 5.02 us -> 12.1 us
  transfers between devices with their start and end apart: 7 -> 7, of which waited for: 1 -> 1; matrix products, arithmetic and copies ran while one was open for 0% -> 0% of each run, Pallas kernels for 64% -> 61%
where the time goes in v2:
time: 442 us; the launch traced here: 440 us
  Pallas kernels  284 us (64%)
  blocking collectives  81.2 us (18%)
  starting transfers between devices  39.2 us (9%)
  waiting for transfers between devices  20.7 us (5%)
  local copies, waits for them, and re-layouts  13.8 us (3%)
    pallas_call x4, Pallas kernels, body(): made(bounds, got, *[pltpu.with_memory_space_constraint(w, pltpu.HBM) for...  181 us
    all_to_all x2, blocking collectives, body(): lax.all_to_all(sends[index].reshape(n, size, dim), 'ep', 0, 0, tiled=True)  81.2 us
    pallas_call x4, Pallas kernels, body(): acc = combine(dev_counts, *ins)  66.7 us
    pallas_call x2, Pallas kernels, body(): sends += pack(dev_counts, slots, x)  32.3 us
    all_to_all x4, starting transfers between devices, body(): lax.all_to_all(made.reshape(n, size, dim), 'ep', 0, 0, tiled=True)  25.5 us
    all_to_all x2, waiting for transfers between devices, body(): lax.all_to_all(sends[index].reshape(n, size, dim), 'ep', 0, 0, tiled=True)  20.7 us
    unnamed x18, local copies, waits for them, and re-layouts  12.1 us
    all_to_all x2, starting transfers between devices, body(): lax.all_to_all(sends[index].reshape(n, size, dim), 'ep', 0, 0, tiled=True)  9.47 us
  transfers between devices with their start and end apart: 7, of which 1 were waited for; matrix products, arithmetic and copies ran while one was open for 0% of the time, Pallas kernels for 61%

profile of v2, /device:TPU:11, one launch (start us, length us, event | category | flops | bytes accessed | tf_op | source)
XLA Modules:
  0.0 439.9 jit_solution(18076969157180567989)
XLA Ops:
  0.0 4.5 %route.1 = (s32[8,2048]{1,0:T(8,128)}, f32[2048,8]{1,0:T(8,128)}, s32[32,128]{1,0:T(8,128)}) custom-call(bf16[2048,768]{1,0:T(8,128)(2,1)} %x_ref.5, f32[32,768]{1,0:T(8,128)} %bitcast.33, s32[2,2048]{1,0:T(2,128)} %bitcast.34), custom_call_target="tpu_custom_call" | custom-call | tf_op jit(solution)/shard_map/route/pallas_call | solution.py:280
  4.5 0.8 slice_reduce_fusion
  5.4 0.7 all_to_all.32
  6.0 4.2 all-to-all-start
  10.2 0.1 reshape_squeeze.4
  10.3 0.6 reduce_sum.9.counts_ref
  10.9 13.5 %shard_map.68 = bf16[2048,768]{1,0:T(8,128)(2,1)} custom-call(s32[16]{0:T(128)} %reduce_sum.9.counts_ref, s32[8,2048]{1,0:T(8,128)} %get-tuple-element.13.slot_ref, bf16[2048,768]{1,0:T(8,128)(2,1)} %x_ref.5), custom_call_target="tpu_custom_call" | custom-call | flops 6442450944 | bytes 1 | tf_op jit(solution)/shard_map/pallas_call | solution.py:309
  24.4 0.0 all-to-all-done
  24.4 3.8 all-to-all-start.7
  28.2 18.8 %shard_map.64 = (bf16[2048,768]{1,0:T(8,128)(2,1)}, bf16[2048,768]{1,0:T(8,128)(2,1)}, bf16[2048,768]{1,0:T(8,128)(2,1)}) custom-call(s32[16]{0:T(128)} %reduce_sum.9.counts_ref, s32[8,2048]{1,0:T(8,128)} %get-tuple-element.13.slot_ref, bf16[2048,768]{1,0:T(8,128)(2,1)} %x_ref.5), custom_call_target="tpu_custom_call" | custom-call | flops 19327352832 | bytes 1 | tf_op jit(solution)/shard_map/pallas_call | solution.py:309
  47.0 20.7 %all-to-all-done.7 = bf16[16,128,768]{2,1,0:T(8,128)(2,1)S(1)} async-done(((bf16[16,128,768]{2,1,0:T(8,128)(2,1)}), bf16[16,128,768]{2,1,0:T(8,128)(2,1)S(1)}, u32[]{:S(2)}, u32[]{:S(2)}) %all-to-all-start.7) | async-done | bytes 3145760 | tf_op jit(solution)/shard_map/all_to_all | solution.py:312
  67.7 0.0 copy-start
  67.7 0.0 copy-start.8
  67.7 41.2 %all_to_all.52 = bf16[16,128,768]{2,1,0:T(8,128)(2,1)} all-to-all(bf16[16,128,768]{2,1,0:T(8,128)(2,1)} %bitcast.32), channel_id=1, replica_groups=mesh['ep'=16] {'ep'}, dimensions={0} | all-to-all | bytes 6291456 | tf_op jit(solution)/shard_map/all_to_all | solution.py:312
  108.9 0.0 copy-done
  108.9 0.0 copy-done.8
  108.9 40.0 %all_to_all.53 = bf16[16,128,768]{2,1,0:T(8,128)(2,1)S(1)} all-to-all(bf16[16,128,768]{2,1,0:T(8,128)(2,1)S(1)} %bitcast.31), channel_id=1, replica_groups=mesh['ep'=16] {'ep'}, dimensions={0} | all-to-all | bytes 6291456 | tf_op jit(solution)/shard_map/all_to_all | solution.py:312
  148.9 5.6 %all-to-all-start.5 = ((bf16[16,128,768]{2,1,0:T(8,128)(2,1)}), bf16[16,128,768]{2,1,0:T(8,128)(2,1)}, u32[]{:S(2)}, u32[]{:S(2)}) async-start(bf16[16,128,768]{2,1,0:T(8,128)(2,1)} %bitcast.28), calls=%async_computation.5 | async-start | bytes 6291456 | tf_op jit(solution)/shard_map/all_to_all | solution.py:312
  154.6 0.1 copy.10
  154.7 0.0 copy-start.1
  154.7 1.9 copy-done.1
  156.6 40.5 %shard_map.69 = bf16[2048,768]{1,0:T(8,128)(2,1)S(1)} custom-call(s32[3,16]{1,0:T(4,128)S(1)} %concatenate.3.bound_ref, bf16[2048,768]{1,0:T(8,128)(2,1)S(1)} %bitcast.22, bf16[2,768,3072]{2,1,0:T(8,128)(2,1)} %w1_hbm.7, bf16[2,768,3072]{2,1,0:T(8,128)(2,1)} %w3_hbm.7, bf16[2,3072,768]{2,1,0:T(8,128)(2,1)} %w2_hbm.7), custom_call_target="tpu_custom_call" | custom-call | flops 28991029248 | bytes 1 | tf_op jit(solution)/shard_map/pallas_call | solution.py:334
  197.1 0.0 copy-start.5
  197.1 1.7 copy-done.5
  198.8 0.0 all-to-all-done.5
  198.8 16.5 %all-to-all-start.8 = ((bf16[16,128,768]{2,1,0:T(8,128)(2,1)}), bf16[16,128,768]{2,1,0:T(8,128)(2,1)}, u32[]{:S(2)}, u32[]{:S(2)}) async-start(bf16[16,128,768]{2,1,0:T(8,128)(2,1)} %bitcast.26), calls=%async_computation.8 | async-start | bytes 6291456 | tf_op jit(solution)/shard_map/all_to_all | solution.py:335
  215.3 0.0 copy-start.2
  215.3 1.9 copy-done.2
  217.2 49.1 %shard_map.66 = bf16[2048,768]{1,0:T(8,128)(2,1)S(1)} custom-call(s32[3,16]{1,0:T(4,128)S(1)} %concatenate.3.bound_ref, bf16[2048,768]{1,0:T(8,128)(2,1)S(1)} %bitcast.23, bf16[2,768,3072]{2,1,0:T(8,128)(2,1)} %w1_hbm.7, bf16[2,768,3072]{2,1,0:T(8,128)(2,1)} %w3_hbm.7, bf16[2,3072,768]{2,1,0:T(8,128)(2,1)} %w2_hbm.7), custom_call_target="tpu_custom_call" | custom-call | flops 28991029248 | bytes 1 | tf_op jit(solution)/shard_map/pallas_call | solution.py:334
  266.3 0.0 copy-start.6
  266.3 1.7 copy-done.6
  268.0 0.0 all-to-all-done.8
  268.0 3.2 all-to-all-start.4
  271.2 50.4 %shard_map.67 = bf16[2048,768]{1,0:T(8,128)(2,1)S(1)} custom-call(s32[3,16]{1,0:T(4,128)S(1)} %concatenate.3.bound_ref, bf16[2048,768]{1,0:T(8,128)(2,1)} %bitcast.14.x_ref, bf16[2,768,3072]{2,1,0:T(8,128)(2,1)} %w1_hbm.7, bf16[2,768,3072]{2,1,0:T(8,128)(2,1)} %w3_hbm.7, bf16[2,3072,768]{2,1,0:T(8,128)(2,1)} %w2_hbm.7), custom_call_target="tpu_custom_call" | custom-call | flops 28991029248 | bytes 1 | tf_op jit(solution)/shard_map/pallas_call | solution.py:334
  321.6 0.0 copy-start.4
  321.6 1.7 copy-done.4
  323.3 0.0 all-to-all-done.4
  323.3 3.2 all-to-all-start.6
  326.5 40.7 %shard_map.65 = bf16[2048,768]{1,0:T(8,128)(2,1)S(1)} custom-call(s32[3,16]{1,0:T(4,128)S(1)} %concatenate.3.bound_ref, bf16[2048,768]{1,0:T(8,128)(2,1)S(1)} %bitcast.21, bf16[2,768,3072]{2,1,0:T(8,128)(2,1)} %w1_hbm.7, bf16[2,768,3072]{2,1,0:T(8,128)(2,1)} %w3_hbm.7, bf16[2,3072,768]{2,1,0:T(8,128)(2,1)} %w2_hbm.7), custom_call_target="tpu_custom_call" | custom-call | flops 28991029248 | bytes 1 | tf_op jit(solution)/shard_map/pallas_call | solution.py:334
  367.2 0.0 copy-start.3
  367.2 1.7 copy-done.3
  368.8 0.0 all-to-all-done.6
  368.8 2.7 all-to-all-start.2
  371.5 23.7 %shard_map.70.refs_0_ = f32[2048,768]{1,0:T(8,128)} custom-call(s32[16]{0:T(128)} %reduce_sum.9.counts_ref, f32[2048,8]{1,0:T(8,128)} %get-tuple-element.12.cols_ref, bf16[2048,768]{1,0:T(8,128)(2,1)} %bitcast.20.back_ref), custom_call_target="tpu_custom_call" | custom-call | flops 12884901888 | bytes 1 | tf_op jit(solution)/shard_map/pallas_call | solution.py:359
  395.2 19.9 %shard_map.71.refs_0_ = f32[2048,768]{1,0:T(8,128)} custom-call(s32[16]{0:T(128)} %reduce_sum.9.counts_ref, f32[2048,8]{1,0:T(8,128)} %get-tuple-element.12.cols_ref, bf16[2048,768]{1,0:T(8,128)(2,1)} %bitcast.16.back_ref, f32[2048,768]{1,0:T(8,128)} %shard_map.70.refs_0_), custom_call_target="tpu_custom_call" | custom-call | flops 12884901888 | bytes 1 | tf_op jit(solution)/shard_map/pallas_call | solution.py:359
  415.1 11.9 %shard_map.72.refs_0_ = f32[2048,768]{1,0:T(8,128)} custom-call(s32[16]{0:T(128)} %reduce_sum.9.counts_ref, f32[2048,8]{1,0:T(8,128)} %get-tuple-element.12.cols_ref, bf16[2048,768]{1,0:T(8,128)(2,1)} %bitcast.12.back_ref, f32[2048,768]{1,0:T(8,128)} %shard_map.71.refs_0_), custom_call_target="tpu_custom_call" | custom-call | flops 12884901888 | bytes 1 | tf_op jit(solution)/shard_map/pallas_call | solution.py:359
  427.0 0.0 all-to-all-done.2
  427.0 0.0 copy-start.7
  427.0 1.7 copy-done.7
  428.7 11.2 %shard_map.73 = bf16[2048,768]{1,0:T(8,128)(2,1)} custom-call(s32[16]{0:T(128)} %reduce_sum.9.counts_ref, f32[2048,8]{1,0:T(8,128)} %get-tuple-element.12.cols_ref, bf16[2048,768]{1,0:T(8,128)(2,1)} %bitcast.29, f32[2048,768]{1,0:T(8,128)} %shard_map.72.refs_0_), custom_call_target="tpu_custom_call" | custom-call | flops 12884901888 | bytes 1 | tf_op jit(solution)/shard_map/pallas_call | solution.py:359
  (2 shorter events, 0.0 us)
Async XLA Ops:
  6.0 18.4 %all-to-all-start = ((s32[16,1,2]{2,1,0:T(1,128)}), s32[16,1,2]{2,1,0:T(1,128)S(1)}, u32[]{:S(2)}, u32[]{:S(2)}) async-start(s32[16,1,2]{2,1,0:T(1,128)} %bitcast.2), calls=%async_computation | async-start | bytes 16384 | tf_op jit(solution)/shard_map/all_to_all | solution.py:290
  24.4 43.3 %all-to-all-start.7 = ((bf16[16,128,768]{2,1,0:T(8,128)(2,1)}), bf16[16,128,768]{2,1,0:T(8,128)(2,1)S(1)}, u32[]{:S(2)}, u32[]{:S(2)}) async-start(bf16[16,128,768]{2,1,0:T(8,128)(2,1)} %bitcast.30), calls=%async_computation.7 | async-start | bytes 6291456 | tf_op jit(solution)/shard_map/all_to_all | solution.py:312
  67.7 41.2 %copy-start = (bf16[16,128,768]{2,1,0:T(8,128)(2,1)}, bf16[16,128,768]{2,1,0:T(8,128)(2,1)S(1)}, u32[]{:S(2)}) copy-start(bf16[16,128,768]{2,1,0:T(8,128)(2,1)S(1)} %all-to-all-done.7) | copy-start | bytes 9437188
  67.7 41.2 %copy-start.8 = (bf16[2048,768]{1,0:T(8,128)(2,1)S(1)}, bf16[2048,768]{1,0:T(8,128)(2,1)}, u32[]{:S(2)}) copy-start(bf16[2048,768]{1,0:T(8,128)(2,1)} %get-tuple-element.14) | copy-start | bytes 9437188
  148.9 49.8 %all-to-all-start.5 = ((bf16[16,128,768]{2,1,0:T(8,128)(2,1)}), bf16[16,128,768]{2,1,0:T(8,128)(2,1)}, u32[]{:S(2)}, u32[]{:S(2)}) async-start(bf16[16,128,768]{2,1,0:T(8,128)(2,1)} %bitcast.28), calls=%async_computation.5 | async-start | bytes 6291456 | tf_op jit(solution)/shard_map/all_to_all | solution.py:312
  154.7 1.9 copy-start.1
  197.1 1.7 copy-start.5
  198.8 69.2 %all-to-all-start.8 = ((bf16[16,128,768]{2,1,0:T(8,128)(2,1)}), bf16[16,128,768]{2,1,0:T(8,128)(2,1)}, u32[]{:S(2)}, u32[]{:S(2)}) async-start(bf16[16,128,768]{2,1,0:T(8,128)(2,1)} %bitcast.26), calls=%async_computation.8 | async-start | bytes 6291456 | tf_op jit(solution)/shard_map/all_to_all | solution.py:335
  215.3 1.9 copy-start.2
  266.3 1.7 copy-start.6
  268.0 55.3 %all-to-all-start.4 = ((bf16[16,128,768]{2,1,0:T(8,128)(2,1)}), bf16[16,128,768]{2,1,0:T(8,128)(2,1)}, u32[]{:S(2)}, u32[]{:S(2)}) async-start(bf16[16,128,768]{2,1,0:T(8,128)(2,1)} %bitcast.27), calls=%async_computation.4 | async-start | bytes 6291456 | tf_op jit(solution)/shard_map/all_to_all | solution.py:335
  321.6 1.7 copy-start.4
  323.3 45.6 %all-to-all-start.6 = ((bf16[16,128,768]{2,1,0:T(8,128)(2,1)}), bf16[16,128,768]{2,1,0:T(8,128)(2,1)}, u32[]{:S(2)}, u32[]{:S(2)}) async-start(bf16[16,128,768]{2,1,0:T(8,128)(2,1)} %bitcast.25), calls=%async_computation.6 | async-start | bytes 6291456 | tf_op jit(solution)/shard_map/all_to_all | solution.py:335
  367.2 1.7 copy-start.3
  368.8 58.2 %all-to-all-start.2 = ((bf16[16,128,768]{2,1,0:T(8,128)(2,1)}), bf16[16,128,768]{2,1,0:T(8,128)(2,1)S(1)}, u32[]{:S(2)}, u32[]{:S(2)}) async-start(bf16[16,128,768]{2,1,0:T(8,128)(2,1)} %bitcast.24), calls=%async_computation.2 | async-start | bytes 6291456 | tf_op jit(solution)/shard_map/all_to_all | solution.py:335
  427.0 1.7 copy-start.7

commit v3 on v2

--- a/solution.py
+++ b/solution.py
@@ -12,9 +12,9 @@
 BF16 = jnp.bfloat16
 I32 = jnp.int32
 TILE = 16
-CHUNKS = ((0, 128), (128, 128), (256, 128), (384, 128))
+CHUNKS = ((0, 256), (256, 256))
 VMEM_BYTES = 60 * 1024 * 1024
-FFN_VMEM = 44 * 1024 * 1024
+FFN_VMEM = 50 * 1024 * 1024
 
 
 def _dot(a, b):
@@ -123,7 +123,7 @@
 STEP = 256
 
 
-def ffn_kernel(start, size, n_src, bound_ref, x_ref, w1_hbm, w3_hbm, w2_hbm, out_ref, w1, w3, w2, xbuf, hbuf, ybuf, list_ref, used_ref, sems):
+def ffn_kernel(start, size, n_src, bound_ref, x_ref, w1_hbm, w3_hbm, w2_hbm, out_ref, w1, w3, w2, xbuf, hbuf, list_ref, used_ref, sems):
     n_loc, _, ff = w1.shape
     n_f = ff // WIDE
     per = size // TILE
@@ -203,7 +203,7 @@
                     for f in range(n_f):
                         columns(at, f)
 
-                ybuf[at, :] = _dot(hbuf[...], w2[e]).astype(BF16)
+                xbuf[at, :] = _dot(hbuf[...], w2[e]).astype(BF16)
 
             def put(k, _):
                 i = list_ref[k]
@@ -212,7 +212,7 @@
                 pos = t0 + lax.broadcasted_iota(I32, (TILE, 1), 0)
                 own = (pos >= bound_ref[e, s]) & (pos < bound_ref[e + 1, s])
                 at = pl.ds(pl.multiple_of(i * TILE, TILE), TILE)
-                y = ybuf[pl.ds(pl.multiple_of(k * TILE, TILE), TILE), :]
+                y = xbuf[pl.ds(pl.multiple_of(k * TILE, TILE), TILE), :]
                 out_ref[at, :] = jnp.where(own, y, out_ref[at, :])
                 return 0
 
@@ -321,7 +321,6 @@
                     pltpu.VMEM((local, ff, dim), BF16),
                     pltpu.VMEM((rows, dim), BF16),
                     pltpu.VMEM((STEP, ff), BF16),
-                    pltpu.VMEM((rows, dim), BF16),
                     pltpu.SMEM((rows // TILE,), I32),
                     pltpu.SMEM((local,), I32),
                     pltpu.SemaphoreType.DMA((local, 3, ff // WIDE)),

time: 442 us -> 412 us (0.932)
  waiting for transfers between devices: 20.7 us -> 104 us
  blocking collectives: 81.2 us -> 0 us
  starting transfers between devices: 39.2 us -> 19.3 us
  local copies, waits for them, and re-layouts: 13.8 us -> 7.43 us
  Pallas kernels: 284 us -> 279 us
    all_to_all x2 -> x0, blocking collectives: 81.2 us -> none  [body(): lax.all_to_all(sends[index].reshape(n, size, dim), 'ep', 0, 0, tiled=True)]
    all_to_all x2, waiting for transfers between devices: 20.7 us -> 65.9 us  [body(): lax.all_to_all(sends[index].reshape(n, size, dim), 'ep', 0, 0, tiled=True)]
    all_to_all x4 -> x2, waiting for transfers between devices: 0.01 us -> 37.9 us  [body(): lax.all_to_all(made.reshape(n, size, dim), 'ep', 0, 0, tiled=True)]
    all_to_all x4 -> x2, starting transfers between devices: 25.5 us -> 6.83 us  [body(): lax.all_to_all(made.reshape(n, size, dim), 'ep', 0, 0, tiled=True)]
    pallas_call x4 -> x2, Pallas kernels: 66.7 us -> 56.4 us  [body(): acc = combine(dev_counts, *ins)]
    unnamed x18 -> x4, local copies, waits for them, and re-layouts: 12.1 us -> 5.16 us
    pallas_call x4 -> x2, Pallas kernels: 181 us -> 185 us  [body(): made(bounds, got, *[pltpu.with_memory_space_constraint(w, pltpu.HBM) for...]
  transfers between devices with their start and end apart: 7 -> 5, of which waited for: 1 -> 2; matrix products, arithmetic and copies ran while one was open for 0% -> 0% of each run, Pallas kernels for 61% -> 63%
where the time goes in v3:
time: 412 us; the launch traced here: 410 us
  Pallas kernels  279 us (68%)
  waiting for transfers between devices  104 us (25%)
  starting transfers between devices  19.3 us (5%)
  local copies, waits for them, and re-layouts  7.43 us (2%)
    pallas_call x2, Pallas kernels, body(): made(bounds, got, *[pltpu.with_memory_space_constraint(w, pltpu.HBM) for...  185 us
    all_to_all x2, waiting for transfers between devices, body(): lax.all_to_all(sends[index].reshape(n, size, dim), 'ep', 0, 0, tiled=True)  65.9 us
    pallas_call x2, Pallas kernels, body(): acc = combine(dev_counts, *ins)  56.4 us
    all_to_all x2, waiting for transfers between devices, body(): lax.all_to_all(made.reshape(n, size, dim), 'ep', 0, 0, tiled=True)  37.9 us
    pallas_call x2, Pallas kernels, body(): sends += pack(dev_counts, slots, x)  32.1 us
    all_to_all x2, starting transfers between devices, body(): lax.all_to_all(sends[index].reshape(n, size, dim), 'ep', 0, 0, tiled=True)  8.34 us
  transfers between devices with their start and end apart: 5, of which 2 were waited for; matrix products, arithmetic and copies ran while one was open for 0% of the time, Pallas kernels for 63%

profile of v3, /device:TPU:11, one launch (start us, length us, event | category | flops | bytes accessed | tf_op | source)
XLA Modules:
  0.0 409.8 jit_solution(9900669762003954498)
XLA Ops:
  0.0 4.6 %route.1 = (s32[8,2048]{1,0:T(8,128)}, f32[2048,8]{1,0:T(8,128)}, s32[32,128]{1,0:T(8,128)}) custom-call(bf16[2048,768]{1,0:T(8,128)(2,1)} %x_ref.5, f32[32,768]{1,0:T(8,128)} %bitcast.17, s32[2,2048]{1,0:T(2,128)} %bitcast.18), custom_call_target="tpu_custom_call" | custom-call | tf_op jit(solution)/shard_map/route/pallas_call | solution.py:280
  4.6 0.8 slice_reduce_fusion
  5.4 0.7 all_to_all.20
  6.1 4.2 %all-to-all-start = ((s32[16,1,2]{2,1,0:T(1,128)}), s32[16,1,2]{2,1,0:T(1,128)S(1)}, u32[]{:S(2)}, u32[]{:S(2)}) async-start(s32[16,1,2]{2,1,0:T(1,128)} %bitcast.2), calls=%async_computation | async-start | bytes 16384 | tf_op jit(solution)/shard_map/all_to_all | solution.py:290
  10.3 0.1 reshape_squeeze.4
  10.4 0.7 reduce_sum.9.counts_ref
  11.0 21.0 %shard_map.66 = bf16[4096,768]{1,0:T(8,128)(2,1)} custom-call(s32[16]{0:T(128)} %reduce_sum.9.counts_ref, s32[8,2048]{1,0:T(8,128)} %get-tuple-element.10.slot_ref, bf16[2048,768]{1,0:T(8,128)(2,1)} %x_ref.5), custom_call_target="tpu_custom_call" | custom-call | flops 12884901888 | bytes 1 | tf_op jit(solution)/shard_map/pallas_call | solution.py:309
  32.1 0.0 all-to-all-done
  32.1 3.8 all-to-all-start.3
  35.9 11.1 %shard_map.64 = bf16[4096,768]{1,0:T(8,128)(2,1)} custom-call(s32[16]{0:T(128)} %reduce_sum.9.counts_ref, s32[8,2048]{1,0:T(8,128)} %get-tuple-element.10.slot_ref, bf16[2048,768]{1,0:T(8,128)(2,1)} %x_ref.5), custom_call_target="tpu_custom_call" | custom-call | flops 12884901888 | bytes 1 | tf_op jit(solution)/shard_map/pallas_call | solution.py:309
  47.0 65.9 %all-to-all-done.3 = bf16[16,256,768]{2,1,0:T(8,128)(2,1)} async-done(((bf16[16,256,768]{2,1,0:T(8,128)(2,1)}), bf16[16,256,768]{2,1,0:T(8,128)(2,1)}, u32[]{:S(2)}, u32[]{:S(2)}) %all-to-all-start.3) | async-done | bytes 6291488 | tf_op jit(solution)/shard_map/all_to_all | solution.py:312
  112.8 4.5 %all-to-all-start.1 = ((bf16[16,256,768]{2,1,0:T(8,128)(2,1)}), bf16[16,256,768]{2,1,0:T(8,128)(2,1)}, u32[]{:S(2)}, u32[]{:S(2)}) async-start(bf16[16,256,768]{2,1,0:T(8,128)(2,1)} %bitcast.15), calls=%async_computation.1 | async-start | bytes 12582912 | tf_op jit(solution)/shard_map/all_to_all | solution.py:312
  117.4 0.1 copy.10
  117.5 0.6 concatenate.3.bound_ref
  118.1 92.6 %shard_map.67 = bf16[4096,768]{1,0:T(8,128)(2,1)S(1)} custom-call(s32[3,16]{1,0:T(4,128)} %concatenate.3.bound_ref, bf16[4096,768]{1,0:T(8,128)(2,1)} %bitcast.10.x_ref, bf16[2,768,3072]{2,1,0:T(8,128)(2,1)} %w1_hbm.3, bf16[2,768,3072]{2,1,0:T(8,128)(2,1)} %w3_hbm.3, bf16[2,3072,768]{2,1,0:T(8,128)(2,1)} %w2_hbm.3), custom_call_target="tpu_custom_call" | custom-call | flops 57982058496 | bytes 1 | tf_op jit(solution)/shard_map/pallas_call | solution.py:333
  210.6 0.0 copy-start.1
  210.6 2.6 copy-done.1
  213.2 0.0 all-to-all-done.1
  213.2 3.4 all-to-all-start.4
  216.7 92.8 %shard_map.65 = bf16[4096,768]{1,0:T(8,128)(2,1)S(1)} custom-call(s32[3,16]{1,0:T(4,128)} %concatenate.3.bound_ref, bf16[4096,768]{1,0:T(8,128)(2,1)} %bitcast.6.x_ref, bf16[2,768,3072]{2,1,0:T(8,128)(2,1)} %w1_hbm.3, bf16[2,768,3072]{2,1,0:T(8,128)(2,1)} %w3_hbm.3, bf16[2,3072,768]{2,1,0:T(8,128)(2,1)} %w2_hbm.3), custom_call_target="tpu_custom_call" | custom-call | flops 57982058496 | bytes 1 | tf_op jit(solution)/shard_map/pallas_call | solution.py:333
  309.5 0.0 copy-start
  309.5 2.6 copy-done
  312.1 0.0 all-to-all-done.4
  312.1 3.4 all-to-all-start.2
  315.5 39.1 %shard_map.68.refs_0_ = f32[2048,768]{1,0:T(8,128)} custom-call(s32[16]{0:T(128)} %reduce_sum.9.counts_ref, f32[2048,8]{1,0:T(8,128)} %get-tuple-element.9.cols_ref, bf16[4096,768]{1,0:T(8,128)(2,1)} %bitcast.12.back_ref), custom_call_target="tpu_custom_call" | custom-call | flops 25769803776 | bytes 1 | tf_op jit(solution)/shard_map/pallas_call | solution.py:358
  354.6 37.9 %all-to-all-done.2 = bf16[16,256,768]{2,1,0:T(8,128)(2,1)} async-done(((bf16[16,256,768]{2,1,0:T(8,128)(2,1)}), bf16[16,256,768]{2,1,0:T(8,128)(2,1)}, u32[]{:S(2)}, u32[]{:S(2)}) %all-to-all-start.2) | async-done | bytes 6291488 | tf_op jit(solution)/shard_map/all_to_all | solution.py:334
  392.5 17.3 %shard_map.69 = bf16[2048,768]{1,0:T(8,128)(2,1)} custom-call(s32[16]{0:T(128)} %reduce_sum.9.counts_ref, f32[2048,8]{1,0:T(8,128)} %get-tuple-element.9.cols_ref, bf16[4096,768]{1,0:T(8,128)(2,1)} %bitcast.8.back_ref, f32[2048,768]{1,0:T(8,128)} %shard_map.68.refs_0_), custom_call_target="tpu_custom_call" | custom-call | flops 25769803776 | bytes 1 | tf_op jit(solution)/shard_map/pallas_call | solution.py:358
  (1 shorter events, 0.0 us)
Async XLA Ops:
  6.1 25.9 %all-to-all-start = ((s32[16,1,2]{2,1,0:T(1,128)}), s32[16,1,2]{2,1,0:T(1,128)S(1)}, u32[]{:S(2)}, u32[]{:S(2)}) async-start(s32[16,1,2]{2,1,0:T(1,128)} %bitcast.2), calls=%async_computation | async-start | bytes 16384 | tf_op jit(solution)/shard_map/all_to_all | solution.py:290
  32.1 80.8 %all-to-all-start.3 = ((bf16[16,256,768]{2,1,0:T(8,128)(2,1)}), bf16[16,256,768]{2,1,0:T(8,128)(2,1)}, u32[]{:S(2)}, u32[]{:S(2)}) async-start(bf16[16,256,768]{2,1,0:T(8,128)(2,1)} %bitcast.16), calls=%async_computation.3 | async-start | bytes 12582912 | tf_op jit(solution)/shard_map/all_to_all | solution.py:312
  112.8 100.4 %all-to-all-start.1 = ((bf16[16,256,768]{2,1,0:T(8,128)(2,1)}), bf16[16,256,768]{2,1,0:T(8,128)(2,1)}, u32[]{:S(2)}, u32[]{:S(2)}) async-start(bf16[16,256,768]{2,1,0:T(8,128)(2,1)} %bitcast.15), calls=%async_computation.1 | async-start | bytes 12582912 | tf_op jit(solution)/shard_map/all_to_all | solution.py:312
  210.6 2.6 copy-start.1
  213.2 98.9 %all-to-all-start.4 = ((bf16[16,256,768]{2,1,0:T(8,128)(2,1)}), bf16[16,256,768]{2,1,0:T(8,128)(2,1)}, u32[]{:S(2)}, u32[]{:S(2)}) async-start(bf16[16,256,768]{2,1,0:T(8,128)(2,1)} %bitcast.14), calls=%async_computation.4 | async-start | bytes 12582912 | tf_op jit(solution)/shard_map/all_to_all | solution.py:334
  309.5 2.6 copy-start
  312.1 80.4 %all-to-all-start.2 = ((bf16[16,256,768]{2,1,0:T(8,128)(2,1)}), bf16[16,256,768]{2,1,0:T(8,128)(2,1)}, u32[]{:S(2)}, u32[]{:S(2)}) async-start(bf16[16,256,768]{2,1,0:T(8,128)(2,1)} %bitcast.13), calls=%async_computation.2 | async-start | bytes 12582912 | tf_op jit(solution)/shard_map/all_to_all | solution.py:334

commit v4 on v3

--- a/solution.py
+++ b/solution.py
@@ -14,7 +14,6 @@
 TILE = 16
 CHUNKS = ((0, 256), (256, 256))
 VMEM_BYTES = 60 * 1024 * 1024
-FFN_VMEM = 50 * 1024 * 1024
 
 
 def _dot(a, b):
@@ -120,10 +119,11 @@
 
 
 WIDE = 512
-STEP = 256
-
-
-def ffn_kernel(start, size, n_src, bound_ref, x_ref, w1_hbm, w3_hbm, w2_hbm, out_ref, w1, w3, w2, xbuf, hbuf, list_ref, used_ref, sems):
+GROUP = 16
+STEP = GROUP * TILE
+
+
+def ffn_kernel(start, size, n_src, bound_ref, x_hbm, w1_hbm, w3_hbm, w2_hbm, out_ref, x_ref, w1, w3, w2, xbuf, hbuf, list_ref, low_ref, high_ref, used_ref, sems, x_sems):
     n_loc, _, ff = w1.shape
     n_f = ff // WIDE
     per = size // TILE
@@ -133,6 +133,15 @@
         at = (e, cut) if which == 2 else (e, slice(None), cut)
         src, dst = ((w1_hbm, w1), (w3_hbm, w3), (w2_hbm, w2))[which]
         return pltpu.make_async_copy(src.at[at], dst.at[at], sems.at[e, which, f])
+
+    quarter = x_ref.shape[0] // 4
+
+    def row_copy(q):
+        at = pl.ds(q * quarter, quarter)
+        return pltpu.make_async_copy(x_hbm.at[at], x_ref.at[at], x_sems.at[q])
+
+    for q in range(4):
+        row_copy(q).start()
 
     @pl.loop(0, n_loc)
     def _(e):
@@ -155,68 +164,74 @@
                 copy(e, 2, f).start()
 
     out_ref[...] = jnp.zeros_like(out_ref)
+    for q in range(4):
+        row_copy(q).wait()
 
     @pl.loop(0, n_loc)
     def _(e):
         @pl.when(used_ref[e] > 0)
         def _():
-            def collect(i, cnt):
-                s = i // per
-                t0 = start + (i % per) * TILE
-                lo = bound_ref[e, s]
-                hi = bound_ref[e + 1, s]
-                hit = (lo < t0 + TILE) & (hi > t0) & (hi > lo)
-
-                @pl.when(hit)
-                def _():
-                    list_ref[cnt] = i
-                    here = pl.ds(pl.multiple_of(i * TILE, TILE), TILE)
-                    xbuf[pl.ds(pl.multiple_of(cnt * TILE, TILE), TILE), :] = x_ref[here, :]
-
-                return cnt + hit.astype(I32)
-
-            cnt = lax.fori_loop(0, n_src * per, collect, jnp.int32(0))
-
-            def columns(at, f):
+            def collect(s, cnt):
+                lo = jnp.clip(bound_ref[e, s] - start, 0, size)
+                hi = jnp.clip(bound_ref[e + 1, s] - start, 0, size)
+                t_lo = lo // TILE
+                t_hi = jnp.where(hi > lo, (hi + TILE - 1) // TILE, t_lo)
+
+                def add(t, k):
+                    list_ref[k] = s * per + t
+                    low_ref[k] = lo - t * TILE
+                    high_ref[k] = hi - t * TILE
+                    return k + 1
+
+                return lax.fori_loop(t_lo, t_hi, add, cnt)
+
+            cnt = lax.fori_loop(0, n_src, collect, jnp.int32(0))
+            groups = (cnt + GROUP - 1) // GROUP
+
+            @pl.loop(cnt, groups * GROUP)
+            def _(k):
+                list_ref[k] = 0
+                low_ref[k] = 0
+                high_ref[k] = 0
+
+            def tile_of(g, j):
+                return pl.ds(pl.multiple_of(list_ref[g * GROUP + j] * TILE, TILE), TILE)
+
+            def columns(f):
                 cut = pl.ds(f * WIDE if isinstance(f, int) else pl.multiple_of(f * WIDE, WIDE), WIDE)
-                xb = xbuf[at, :]
+                xb = xbuf[...]
                 u = _dot(xb, w1[e, :, cut])
                 v = _dot(xb, w3[e, :, cut])
                 hbuf[:, cut] = (u * jax.nn.sigmoid(u) * v).astype(BF16)
 
-            @pl.loop(0, n_f)
-            def _(f):
-                copy(e, 0, f).wait()
-                copy(e, 1, f).wait()
-                columns(pl.ds(0, STEP), f)
-
-            @pl.loop(0, n_f)
-            def _(f):
-                copy(e, 2, f).wait()
-
-            @pl.loop(0, (cnt * TILE + STEP - 1) // STEP)
+            @pl.loop(0, groups)
             def _(g):
-                at = pl.ds(pl.multiple_of(g * STEP, STEP), STEP)
+                for j in range(GROUP):
+                    xbuf[j * TILE : (j + 1) * TILE, :] = x_ref[tile_of(g, j), :]
+
+                @pl.when(g == 0)
+                def _():
+                    @pl.loop(0, n_f)
+                    def _(f):
+                        copy(e, 0, f).wait()
+                        copy(e, 1, f).wait()
+                        columns(f)
+
+                    @pl.loop(0, n_f)
+                    def _(f):
+                        copy(e, 2, f).wait()
 
                 @pl.when(g > 0)
                 def _():
                     for f in range(n_f):
-                        columns(at, f)
-
-                xbuf[at, :] = _dot(hbuf[...], w2[e]).astype(BF16)
-
-            def put(k, _):
-                i = list_ref[k]
-                s = i // per
-                t0 = start + (i % per) * TILE
-                pos = t0 + lax.broadcasted_iota(I32, (TILE, 1), 0)
-                own = (pos >= bound_ref[e, s]) & (pos < bound_ref[e + 1, s])
-                at = pl.ds(pl.multiple_of(i * TILE, TILE), TILE)
-                y = xbuf[pl.ds(pl.multiple_of(k * TILE, TILE), TILE), :]
-                out_ref[at, :] = jnp.where(own, y, out_ref[at, :])
-                return 0
-
-            lax.fori_loop(0, cnt, put, 0)
+                        columns(f)
+
+                y = _dot(hbuf[...], w2[e]).astype(BF16)
+                row = lax.broadcasted_iota(I32, (TILE, 1), 0)
+                for j in range(GROUP):
+                    own = (row >= low_ref[g * GROUP + j]) & (row < high_ref[g * GROUP + j])
+                    at = tile_of(g, j)
+                    out_ref[at, :] = jnp.where(own, y[j * TILE : (j + 1) * TILE], out_ref[at, :])
 
 
 def combine_kernel(row_cap, start, size, n_dev, has_acc, counts_ref, cols_ref, back_ref, *refs):
@@ -229,18 +244,13 @@
 
     @pl.when(pl.program_id(0) == 0)
     def _():
-        def bring(i, k):
-            src = pl.ds(pl.multiple_of(i * SLOT_TILE, SLOT_TILE), SLOT_TILE)
-            rows_ref[pl.ds(pl.multiple_of(k * SLOT_TILE, SLOT_TILE), SLOT_TILE), :] = back_ref[src, :]
-
-        cnt = list_tiles(n_dev, size, start, counts_ref, list_ref, bring)
+        cnt = list_tiles(n_dev, size, start, counts_ref, list_ref)
         groups = (cnt + SUM_GROUP - 1) // SUM_GROUP
         cnt_ref[0] = groups
 
         @pl.loop(cnt, groups * SUM_GROUP)
         def _(k):
             list_ref[k] = -1
-            rows_ref[pl.ds(pl.multiple_of(k * SLOT_TILE, SLOT_TILE), SLOT_TILE), :] = jnp.zeros((SLOT_TILE, dim), BF16)
 
     c = cols_ref[...]
     sum_ref[...] = acc_ref[...] if has_acc else jnp.zeros((toks, dim), F32)
@@ -248,12 +258,14 @@
 
     @pl.loop(0, cnt_ref[0])
     def _(g):
-        rows = rows_ref[pl.ds(pl.multiple_of(g * group, group), group), :]
         ids = jnp.full((1, group), -1, I32)
         for j in range(SUM_GROUP):
             i = list_ref[g * SUM_GROUP + j]
             base = jnp.where(i < 0, -1 - group, first_slot(i, size, start, row_cap))
             ids = jnp.where(lane // SLOT_TILE == j, base + lane % SLOT_TILE, ids)
+            src = pl.ds(pl.multiple_of(jnp.maximum(i, 0) * SLOT_TILE, SLOT_TILE), SLOT_TILE)
+            rows_ref[j * SLOT_TILE : (j + 1) * SLOT_TILE, :] = back_ref[src, :]
+        rows = rows_ref[...]
         ids = ids.astype(F32)
         add = 0.0
         for k in range(2):
@@ -313,24 +325,27 @@
             rows = n * size
             made = pl.pallas_call(
                 functools.partial(ffn_kernel, start, size, n),
-                in_specs=[smem, vmem, hbm, hbm, hbm],
+                in_specs=[smem, hbm, hbm, hbm, hbm],
                 out_specs=vmem,
                 scratch_shapes=[
+                    pltpu.VMEM((rows, dim), BF16),
                     pltpu.VMEM((local, dim, ff), BF16),
                     pltpu.VMEM((local, dim, ff), BF16),
                     pltpu.VMEM((local, ff, dim), BF16),
-                    pltpu.VMEM((rows, dim), BF16),
+                    pltpu.VMEM((STEP, dim), BF16),
                     pltpu.VMEM((STEP, ff), BF16),
-                    pltpu.SMEM((rows // TILE,), I32),
+                    pltpu.SMEM((rows // TILE + GROUP,), I32),
+                    pltpu.SMEM((rows // TILE + GROUP,), I32),
+                    pltpu.SMEM((rows // TILE + GROUP,), I32),
                     pltpu.SMEM((local,), I32),
                     pltpu.SemaphoreType.DMA((local, 3, ff // WIDE)),
+                    pltpu.SemaphoreType.DMA((4,)),
                 ],
-                out_shape=pltpu.VMEM((rows, dim), BF16),
-                compiler_params=_params(FFN_VMEM),
+                out_shape=jax.ShapeDtypeStruct((rows, dim), BF16),
+                compiler_params=_params(),
                 cost_estimate=pl.CostEstimate(flops=6 * rows * dim * ff, bytes_accessed=1, transcendentals=0),
             )
-            got = pltpu.with_memory_space_constraint(got.reshape(rows, dim), pltpu.VMEM)
-            made = made(bounds, got, *[pltpu.with_memory_space_constraint(w, pltpu.HBM) for w in (w1, w3, w2)])
+            made = made(bounds, got.reshape(rows, dim), w1, w3, w2)
             back = lax.all_to_all(made.reshape(n, size, dim), "ep", 0, 0, tiled=True).reshape(rows, dim)
             last = index == len(CHUNKS) - 1
             tb = 512
@@ -345,7 +360,7 @@
                     in_specs=specs + ([] if acc is None else [tile_spec]),
                     out_specs=tile_spec,
                     scratch_shapes=[
-                        pltpu.VMEM((rows, dim), BF16),
+                        pltpu.VMEM((SUM_GROUP * SLOT_TILE, dim), BF16),
                         pltpu.VMEM((tb, dim), F32),
                         pltpu.SMEM((rows // SLOT_TILE,), I32),
                         pltpu.SMEM((1,), I32),

time: 412 us -> 379 us (0.920)
  Pallas kernels: 279 us -> 248 us
  local copies, waits for them, and re-layouts: 7.43 us -> 2.26 us
    pallas_call x2, Pallas kernels: 185 us -> 160 us  [body(): made = made(bounds, got.reshape(rows, dim), w1, w3, w2)]
    pallas_call x2, Pallas kernels: 56.4 us -> 51.1 us  [body(): acc = combine(dev_counts, *ins)]
    unnamed x4 -> x0, local copies, waits for them, and re-layouts: 5.16 us -> none
  transfers between devices with their start and end apart: 5 -> 5, of which waited for: 2 -> 2; matrix products, arithmetic and copies ran while one was open for 0% -> 0% of each run, Pallas kernels for 63% -> 61%
where the time goes in v4:
time: 379 us; the launch traced here: 377 us
  Pallas kernels  248 us (65%)
  waiting for transfers between devices  107 us (28%)
  starting transfers between devices  19.4 us (5%)
    pallas_call x2, Pallas kernels, body(): made = made(bounds, got.reshape(rows, dim), w1, w3, w2)  160 us
    all_to_all x2, waiting for transfers between devices, body(): lax.all_to_all(sends[index].reshape(n, size, dim), 'ep', 0, 0, tiled=True)  65.9 us
    pallas_call x2, Pallas kernels, body(): acc = combine(dev_counts, *ins)  51.1 us
    all_to_all x2, waiting for transfers between devices, body(): lax.all_to_all(made.reshape(n, size, dim), 'ep', 0, 0, tiled=True)  40.6 us
    pallas_call x2, Pallas kernels, body(): sends += pack(dev_counts, slots, x)  32.1 us
    all_to_all x2, starting transfers between devices, body(): lax.all_to_all(sends[index].reshape(n, size, dim), 'ep', 0, 0, tiled=True)  8.34 us
  transfers between devices with their start and end apart: 5, of which 2 were waited for; matrix products, arithmetic and copies ran while one was open for 0% of the time, Pallas kernels for 61%

profile of v4, /device:TPU:11, one launch (start us, length us, event | category | flops | bytes accessed | tf_op | source)
XLA Modules:
  0.0 377.1 jit_solution(2984962303055520958)
XLA Ops:
  0.0 4.6 %route.1 = (s32[8,2048]{1,0:T(8,128)}, f32[2048,8]{1,0:T(8,128)}, s32[32,128]{1,0:T(8,128)}) custom-call(bf16[2048,768]{1,0:T(8,128)(2,1)} %x_ref.5, f32[32,768]{1,0:T(8,128)} %bitcast.17, s32[2,2048]{1,0:T(2,128)} %bitcast.18), custom_call_target="tpu_custom_call" | custom-call | tf_op jit(solution)/shard_map/route/pallas_call | solution.py:292
  4.6 0.8 slice_reduce_fusion
  5.4 0.7 all_to_all.20
  6.1 4.2 %all-to-all-start = ((s32[16,1,2]{2,1,0:T(1,128)}), s32[16,1,2]{2,1,0:T(1,128)S(1)}, u32[]{:S(2)}, u32[]{:S(2)}) async-start(s32[16,1,2]{2,1,0:T(1,128)} %bitcast.2), calls=%async_computation | async-start | bytes 16384 | tf_op jit(solution)/shard_map/all_to_all | solution.py:302
  10.3 0.1 reshape_squeeze.4
  10.4 0.7 reduce_sum.9.counts_ref
  11.1 21.0 %shard_map.66 = bf16[4096,768]{1,0:T(8,128)(2,1)} custom-call(s32[16]{0:T(128)} %reduce_sum.9.counts_ref, s32[8,2048]{1,0:T(8,128)} %get-tuple-element.10.slot_ref, bf16[2048,768]{1,0:T(8,128)(2,1)} %x_ref.5), custom_call_target="tpu_custom_call" | custom-call | flops 12884901888 | bytes 1 | tf_op jit(solution)/shard_map/pallas_call | solution.py:321
  32.1 0.0 all-to-all-done
  32.1 3.8 %all-to-all-start.3 = ((bf16[16,256,768]{2,1,0:T(8,128)(2,1)}), bf16[16,256,768]{2,1,0:T(8,128)(2,1)}, u32[]{:S(2)}, u32[]{:S(2)}) async-start(bf16[16,256,768]{2,1,0:T(8,128)(2,1)} %bitcast.16), calls=%async_computation.3 | async-start | bytes 12582912 | tf_op jit(solution)/shard_map/all_to_all | solution.py:324
  35.9 11.0 %shard_map.64 = bf16[4096,768]{1,0:T(8,128)(2,1)} custom-call(s32[16]{0:T(128)} %reduce_sum.9.counts_ref, s32[8,2048]{1,0:T(8,128)} %get-tuple-element.10.slot_ref, bf16[2048,768]{1,0:T(8,128)(2,1)} %x_ref.5), custom_call_target="tpu_custom_call" | custom-call | flops 12884901888 | bytes 1 | tf_op jit(solution)/shard_map/pallas_call | solution.py:321
  47.0 65.9 %all-to-all-done.3 = bf16[16,256,768]{2,1,0:T(8,128)(2,1)} async-done(((bf16[16,256,768]{2,1,0:T(8,128)(2,1)}), bf16[16,256,768]{2,1,0:T(8,128)(2,1)}, u32[]{:S(2)}, u32[]{:S(2)}) %all-to-all-start.3) | async-done | bytes 6291488 | tf_op jit(solution)/shard_map/all_to_all | solution.py:324
  112.9 4.5 %all-to-all-start.1 = ((bf16[16,256,768]{2,1,0:T(8,128)(2,1)}), bf16[16,256,768]{2,1,0:T(8,128)(2,1)}, u32[]{:S(2)}, u32[]{:S(2)}) async-start(bf16[16,256,768]{2,1,0:T(8,128)(2,1)} %bitcast.13), calls=%async_computation.1 | async-start | bytes 12582912 | tf_op jit(solution)/shard_map/all_to_all | solution.py:324
  117.4 0.1 copy.10
  117.5 0.6 concatenate.3.bound_ref
  118.1 79.3 %shard_map.67 = bf16[4096,768]{1,0:T(8,128)(2,1)} custom-call(s32[3,16]{1,0:T(4,128)} %concatenate.3.bound_ref, bf16[4096,768]{1,0:T(8,128)(2,1)} %bitcast.10.x_hbm, bf16[2,768,3072]{2,1,0:T(8,128)(2,1)} %w1_hbm.3, bf16[2,768,3072]{2,1,0:T(8,128)(2,1)} %w3_hbm.3, bf16[2,3072,768]{2,1,0:T(8,128)(2,1)} %w2_hbm.3), custom_call_target="tpu_custom_call" | custom-call | flops 57982058496 | bytes 1 | tf_op jit(solution)/shard_map/pallas_call | solution.py:348
  197.4 0.0 all-to-all-done.1
  197.4 3.5 all-to-all-start.4
  200.9 81.0 %shard_map.65 = bf16[4096,768]{1,0:T(8,128)(2,1)} custom-call(s32[3,16]{1,0:T(4,128)} %concatenate.3.bound_ref, bf16[4096,768]{1,0:T(8,128)(2,1)} %bitcast.6.x_hbm, bf16[2,768,3072]{2,1,0:T(8,128)(2,1)} %w1_hbm.3, bf16[2,768,3072]{2,1,0:T(8,128)(2,1)} %w3_hbm.3, bf16[2,3072,768]{2,1,0:T(8,128)(2,1)} %w2_hbm.3), custom_call_target="tpu_custom_call" | custom-call | flops 57982058496 | bytes 1 | tf_op jit(solution)/shard_map/pallas_call | solution.py:348
  281.9 0.0 all-to-all-done.4
  281.9 3.4 all-to-all-start.2
  285.4 36.4 %shard_map.68.refs_0_ = f32[2048,768]{1,0:T(8,128)} custom-call(s32[16]{0:T(128)} %reduce_sum.9.counts_ref, f32[2048,8]{1,0:T(8,128)} %get-tuple-element.9.cols_ref, bf16[4096,768]{1,0:T(8,128)(2,1)} %bitcast.12.back_ref), custom_call_target="tpu_custom_call" | custom-call | flops 25769803776 | bytes 1 | tf_op jit(solution)/shard_map/pallas_call | solution.py:373
  321.8 40.6 %all-to-all-done.2 = bf16[16,256,768]{2,1,0:T(8,128)(2,1)} async-done(((bf16[16,256,768]{2,1,0:T(8,128)(2,1)}), bf16[16,256,768]{2,1,0:T(8,128)(2,1)}, u32[]{:S(2)}, u32[]{:S(2)}) %all-to-all-start.2) | async-done | bytes 6291488 | tf_op jit(solution)/shard_map/all_to_all | solution.py:349
  362.4 14.7 %shard_map.69 = bf16[2048,768]{1,0:T(8,128)(2,1)} custom-call(s32[16]{0:T(128)} %reduce_sum.9.counts_ref, f32[2048,8]{1,0:T(8,128)} %get-tuple-element.9.cols_ref, bf16[4096,768]{1,0:T(8,128)(2,1)} %bitcast.8.back_ref, f32[2048,768]{1,0:T(8,128)} %shard_map.68.refs_0_), custom_call_target="tpu_custom_call" | custom-call | flops 25769803776 | bytes 1 | tf_op jit(solution)/shard_map/pallas_call | solution.py:373
  (1 shorter events, 0.0 us)
Async XLA Ops:
  6.1 26.0 %all-to-all-start = ((s32[16,1,2]{2,1,0:T(1,128)}), s32[16,1,2]{2,1,0:T(1,128)S(1)}, u32[]{:S(2)}, u32[]{:S(2)}) async-start(s32[16,1,2]{2,1,0:T(1,128)} %bitcast.2), calls=%async_computation | async-start | bytes 16384 | tf_op jit(solution)/shard_map/all_to_all | solution.py:302
  32.1 80.8 %all-to-all-start.3 = ((bf16[16,256,768]{2,1,0:T(8,128)(2,1)}), bf16[16,256,768]{2,1,0:T(8,128)(2,1)}, u32[]{:S(2)}, u32[]{:S(2)}) async-start(bf16[16,256,768]{2,1,0:T(8,128)(2,1)} %bitcast.16), calls=%async_computation.3 | async-start | bytes 12582912 | tf_op jit(solution)/shard_map/all_to_all | solution.py:324
  112.9 84.5 %all-to-all-start.1 = ((bf16[16,256,768]{2,1,0:T(8,128)(2,1)}), bf16[16,256,768]{2,1,0:T(8,128)(2,1)}, u32[]{:S(2)}, u32[]{:S(2)}) async-start(bf16[16,256,768]{2,1,0:T(8,128)(2,1)} %bitcast.13), calls=%async_computation.1 | async-start | bytes 12582912 | tf_op jit(solution)/shard_map/all_to_all | solution.py:324
  197.4 84.5 %all-to-all-start.4 = ((bf16[16,256,768]{2,1,0:T(8,128)(2,1)}), bf16[16,256,768]{2,1,0:T(8,128)(2,1)}, u32[]{:S(2)}, u32[]{:S(2)}) async-start(bf16[16,256,768]{2,1,0:T(8,128)(2,1)} %bitcast.15), calls=%async_computation.4 | async-start | bytes 12582912 | tf_op jit(solution)/shard_map/all_to_all | solution.py:349
  281.9 80.5 %all-to-all-start.2 = ((bf16[16,256,768]{2,1,0:T(8,128)(2,1)}), bf16[16,256,768]{2,1,0:T(8,128)(2,1)}, u32[]{:S(2)}, u32[]{:S(2)}) async-start(bf16[16,256,768]{2,1,0:T(8,128)(2,1)} %bitcast.14), calls=%async_computation.2 | async-start | bytes 12582912 | tf_op jit(solution)/shard_map/all_to_all | solution.py:349

commit v5 on v4

--- a/solution.py
+++ b/solution.py
@@ -70,7 +70,6 @@
 
 
 SLOT_TILE = 32
-PACK_GROUP = 8
 SUM_GROUP = 16
 
 
@@ -96,31 +95,112 @@
     return (i // per) * row_cap + start + (i % per) * SLOT_TILE
 
 
-def pack_kernel(row_cap, chunks, counts_ref, slot_ref, x_ref, *refs):
-    out_refs, list_ref = refs[:-1], refs[-1]
-    tok = x_ref.shape[0]
-    for (start, size), out_ref in zip(chunks, out_refs):
-        n_dev = out_ref.shape[0] // size
-        list_ref[0] = 0
-        cnt = list_tiles(n_dev, size, start, counts_ref, list_ref)
-        last = jnp.maximum(cnt - 1, 0)
-
-        @pl.loop(0, (cnt + PACK_GROUP - 1) // PACK_GROUP)
-        def _(g):
-            tiles = [list_ref[jnp.minimum(g * PACK_GROUP + j, last)] for j in range(PACK_GROUP)]
-            pos = lax.broadcasted_iota(I32, (SLOT_TILE, tok), 0)
-            want = jnp.concatenate([pos + first_slot(i, size, start, row_cap) for i in tiles], axis=0)
-            hit = (want == slot_ref[0:1, :]) | (want == slot_ref[1:2, :])
-            pick = jnp.where(hit, 1.0, 0.0).astype(BF16)
-            rows = _dot(pick, x_ref[...]).astype(BF16)
-            for j, i in enumerate(tiles):
-                at = pl.ds(pl.multiple_of(i * SLOT_TILE, SLOT_TILE), SLOT_TILE)
-                out_ref[at, :] = rows[j * SLOT_TILE : (j + 1) * SLOT_TILE]
-
-
 WIDE = 512
 GROUP = 16
 STEP = GROUP * TILE
+
+
+MESH = pl.DeviceIdType.MESH
+
+
+def partner(me, offset):
+    other = me
+    for bit in (1, 2, 4, 8):
+        other = other + ((offset // bit) % 2) * (bit - 2 * bit * ((me // bit) % 2))
+    return other
+
+
+def pair_of(p):
+    j, r = (p - 1) // 2, (p - 1) % 2
+    near = 8 - 4 * j + 2 * (j // 2)
+    return 14 - near + r, near + r
+
+
+def ship_kernel(row_cap, n_dev, chunks, slot_ref, x_ref, got_ref, next_ref, sbuf, vbuf, send_sems, recv_sems, own_sem, next_sems):
+    me = lax.axis_index("ep")
+    tok = x_ref.shape[0]
+    (start, size), (start1, size1) = chunks
+
+    def pack(dev, first, rows):
+        want = lax.broadcasted_iota(I32, (rows, tok), 0) + (dev * row_cap + first)
+        hit = (want == slot_ref[0:1, :]) | (want == slot_ref[1:2, :])
+        pick = jnp.where(hit, 1.0, 0.0).astype(BF16)
+        return _dot(pick, x_ref[...]).astype(BF16)
+
+    def send(k):
+        return pltpu.make_async_remote_copy(
+            src_ref=sbuf.at[k],
+            dst_ref=got_ref.at[me],
+            send_sem=send_sems.at[k],
+            recv_sem=recv_sems.at[k],
+            device_id=(partner(me, k),),
+            device_id_type=MESH,
+        )
+
+    def keep(d):
+        return pltpu.make_async_copy(vbuf.at[d], next_ref.at[d], next_sems.at[d])
+
+    def pack_first(k0, k1):
+        @pl.loop(0, 2)
+        def _(r):
+            k = k0 + r * (k1 - k0)
+            sbuf[k] = pack(partner(me, k), start, size)
+
+    barrier = pltpu.get_barrier_semaphore()
+    for k in range(1, n_dev):
+        pl.semaphore_signal(barrier, inc=1, device_id=(partner(me, k),), device_id_type=MESH)
+    pack_first(14, 15)
+    pl.semaphore_wait(barrier, n_dev - 1)
+    send(14).start()
+    send(15).start()
+    pack_first(6, 8)
+    pack_first(0, 1)
+
+    @pl.loop(1, 7)
+    def _(p):
+        k0, k1 = pair_of(p)
+
+        @pl.when(p <= 2)
+        def _():
+            send(13 + p).wait_send()
+
+        @pl.when(p >= 3)
+        def _():
+            for k in pair_of(p - 2):
+                send(k).wait_send()
+
+        send(k0).start()
+        send(k1).start()
+
+        @pl.when(p < 6)
+        def _():
+            pack_first(*pair_of(p + 1))
+
+        @pl.loop((n_dev * (p - 1)) // 6, (n_dev * p) // 6)
+        def _(d):
+            vbuf[d] = pack(d, start1, size1)
+
+            @pl.when(d > 0)
+            def _():
+                keep(d - 1).start()
+
+    keep(n_dev - 1).start()
+    send(1).start()
+    own = pltpu.make_async_copy(sbuf.at[0], got_ref.at[me], own_sem)
+    own.start()
+    for p in (5, 6):
+        for k in pair_of(p):
+            send(k).wait_send()
+    send(1).wait_send()
+    own.wait()
+
+    @pl.loop(0, n_dev)
+    def _(d):
+        keep(d).wait()
+
+    @pl.loop(1, n_dev)
+    def _(k):
+        send(k).wait_recv()
 
 
 def ffn_kernel(start, size, n_src, bound_ref, x_hbm, w1_hbm, w3_hbm, w2_hbm, out_ref, x_ref, w1, w3, w2, xbuf, hbuf, list_ref, low_ref, high_ref, used_ref, sems, x_sems):
@@ -299,29 +379,40 @@
             compiler_params=_params(),
             name="route",
         )(x, w_router.T, ids.T)
-        per_exp = lax.all_to_all(counts[:, 0].reshape(n, local), "ep", 0, 0, tiled=True)
+        every = lax.all_gather(counts[:, :1].reshape(n, local), "ep", axis=0)
+        per_exp = lax.dynamic_index_in_dim(every, lax.axis_index("ep"), axis=1, keepdims=False)
         ends = jnp.cumsum(per_exp, axis=1).T
         bounds = jnp.concatenate([jnp.zeros((1, n), I32), ends], axis=0)
         dev_counts = jnp.sum(counts[:, 0].reshape(n, local), axis=1)
         smem = pl.BlockSpec(memory_space=pltpu.SMEM)
         vmem = pl.BlockSpec(memory_space=pltpu.VMEM)
         hbm = pl.BlockSpec(memory_space=pl.ANY)
-        sends = []
-        for part in (CHUNKS[:1], CHUNKS[1:]):
-            total = sum(size for _, size in part)
-            pack = pl.pallas_call(
-                functools.partial(pack_kernel, cap, part),
-                in_specs=[smem, vmem, vmem],
-                out_specs=[vmem] * len(part),
-                out_shape=[jax.ShapeDtypeStruct((n * size, dim), BF16) for _, size in part],
-                scratch_shapes=[pltpu.SMEM((cap * n // SLOT_TILE,), I32)],
-                compiler_params=_params(),
-                cost_estimate=pl.CostEstimate(flops=2 * n * total * tok * dim, bytes_accessed=1, transcendentals=0),
-            )
-            sends += pack(dev_counts, slots, x)
+        ship = pl.pallas_call(
+            functools.partial(ship_kernel, cap, n, CHUNKS),
+            in_specs=[vmem, vmem],
+            out_specs=[hbm, hbm],
+            out_shape=[jax.ShapeDtypeStruct((n, size, dim), BF16) for _, size in CHUNKS],
+            scratch_shapes=[
+                pltpu.VMEM((n, CHUNKS[0][1], dim), BF16),
+                pltpu.VMEM((n, CHUNKS[1][1], dim), BF16),
+                pltpu.SemaphoreType.DMA((n,)),
+                pltpu.SemaphoreType.DMA((n,)),
+                pltpu.SemaphoreType.DMA,
+                pltpu.SemaphoreType.DMA((n,)),
+            ],
+            compiler_params=pltpu.CompilerParams(
+                vmem_limit_bytes=VMEM_BYTES, collective_id=0, has_side_effects=True
+            ),
+            cost_estimate=pl.CostEstimate(flops=10**11, bytes_accessed=1, transcendentals=0),
+            name="ship",
+        )
+        first_rows, second_rows = ship(slots, x)
         acc = None
         for index, (start, size) in enumerate(CHUNKS):
-            got = lax.all_to_all(sends[index].reshape(n, size, dim), "ep", 0, 0, tiled=True)
+            if index == 0:
+                got = first_rows
+            else:
+                got = lax.all_to_all(second_rows, "ep", 0, 0, tiled=True)
             rows = n * size
             made = pl.pallas_call(
                 functools.partial(ffn_kernel, start, size, n),

time: 379 us -> 442 us (1.17)
  blocking collectives: 0 us -> 81.5 us
  waiting for transfers between devices: 107 us -> 39.9 us
  Pallas kernels: 248 us -> 304 us
  starting transfers between devices: 19.4 us -> 12.8 us
    all_gather x0 -> x1, blocking collectives: none -> 81.5 us  [body(): every = lax.all_gather(counts[:, :1].reshape(n, local), 'ep', axis=0)]
    all_to_all x3 -> x1, waiting for transfers between devices: 65.9 us -> 0.01 us  [body(): got = lax.all_to_all(second_rows, 'ep', 0, 0, tiled=True)]
    pallas_call x2 -> x1, Pallas kernels: 32.1 us -> 87.9 us  [body(): first_rows, second_rows = ship(slots, x)]
    all_to_all x3 -> x1, starting transfers between devices: 12.5 us -> 3.26 us  [body(): got = lax.all_to_all(second_rows, 'ep', 0, 0, tiled=True)]
  transfers between devices with their start and end apart: 5 -> 3, of which waited for: 2 -> 1; matrix products, arithmetic and copies ran while one was open for 0% -> 0% of each run, Pallas kernels for 61% -> 45%
where the time goes in v5:
time: 442 us; the launch traced here: 440 us
  Pallas kernels  304 us (69%)
  blocking collectives  81.5 us (18%)
  waiting for transfers between devices  39.9 us (9%)
  starting transfers between devices  12.8 us (3%)
    pallas_call x2, Pallas kernels, body(): made = made(bounds, got.reshape(rows, dim), w1, w3, w2)  160 us
    pallas_call x1, Pallas kernels, body(): first_rows, second_rows = ship(slots, x)  87.9 us
    all_gather x1, blocking collectives, body(): every = lax.all_gather(counts[:, :1].reshape(n, local), 'ep', axis=0)  81.5 us
    pallas_call x2, Pallas kernels, body(): acc = combine(dev_counts, *ins)  51.1 us
    all_to_all x2, waiting for transfers between devices, body(): lax.all_to_all(made.reshape(n, size, dim), 'ep', 0, 0, tiled=True)  39.9 us
    all_to_all x2, starting transfers between devices, body(): lax.all_to_all(made.reshape(n, size, dim), 'ep', 0, 0, tiled=True)  9.53 us
  transfers between devices with their start and end apart: 3, of which 1 were waited for; matrix products, arithmetic and copies ran while one was open for 0% of the time, Pallas kernels for 45%

profile of v5, /device:TPU:11, one launch (start us, length us, event | category | flops | bytes accessed | tf_op | source)
XLA Modules:
  0.0 440.1 jit_solution(9751397016580200647)
XLA Ops:
  0.0 4.6 %route.1 = (s32[8,2048]{1,0:T(8,128)}, f32[2048,8]{1,0:T(8,128)}, s32[32,128]{1,0:T(8,128)}) custom-call(bf16[2048,768]{1,0:T(8,128)(2,1)} %x_ref.3, f32[32,768]{1,0:T(8,128)} %bitcast.12, s32[2,2048]{1,0:T(2,128)} %bitcast.13), custom_call_target="tpu_custom_call" | custom-call | tf_op jit(solution)/shard_map/route/pallas_call | solution.py:372
  4.6 87.9 %ship.1 = (bf16[16,256,768]{2,1,0:T(8,128)(2,1)}, bf16[16,256,768]{2,1,0:T(8,128)(2,1)}) custom-call(s32[8,2048]{1,0:T(8,128)} %get-tuple-element.12.slot_ref, bf16[2048,768]{1,0:T(8,128)(2,1)} %x_ref.3), custom_call_target="tpu_custom_call" | custom-call | flops 99999997952 | bytes 1 | tf_op jit(solution)/shard_map/ship/pallas_call | solution.py:409
  92.6 0.0 copy-start
  92.6 3.3 all-to-all-start
  95.9 0.0 copy-done
  95.9 0.1 slice_reduce_fusion
  96.0 0.1 all_gather_reshape.3
  96.1 0.1 copy.9
  96.2 81.5 %all_gather.3 = s32[16,16,2]{1,2,0:T(2,128)S(1)} all-gather(s32[1,16,2]{1,2,0:T(2,128)S(1)} %copy.9), channel_id=1, replica_groups=mesh['ep'=16] {'ep'}, dimensions={0}, use_global_device_ids=true | all-gather | bytes 2176 | tf_op jit(solution)/shard_map/all_gather | solution.py:382
  177.6 0.1 constant_dynamic-slice_fusion
  177.7 0.1 copy.10
  177.9 0.6 concatenate.3.bound_ref
  178.5 79.3 %shard_map.65 = bf16[4096,768]{1,0:T(8,128)(2,1)} custom-call(s32[3,16]{1,0:T(4,128)} %concatenate.3.bound_ref, bf16[4096,768]{1,0:T(8,128)(2,1)} %bitcast.16, bf16[2,768,3072]{2,1,0:T(8,128)(2,1)} %w1_hbm.3, bf16[2,768,3072]{2,1,0:T(8,128)(2,1)} %w3_hbm.3, bf16[2,3072,768]{2,1,0:T(8,128)(2,1)} %w2_hbm.3), custom_call_target="tpu_custom_call" | custom-call | flops 57982058496 | bytes 1 | tf_op jit(solution)/shard_map/pallas_call | solution.py:439
  257.7 0.0 all-to-all-done
  257.8 6.0 %all-to-all-start.2 = ((bf16[16,256,768]{2,1,0:T(8,128)(2,1)}), bf16[16,256,768]{2,1,0:T(8,128)(2,1)}, u32[]{:S(2)}, u32[]{:S(2)}) async-start(bf16[16,256,768]{2,1,0:T(8,128)(2,1)} %bitcast.11), calls=%async_computation.2 | async-start | bytes 12582912 | tf_op jit(solution)/shard_map/all_to_all | solution.py:440
  263.7 81.1 %shard_map.64 = bf16[4096,768]{1,0:T(8,128)(2,1)} custom-call(s32[3,16]{1,0:T(4,128)} %concatenate.3.bound_ref, bf16[4096,768]{1,0:T(8,128)(2,1)} %bitcast.4.x_hbm, bf16[2,768,3072]{2,1,0:T(8,128)(2,1)} %w1_hbm.3, bf16[2,768,3072]{2,1,0:T(8,128)(2,1)} %w3_hbm.3, bf16[2,3072,768]{2,1,0:T(8,128)(2,1)} %w2_hbm.3), custom_call_target="tpu_custom_call" | custom-call | flops 57982058496 | bytes 1 | tf_op jit(solution)/shard_map/pallas_call | solution.py:439
  344.8 0.0 all-to-all-done.2
  344.8 3.6 all-to-all-start.1
  348.4 0.1 reshape_squeeze.3
  348.4 0.7 reduce_sum.9.counts_ref
  349.1 36.4 %shard_map.66.refs_0_ = f32[2048,768]{1,0:T(8,128)} custom-call(s32[16]{0:T(128)} %reduce_sum.9.counts_ref, f32[2048,8]{1,0:T(8,128)} %get-tuple-element.11.cols_ref, bf16[4096,768]{1,0:T(8,128)(2,1)} %bitcast.9.back_ref), custom_call_target="tpu_custom_call" | custom-call | flops 25769803776 | bytes 1 | tf_op jit(solution)/shard_map/pallas_call | solution.py:464
  385.5 39.9 %all-to-all-done.1 = bf16[16,256,768]{2,1,0:T(8,128)(2,1)} async-done(((bf16[16,256,768]{2,1,0:T(8,128)(2,1)}), bf16[16,256,768]{2,1,0:T(8,128)(2,1)}, u32[]{:S(2)}, u32[]{:S(2)}) %all-to-all-start.1) | async-done | bytes 6291488 | tf_op jit(solution)/shard_map/all_to_all | solution.py:440
  425.4 14.7 %shard_map.67 = bf16[2048,768]{1,0:T(8,128)(2,1)} custom-call(s32[16]{0:T(128)} %reduce_sum.9.counts_ref, f32[2048,8]{1,0:T(8,128)} %get-tuple-element.11.cols_ref, bf16[4096,768]{1,0:T(8,128)(2,1)} %bitcast.6.back_ref, f32[2048,768]{1,0:T(8,128)} %shard_map.66.refs_0_), custom_call_target="tpu_custom_call" | custom-call | flops 25769803776 | bytes 1 | tf_op jit(solution)/shard_map/pallas_call | solution.py:464
  (1 shorter events, 0.0 us)
Async XLA Ops:
  92.6 3.3 copy-start
  92.6 165.2 %all-to-all-start = ((bf16[16,256,768]{2,1,0:T(8,128)(2,1)}), bf16[16,256,768]{2,1,0:T(8,128)(2,1)}, u32[]{:S(2)}, u32[]{:S(2)}) async-start(bf16[16,256,768]{2,1,0:T(8,128)(2,1)} %get-tuple-element.13), calls=%async_computation | async-start | bytes 12582912 | tf_op jit(solution)/shard_map/all_to_all | solution.py:415
  257.8 87.0 %all-to-all-start.2 = ((bf16[16,256,768]{2,1,0:T(8,128)(2,1)}), bf16[16,256,768]{2,1,0:T(8,128)(2,1)}, u32[]{:S(2)}, u32[]{:S(2)}) async-start(bf16[16,256,768]{2,1,0:T(8,128)(2,1)} %bitcast.11), calls=%async_computation.2 | async-start | bytes 12582912 | tf_op jit(solution)/shard_map/all_to_all | solution.py:440
  344.8 80.6 %all-to-all-start.1 = ((bf16[16,256,768]{2,1,0:T(8,128)(2,1)}), bf16[16,256,768]{2,1,0:T(8,128)(2,1)}, u32[]{:S(2)}, u32[]{:S(2)}) async-start(bf16[16,256,768]{2,1,0:T(8,128)(2,1)} %bitcast.10), calls=%async_computation.1 | async-start | bytes 12582912 | tf_op jit(solution)/shard_map/all_to_all | solution.py:440

commit v6 on v5

--- a/solution.py
+++ b/solution.py
@@ -116,7 +116,7 @@
     return 14 - near + r, near + r
 
 
-def ship_kernel(row_cap, n_dev, chunks, slot_ref, x_ref, got_ref, next_ref, sbuf, vbuf, send_sems, recv_sems, own_sem, next_sems):
+def ship_kernel(row_cap, n_dev, chunks, slot_ref, cnt_ref, x_ref, got_ref, next_ref, all_ref, sbuf, vbuf, send_sems, recv_sems, own_sem, next_sems, cs_sems, cr_sems, co_sem):
     me = lax.axis_index("ep")
     tok = x_ref.shape[0]
     (start, size), (start1, size1) = chunks
@@ -137,6 +137,18 @@
             device_id_type=MESH,
         )
 
+    def tell(k):
+        return pltpu.make_async_remote_copy(
+            src_ref=cnt_ref,
+            dst_ref=all_ref.at[me],
+            send_sem=cs_sems.at[k],
+            recv_sem=cr_sems.at[k],
+            device_id=(partner(me, k),),
+            device_id_type=MESH,
+        )
+
+    own_counts = pltpu.make_async_copy(cnt_ref, all_ref.at[me], co_sem)
+
     def keep(d):
         return pltpu.make_async_copy(vbuf.at[d], next_ref.at[d], next_sems.at[d])
 
@@ -153,6 +165,12 @@
     pl.semaphore_wait(barrier, n_dev - 1)
     send(14).start()
     send(15).start()
+    own_counts.start()
+
+    @pl.loop(1, n_dev)
+    def _(k):
+        tell(k).start()
+
     pack_first(6, 8)
     pack_first(0, 1)
 
@@ -193,6 +211,7 @@
             send(k).wait_send()
     send(1).wait_send()
     own.wait()
+    own_counts.wait()
 
     @pl.loop(0, n_dev)
     def _(d):
@@ -200,6 +219,8 @@
 
     @pl.loop(1, n_dev)
     def _(k):
+        tell(k).wait_send()
+        tell(k).wait_recv()
         send(k).wait_recv()
 
 
@@ -379,19 +400,16 @@
             compiler_params=_params(),
             name="route",
         )(x, w_router.T, ids.T)
-        every = lax.all_gather(counts[:, :1].reshape(n, local), "ep", axis=0)
-        per_exp = lax.dynamic_index_in_dim(every, lax.axis_index("ep"), axis=1, keepdims=False)
-        ends = jnp.cumsum(per_exp, axis=1).T
-        bounds = jnp.concatenate([jnp.zeros((1, n), I32), ends], axis=0)
         dev_counts = jnp.sum(counts[:, 0].reshape(n, local), axis=1)
         smem = pl.BlockSpec(memory_space=pltpu.SMEM)
         vmem = pl.BlockSpec(memory_space=pltpu.VMEM)
         hbm = pl.BlockSpec(memory_space=pl.ANY)
         ship = pl.pallas_call(
             functools.partial(ship_kernel, cap, n, CHUNKS),
-            in_specs=[vmem, vmem],
-            out_specs=[hbm, hbm],
-            out_shape=[jax.ShapeDtypeStruct((n, size, dim), BF16) for _, size in CHUNKS],
+            in_specs=[vmem, vmem, vmem],
+            out_specs=[hbm, hbm, hbm],
+            out_shape=[jax.ShapeDtypeStruct((n, size, dim), BF16) for _, size in CHUNKS]
+            + [jax.ShapeDtypeStruct((n,) + counts.shape, I32)],
             scratch_shapes=[
                 pltpu.VMEM((n, CHUNKS[0][1], dim), BF16),
                 pltpu.VMEM((n, CHUNKS[1][1], dim), BF16),
@@ -399,6 +417,9 @@
                 pltpu.SemaphoreType.DMA((n,)),
                 pltpu.SemaphoreType.DMA,
                 pltpu.SemaphoreType.DMA((n,)),
+                pltpu.SemaphoreType.DMA((n,)),
+                pltpu.SemaphoreType.DMA((n,)),
+                pltpu.SemaphoreType.DMA,
             ],
             compiler_params=pltpu.CompilerParams(
                 vmem_limit_bytes=VMEM_BYTES, collective_id=0, has_side_effects=True
@@ -406,7 +427,11 @@
             cost_estimate=pl.CostEstimate(flops=10**11, bytes_accessed=1, transcendentals=0),
             name="ship",
         )
-        first_rows, second_rows = ship(slots, x)
+        first_rows, second_rows, every = ship(slots, counts, x)
+        at = lax.axis_index("ep") * local
+        per_exp = lax.dynamic_slice(every, (0, at, 0), (n, local, 1))[:, :, 0]
+        ends = jnp.cumsum(per_exp, axis=1).T
+        bounds = jnp.concatenate([jnp.zeros((1, n), I32), ends], axis=0)
         acc = None
         for index, (start, size) in enumerate(CHUNKS):
             if index == 0:

time: 442 us -> 350 us (0.79)
  blocking collectives: 81.5 us -> 0 us
  Pallas kernels: 304 us -> 294 us
    all_gather x1 -> x0, blocking collectives: 81.5 us -> none  [body(): every = lax.all_gather(counts[:, :1].reshape(n, local), 'ep', axis=0)]
    pallas_call x1, Pallas kernels: 87.9 us -> 78.3 us  [body(): first_rows, second_rows, every = ship(slots, counts, x)]
  transfers between devices with their start and end apart: 3 -> 3, of which waited for: 1 -> 1; matrix products, arithmetic and copies ran while one was open for 0% -> 1% of each run, Pallas kernels for 45% -> 56%
where the time goes in v6:
time: 350 us; the launch traced here: 349 us
  Pallas kernels  294 us (84%)
  waiting for transfers between devices  39.7 us (11%)
  starting transfers between devices  12 us (3%)
    pallas_call x2, Pallas kernels, body(): made = made(bounds, got.reshape(rows, dim), w1, w3, w2)  160 us
    pallas_call x1, Pallas kernels, body(): first_rows, second_rows, every = ship(slots, counts, x)  78.3 us
    pallas_call x2, Pallas kernels, body(): acc = combine(dev_counts, *ins)  51.1 us
    all_to_all x2, waiting for transfers between devices, body(): lax.all_to_all(made.reshape(n, size, dim), 'ep', 0, 0, tiled=True)  39.7 us
  transfers between devices with their start and end apart: 3, of which 1 were waited for; matrix products, arithmetic and copies ran while one was open for 1% of the time, Pallas kernels for 56%

profile of v6, /device:TPU:11, one launch (start us, length us, event | category | flops | bytes accessed | tf_op | source)
XLA Modules:
  0.0 348.7 jit_solution(12533484863827232593)
XLA Ops:
  0.0 4.6 %route.1 = (s32[8,2048]{1,0:T(8,128)}, f32[2048,8]{1,0:T(8,128)}, s32[32,128]{1,0:T(8,128)}) custom-call(bf16[2048,768]{1,0:T(8,128)(2,1)} %x_ref.3, f32[32,768]{1,0:T(8,128)} %bitcast.12, s32[2,2048]{1,0:T(2,128)} %bitcast.13), custom_call_target="tpu_custom_call" | custom-call | tf_op jit(solution)/shard_map/route/pallas_call | solution.py:393
  4.6 78.3 %ship.1 = (bf16[16,256,768]{2,1,0:T(8,128)(2,1)}, bf16[16,256,768]{2,1,0:T(8,128)(2,1)}, s32[16,32,128]{2,1,0:T(8,128)}) custom-call(s32[8,2048]{1,0:T(8,128)} %get-tuple-element.13.slot_ref, s32[32,128]{1,0:T(8,128)} %get-tuple-element.11.cnt_ref, bf16[2048,768]{1,0:T(8,128)(2,1)} %x_ref.3), custom_call_target="tpu_custom_call" | custom-call | flops 99999997952 | bytes 1 | tf_op jit(solution)/shard_map/ship/pallas_call | solution.py:430
  82.9 5.0 %all-to-all-start = ((bf16[16,256,768]{2,1,0:T(8,128)(2,1)}), bf16[16,256,768]{2,1,0:T(8,128)(2,1)}, u32[]{:S(2)}, u32[]{:S(2)}) async-start(bf16[16,256,768]{2,1,0:T(8,128)(2,1)} %get-tuple-element.15), calls=%async_computation | async-start | bytes 12582912 | tf_op jit(solution)/shard_map/all_to_all | solution.py:440
  88.0 0.8 constant_dynamic-slice_fusion
  88.8 0.1 copy.8
  89.0 0.6 concatenate.3.bound_ref
  89.5 79.3 %shard_map.65 = bf16[4096,768]{1,0:T(8,128)(2,1)} custom-call(s32[3,16]{1,0:T(4,128)} %concatenate.3.bound_ref, bf16[4096,768]{1,0:T(8,128)(2,1)} %bitcast.16, bf16[2,768,3072]{2,1,0:T(8,128)(2,1)} %w1_hbm.3, bf16[2,768,3072]{2,1,0:T(8,128)(2,1)} %w3_hbm.3, bf16[2,3072,768]{2,1,0:T(8,128)(2,1)} %w2_hbm.3), custom_call_target="tpu_custom_call" | custom-call | flops 57982058496 | bytes 1 | tf_op jit(solution)/shard_map/pallas_call | solution.py:464
  168.8 0.0 all-to-all-done
  168.8 3.4 all-to-all-start.2
  172.3 81.1 %shard_map.64 = bf16[4096,768]{1,0:T(8,128)(2,1)} custom-call(s32[3,16]{1,0:T(4,128)} %concatenate.3.bound_ref, bf16[4096,768]{1,0:T(8,128)(2,1)} %bitcast.4.x_hbm, bf16[2,768,3072]{2,1,0:T(8,128)(2,1)} %w1_hbm.3, bf16[2,768,3072]{2,1,0:T(8,128)(2,1)} %w3_hbm.3, bf16[2,3072,768]{2,1,0:T(8,128)(2,1)} %w2_hbm.3), custom_call_target="tpu_custom_call" | custom-call | flops 57982058496 | bytes 1 | tf_op jit(solution)/shard_map/pallas_call | solution.py:464
  253.4 0.0 all-to-all-done.2
  253.4 0.0 copy-start
  253.4 3.5 %all-to-all-start.1 = ((bf16[16,256,768]{2,1,0:T(8,128)(2,1)}), bf16[16,256,768]{2,1,0:T(8,128)(2,1)}, u32[]{:S(2)}, u32[]{:S(2)}) async-start(bf16[16,256,768]{2,1,0:T(8,128)(2,1)} %bitcast.10), calls=%async_computation.1 | async-start | bytes 12582912 | tf_op jit(solution)/shard_map/all_to_all | solution.py:465
  257.0 0.0 copy-done
  257.0 0.1 slice_reduce_fusion
  257.1 0.1 reshape_squeeze.3
  257.2 0.7 reduce_sum.9.counts_ref
  257.9 36.4 %shard_map.66.refs_0_ = f32[2048,768]{1,0:T(8,128)} custom-call(s32[16]{0:T(128)} %reduce_sum.9.counts_ref, f32[2048,8]{1,0:T(8,128)} %get-tuple-element.12.cols_ref, bf16[4096,768]{1,0:T(8,128)(2,1)} %bitcast.9.back_ref), custom_call_target="tpu_custom_call" | custom-call | flops 25769803776 | bytes 1 | tf_op jit(solution)/shard_map/pallas_call | solution.py:489
  294.3 39.7 %all-to-all-done.1 = bf16[16,256,768]{2,1,0:T(8,128)(2,1)} async-done(((bf16[16,256,768]{2,1,0:T(8,128)(2,1)}), bf16[16,256,768]{2,1,0:T(8,128)(2,1)}, u32[]{:S(2)}, u32[]{:S(2)}) %all-to-all-start.1) | async-done | bytes 6291488 | tf_op jit(solution)/shard_map/all_to_all | solution.py:465
  334.0 14.7 %shard_map.67 = bf16[2048,768]{1,0:T(8,128)(2,1)} custom-call(s32[16]{0:T(128)} %reduce_sum.9.counts_ref, f32[2048,8]{1,0:T(8,128)} %get-tuple-element.12.cols_ref, bf16[4096,768]{1,0:T(8,128)(2,1)} %bitcast.6.back_ref, f32[2048,768]{1,0:T(8,128)} %shard_map.66.refs_0_), custom_call_target="tpu_custom_call" | custom-call | flops 25769803776 | bytes 1 | tf_op jit(solution)/shard_map/pallas_call | solution.py:489
  (1 shorter events, 0.0 us)
Async XLA Ops:
  82.9 85.9 %all-to-all-start = ((bf16[16,256,768]{2,1,0:T(8,128)(2,1)}), bf16[16,256,768]{2,1,0:T(8,128)(2,1)}, u32[]{:S(2)}, u32[]{:S(2)}) async-start(bf16[16,256,768]{2,1,0:T(8,128)(2,1)} %get-tuple-element.15), calls=%async_computation | async-start | bytes 12582912 | tf_op jit(solution)/shard_map/all_to_all | solution.py:440
  168.8 84.6 %all-to-all-start.2 = ((bf16[16,256,768]{2,1,0:T(8,128)(2,1)}), bf16[16,256,768]{2,1,0:T(8,128)(2,1)}, u32[]{:S(2)}, u32[]{:S(2)}) async-start(bf16[16,256,768]{2,1,0:T(8,128)(2,1)} %bitcast.11), calls=%async_computation.2 | async-start | bytes 12582912 | tf_op jit(solution)/shard_map/all_to_all | solution.py:465
  253.4 3.5 %copy-start = (s32[32,128]{1,0:T(8,128)S(1)}, s32[32,128]{1,0:T(8,128)}, u32[]{:S(2)}) copy-start(s32[32,128]{1,0:T(8,128)} %get-tuple-element.11.cnt_ref) | copy-start | bytes 49156
  253.4 80.6 %all-to-all-start.1 = ((bf16[16,256,768]{2,1,0:T(8,128)(2,1)}), bf16[16,256,768]{2,1,0:T(8,128)(2,1)}, u32[]{:S(2)}, u32[]{:S(2)}) async-start(bf16[16,256,768]{2,1,0:T(8,128)(2,1)} %bitcast.10), calls=%async_computation.1 | async-start | bytes 12582912 | tf_op jit(solution)/shard_map/all_to_all | solution.py:465

commit v7 on v6

--- a/solution.py
+++ b/solution.py
@@ -335,44 +335,132 @@
                     out_ref[at, :] = jnp.where(own, y[j * TILE : (j + 1) * TILE], out_ref[at, :])
 
 
-def combine_kernel(row_cap, start, size, n_dev, has_acc, counts_ref, cols_ref, back_ref, *refs):
-    if has_acc:
-        acc_ref, out_ref, rows_ref, sum_ref, list_ref, cnt_ref = refs
-    else:
-        out_ref, rows_ref, sum_ref, list_ref, cnt_ref = refs
+def gated(cols, ids, rows):
+    add = 0.0
+    for k in range(2):
+        pick = jnp.where(ids == cols[:, k : k + 1], 1.0, 0.0).astype(BF16)
+        add = add + cols[:, 2 + k : 3 + k] * _dot(pick, rows)
+    return add
+
+
+def bring_kernel(row_cap, n_dev, chunk, made_ref, back_hbm, cols_ref, got_ref, acc_ref, back, acc, send_sems, recv_sems, own_sem, back_sems, acc_sem):
+    me = lax.axis_index("ep")
+    start, size = chunk
+    tok = cols_ref.shape[0]
+    block = 512
+
+    def send(k):
+        return pltpu.make_async_remote_copy(
+            src_ref=made_ref.at[partner(me, k)],
+            dst_ref=got_ref.at[me],
+            send_sem=send_sems.at[k],
+            recv_sem=recv_sems.at[k],
+            device_id=(partner(me, k),),
+            device_id_type=MESH,
+        )
+
+    def fetch(g):
+        at = pl.ds(pl.multiple_of(g * 2 * size, 2 * size), 2 * size)
+        return pltpu.make_async_copy(back_hbm.at[at], back.at[at], back_sems.at[g])
+
+    barrier = pltpu.get_barrier_semaphore()
+    for k in range(1, n_dev):
+        pl.semaphore_signal(barrier, inc=1, device_id=(partner(me, k),), device_id_type=MESH)
+    acc[...] = jnp.zeros_like(acc)
+    pl.semaphore_wait(barrier, n_dev - 1)
+    send(14).start()
+    send(15).start()
+    send(1).start()
+    own = pltpu.make_async_copy(made_ref.at[me], got_ref.at[me], own_sem)
+    own.start()
+    groups = n_dev // 2
+
+    @pl.loop(0, groups)
+    def _(g):
+        fetch(g).start()
+
+    @pl.loop(1, 7)
+    def _(p):
+        k0, k1 = pair_of(p)
+
+        @pl.when(p <= 2)
+        def _():
+            send(13 + p).wait_send()
+
+        @pl.when(p >= 3)
+        def _():
+            for k in pair_of(p - 2):
+                send(k).wait_send()
+
+        send(k0).start()
+        send(k1).start()
+
+        @pl.loop((groups * (p - 1)) // 6, (groups * p) // 6)
+        def _(g):
+            fetch(g).wait()
+            rows = back[pl.ds(pl.multiple_of(g * 2 * size, 2 * size), 2 * size), :]
+            lane = lax.broadcasted_iota(I32, (1, 2 * size), 1)
+            ids = ((2 * g + lane // size) * row_cap + start + lane % size).astype(F32)
+
+            @pl.loop(0, tok // block)
+            def _(t):
+                at = pl.ds(pl.multiple_of(t * block, block), block)
+                acc[at, :] += gated(cols_ref[at, :], ids, rows)
+
+    out = pltpu.make_async_copy(acc, acc_ref, acc_sem)
+    for p in (5, 6):
+        for k in pair_of(p):
+            send(k).wait_send()
+    out.start()
+    send(1).wait_send()
+    own.wait()
+
+    @pl.loop(1, n_dev)
+    def _(k):
+        send(k).wait_recv()
+
+    out.wait()
+
+
+def combine_kernel(row_cap, start, size, n_dev, counts_ref, cols_ref, back_hbm, acc_ref, out_ref, rows_ref, sum_ref, list_ref, cnt_ref, sems):
     group = SUM_GROUP * SLOT_TILE
-    toks, dim = out_ref.shape
+
+    def fetch(i, k):
+        src = pl.ds(pl.multiple_of(i * SLOT_TILE, SLOT_TILE), SLOT_TILE)
+        dst = pl.ds(pl.multiple_of(k * SLOT_TILE, SLOT_TILE), SLOT_TILE)
+        return pltpu.make_async_copy(back_hbm.at[src], rows_ref.at[dst], sems.at[k])
 
     @pl.when(pl.program_id(0) == 0)
     def _():
-        cnt = list_tiles(n_dev, size, start, counts_ref, list_ref)
+        cnt = list_tiles(n_dev, size, start, counts_ref, list_ref, lambda i, k: fetch(i, k).start())
         groups = (cnt + SUM_GROUP - 1) // SUM_GROUP
         cnt_ref[0] = groups
 
         @pl.loop(cnt, groups * SUM_GROUP)
         def _(k):
             list_ref[k] = -1
-
-    c = cols_ref[...]
-    sum_ref[...] = acc_ref[...] if has_acc else jnp.zeros((toks, dim), F32)
+            rows_ref[pl.ds(pl.multiple_of(k * SLOT_TILE, SLOT_TILE), SLOT_TILE), :] = jnp.zeros((SLOT_TILE, rows_ref.shape[1]), BF16)
+
+        @pl.loop(0, cnt)
+        def _(k):
+            fetch(list_ref[k], k).wait()
+
     lane = lax.broadcasted_iota(I32, (1, group), 1)
 
-    @pl.loop(0, cnt_ref[0])
-    def _(g):
+    def one(g, total):
         ids = jnp.full((1, group), -1, I32)
         for j in range(SUM_GROUP):
             i = list_ref[g * SUM_GROUP + j]
             base = jnp.where(i < 0, -1 - group, first_slot(i, size, start, row_cap))
             ids = jnp.where(lane // SLOT_TILE == j, base + lane % SLOT_TILE, ids)
-            src = pl.ds(pl.multiple_of(jnp.maximum(i, 0) * SLOT_TILE, SLOT_TILE), SLOT_TILE)
-            rows_ref[j * SLOT_TILE : (j + 1) * SLOT_TILE, :] = back_ref[src, :]
-        rows = rows_ref[...]
-        ids = ids.astype(F32)
-        add = 0.0
-        for k in range(2):
-            pick = jnp.where(ids == c[:, k : k + 1], 1.0, 0.0).astype(BF16)
-            add = add + c[:, 2 + k : 3 + k] * _dot(pick, rows)
-        sum_ref[...] += add
+        rows = rows_ref[pl.ds(pl.multiple_of(g * group, group), group), :]
+        return total + gated(cols_ref[...], ids.astype(F32), rows)
+
+    sum_ref[...] = acc_ref[...]
+
+    @pl.loop(0, cnt_ref[0])
+    def _(g):
+        sum_ref[...] = one(g, sum_ref[...])
 
     out_ref[...] = sum_ref[...].astype(out_ref.dtype)
 
@@ -432,7 +520,6 @@
         per_exp = lax.dynamic_slice(every, (0, at, 0), (n, local, 1))[:, :, 0]
         ends = jnp.cumsum(per_exp, axis=1).T
         bounds = jnp.concatenate([jnp.zeros((1, n), I32), ends], axis=0)
-        acc = None
         for index, (start, size) in enumerate(CHUNKS):
             if index == 0:
                 got = first_rows
@@ -462,32 +549,51 @@
                 cost_estimate=pl.CostEstimate(flops=6 * rows * dim * ff, bytes_accessed=1, transcendentals=0),
             )
             made = made(bounds, got.reshape(rows, dim), w1, w3, w2)
-            back = lax.all_to_all(made.reshape(n, size, dim), "ep", 0, 0, tiled=True).reshape(rows, dim)
-            last = index == len(CHUNKS) - 1
-            tb = 512
-            tile_spec = pl.BlockSpec((tb, dim), lambda i, c: (i, 0))
-            ins = [cols, back] + ([] if acc is None else [acc])
-            specs = [pl.BlockSpec((tb, 8), lambda i, c: (i, 0)), pl.BlockSpec((rows, dim), lambda i, c: (0, 0))]
-            combine = pl.pallas_call(
-                functools.partial(combine_kernel, cap, start, size, n, acc is not None),
-                grid_spec=pltpu.PrefetchScalarGridSpec(
-                    num_scalar_prefetch=1,
-                    grid=(tok // tb,),
-                    in_specs=specs + ([] if acc is None else [tile_spec]),
-                    out_specs=tile_spec,
-                    scratch_shapes=[
-                        pltpu.VMEM((SUM_GROUP * SLOT_TILE, dim), BF16),
-                        pltpu.VMEM((tb, dim), F32),
-                        pltpu.SMEM((rows // SLOT_TILE,), I32),
-                        pltpu.SMEM((1,), I32),
-                    ],
-                ),
-                out_shape=jax.ShapeDtypeStruct((tok, dim), BF16 if last else F32),
-                compiler_params=_params(),
-                cost_estimate=pl.CostEstimate(flops=4 * rows * tok * dim, bytes_accessed=1, transcendentals=0),
-            )
-            acc = combine(dev_counts, *ins)
-        return acc
+            if index == 0:
+                back = lax.all_to_all(made.reshape(n, size, dim), "ep", 0, 0, tiled=True)
+        start, size = CHUNKS[1]
+        rows = n * size
+        got, acc = pl.pallas_call(
+            functools.partial(bring_kernel, cap, n, CHUNKS[0]),
+            in_specs=[hbm, hbm, vmem],
+            out_specs=[hbm, hbm],
+            out_shape=[jax.ShapeDtypeStruct((n, size, dim), BF16), jax.ShapeDtypeStruct((tok, dim), F32)],
+            scratch_shapes=[
+                pltpu.VMEM((n * CHUNKS[0][1], dim), BF16),
+                pltpu.VMEM((tok, dim), F32),
+                pltpu.SemaphoreType.DMA((n,)),
+                pltpu.SemaphoreType.DMA((n,)),
+                pltpu.SemaphoreType.DMA,
+                pltpu.SemaphoreType.DMA((n // 2,)),
+                pltpu.SemaphoreType.DMA,
+            ],
+            compiler_params=pltpu.CompilerParams(
+                vmem_limit_bytes=VMEM_BYTES, collective_id=1, has_side_effects=True
+            ),
+            cost_estimate=pl.CostEstimate(flops=10**11, bytes_accessed=1, transcendentals=0),
+            name="bring",
+        )(made.reshape(n, size, dim), back.reshape(n * CHUNKS[0][1], dim), cols)
+        tb = 512
+        tile_spec = pl.BlockSpec((tb, dim), lambda i, c: (i, 0))
+        return pl.pallas_call(
+            functools.partial(combine_kernel, cap, start, size, n),
+            grid_spec=pltpu.PrefetchScalarGridSpec(
+                num_scalar_prefetch=1,
+                grid=(tok // tb,),
+                in_specs=[pl.BlockSpec((tb, 8), lambda i, c: (i, 0)), hbm, tile_spec],
+                out_specs=tile_spec,
+                scratch_shapes=[
+                    pltpu.VMEM((rows, dim), BF16),
+                    pltpu.VMEM((tb, dim), F32),
+                    pltpu.SMEM((rows // SLOT_TILE,), I32),
+                    pltpu.SMEM((1,), I32),
+                    pltpu.SemaphoreType.DMA((rows // SLOT_TILE,)),
+                ],
+            ),
+            out_shape=jax.ShapeDtypeStruct((tok, dim), BF16),
+            compiler_params=_params(),
+            name="combine",
+        )(dev_counts, cols, got.reshape(rows, dim), acc)
 
     return jax.shard_map(
         body,

time: 350 us -> 348 us (level)
  waiting for transfers between devices: 39.7 us -> 0.01 us
  Pallas kernels: 294 us -> 333 us
  starting transfers between devices: 12 us -> 8.47 us
    all_to_all x2 -> x1, waiting for transfers between devices: 39.7 us -> 0.01 us  [body(): back = lax.all_to_all(made.reshape(n, size, dim), 'ep', 0, 0, tiled=True)]
    pallas_call x2, Pallas kernels: 51.1 us -> 89.7 us  [the longest x1 74.5 us: body(): pl.pallas_call(functools.partial(bring_kernel, cap, n, CHUNKS[0]), in_spe...]
  transfers between devices with their start and end apart: 3 -> 2, of which waited for: 1 -> 0; matrix products, arithmetic and copies ran while one was open for 1% -> 1% of each run, Pallas kernels for 56% -> 47%
where the time goes in v7:
time: 348 us; the launch traced here: 344 us
  Pallas kernels  333 us (96%)
  starting transfers between devices  8.47 us (2%)
    pallas_call x2, Pallas kernels, body(): made = made(bounds, got.reshape(rows, dim), w1, w3, w2)  160 us
    pallas_call x1, Pallas kernels, body(): first_rows, second_rows, every = ship(slots, counts, x)  78.3 us
    pallas_call x1, Pallas kernels, body(): pl.pallas_call(functools.partial(bring_kernel, cap, n, CHUNKS[0]), in_spe...  74.5 us
    pallas_call x1, Pallas kernels, body(): pl.pallas_call(functools.partial(combine_kernel, cap, start, size, n), gr...  15.2 us
  transfers between devices with their start and end apart: 2, of which 0 were waited for; matrix products, arithmetic and copies ran while one was open for 1% of the time, Pallas kernels for 47%

profile of v7, /device:TPU:11, one launch (start us, length us, event | category | flops | bytes accessed | tf_op | source)
XLA Modules:
  0.0 344.2 jit_solution(320537707507710710)
XLA Ops:
  0.0 4.6 %route.1 = (s32[8,2048]{1,0:T(8,128)}, f32[2048,8]{1,0:T(8,128)}, s32[32,128]{1,0:T(8,128)}) custom-call(bf16[2048,768]{1,0:T(8,128)(2,1)} %x_ref.3, f32[32,768]{1,0:T(8,128)} %bitcast.12, s32[2,2048]{1,0:T(2,128)} %bitcast.13), custom_call_target="tpu_custom_call" | custom-call | tf_op jit(solution)/shard_map/route/pallas_call | solution.py:481
  4.6 78.3 %ship.1 = (bf16[16,256,768]{2,1,0:T(8,128)(2,1)}, bf16[16,256,768]{2,1,0:T(8,128)(2,1)}, s32[16,32,128]{2,1,0:T(8,128)}) custom-call(s32[8,2048]{1,0:T(8,128)} %get-tuple-element.15.slot_ref, s32[32,128]{1,0:T(8,128)} %get-tuple-element.13.cnt_ref, bf16[2048,768]{1,0:T(8,128)(2,1)} %x_ref.3), custom_call_target="tpu_custom_call" | custom-call | flops 99999997952 | bytes 1 | tf_op jit(solution)/shard_map/ship/pallas_call | solution.py:518
  82.9 5.0 %all-to-all-start = ((bf16[16,256,768]{2,1,0:T(8,128)(2,1)}), bf16[16,256,768]{2,1,0:T(8,128)(2,1)}, u32[]{:S(2)}, u32[]{:S(2)}) async-start(bf16[16,256,768]{2,1,0:T(8,128)(2,1)} %get-tuple-element.17), calls=%async_computation | async-start | bytes 12582912 | tf_op jit(solution)/shard_map/all_to_all | solution.py:527
  88.0 0.8 constant_dynamic-slice_fusion
  88.8 0.1 copy.8
  88.9 0.6 concatenate.3.bound_ref
  89.5 79.3 %shard_map.65 = bf16[4096,768]{1,0:T(8,128)(2,1)} custom-call(s32[3,16]{1,0:T(4,128)} %concatenate.3.bound_ref, bf16[4096,768]{1,0:T(8,128)(2,1)} %bitcast.16, bf16[2,768,3072]{2,1,0:T(8,128)(2,1)} %w1_hbm.3, bf16[2,768,3072]{2,1,0:T(8,128)(2,1)} %w3_hbm.3, bf16[2,3072,768]{2,1,0:T(8,128)(2,1)} %w2_hbm.3), custom_call_target="tpu_custom_call" | custom-call | flops 57982058496 | bytes 1 | tf_op jit(solution)/shard_map/pallas_call | solution.py:551
  168.8 0.0 all-to-all-done
  168.8 0.0 copy-start
  168.8 3.5 %all-to-all-start.1 = ((bf16[16,256,768]{2,1,0:T(8,128)(2,1)}), bf16[16,256,768]{2,1,0:T(8,128)(2,1)}, u32[]{:S(2)}, u32[]{:S(2)}) async-start(bf16[16,256,768]{2,1,0:T(8,128)(2,1)} %bitcast.11), calls=%async_computation.1 | async-start | bytes 12582912 | tf_op jit(solution)/shard_map/all_to_all | solution.py:553
  172.3 0.0 copy-done
  172.3 0.1 slice_reduce_fusion
  172.4 0.1 reshape_squeeze.3
  172.5 0.7 reduce_sum.9.counts_ref
  173.3 81.0 %shard_map.64 = bf16[4096,768]{1,0:T(8,128)(2,1)} custom-call(s32[3,16]{1,0:T(4,128)} %concatenate.3.bound_ref, bf16[4096,768]{1,0:T(8,128)(2,1)} %bitcast.4.x_hbm, bf16[2,768,3072]{2,1,0:T(8,128)(2,1)} %w1_hbm.3, bf16[2,768,3072]{2,1,0:T(8,128)(2,1)} %w3_hbm.3, bf16[2,3072,768]{2,1,0:T(8,128)(2,1)} %w2_hbm.3), custom_call_target="tpu_custom_call" | custom-call | flops 57982058496 | bytes 1 | tf_op jit(solution)/shard_map/pallas_call | solution.py:551
  254.3 0.0 all-to-all-done.1
  254.3 74.5 %bring.1 = (bf16[16,256,768]{2,1,0:T(8,128)(2,1)}, f32[2048,768]{1,0:T(8,128)}) custom-call(bf16[16,256,768]{2,1,0:T(8,128)(2,1)} %bitcast.17, bf16[4096,768]{1,0:T(8,128)(2,1)} %bitcast.8.back_hbm, f32[2048,8]{1,0:T(8,128)} %get-tuple-element.14.cols_ref), custom_call_target="tpu_custom_call" | custom-call | flops 99999997952 | bytes 1 | tf_op jit(solution)/shard_map/bring/pallas_call | solution.py:556
  328.9 15.2 %combine.1 = bf16[2048,768]{1,0:T(8,128)(2,1)} custom-call(s32[16]{0:T(128)} %reduce_sum.9.counts_ref, f32[2048,8]{1,0:T(8,128)} %get-tuple-element.14.cols_ref, bf16[4096,768]{1,0:T(8,128)(2,1)} %bitcast.10, f32[2048,768]{1,0:T(8,128)} %get-tuple-element.20.acc_ref), custom_call_target="tpu_custom_call" | custom-call | tf_op jit(solution)/shard_map/combine/pallas_call | solution.py:578
  (1 shorter events, 0.0 us)
Async XLA Ops:
  82.9 85.9 %all-to-all-start = ((bf16[16,256,768]{2,1,0:T(8,128)(2,1)}), bf16[16,256,768]{2,1,0:T(8,128)(2,1)}, u32[]{:S(2)}, u32[]{:S(2)}) async-start(bf16[16,256,768]{2,1,0:T(8,128)(2,1)} %get-tuple-element.17), calls=%async_computation | async-start | bytes 12582912 | tf_op jit(solution)/shard_map/all_to_all | solution.py:527
  168.8 3.5 %copy-start = (s32[32,128]{1,0:T(8,128)S(1)}, s32[32,128]{1,0:T(8,128)}, u32[]{:S(2)}) copy-start(s32[32,128]{1,0:T(8,128)} %get-tuple-element.13.cnt_ref) | copy-start | bytes 49156
  168.8 85.5 %all-to-all-start.1 = ((bf16[16,256,768]{2,1,0:T(8,128)(2,1)}), bf16[16,256,768]{2,1,0:T(8,128)(2,1)}, u32[]{:S(2)}, u32[]{:S(2)}) async-start(bf16[16,256,768]{2,1,0:T(8,128)(2,1)} %bitcast.11), calls=%async_computation.1 | async-start | bytes 12582912 | tf_op jit(solution)/shard_map/all_to_all | solution.py:553

commit v8 on v7

--- a/solution.py
+++ b/solution.py
@@ -69,32 +69,6 @@
     cols_ref[...] = both.T
 
 
-SLOT_TILE = 32
-SUM_GROUP = 16
-
-
-def list_tiles(n_dev, size, start, counts_ref, list_ref, visit=None):
-    per = size // SLOT_TILE
-
-    def collect(i, cnt):
-        hit = counts_ref[i // per] > start + (i % per) * SLOT_TILE
-
-        @pl.when(hit)
-        def _():
-            list_ref[cnt] = i
-            if visit is not None:
-                visit(i, cnt)
-
-        return cnt + hit.astype(I32)
-
-    return lax.fori_loop(0, n_dev * per, collect, jnp.int32(0))
-
-
-def first_slot(i, size, start, row_cap):
-    per = size // SLOT_TILE
-    return (i // per) * row_cap + start + (i % per) * SLOT_TILE
-
-
 WIDE = 512
 GROUP = 16
 STEP = GROUP * TILE
@@ -343,16 +317,16 @@
     return add
 
 
-def bring_kernel(row_cap, n_dev, chunk, made_ref, back_hbm, cols_ref, got_ref, acc_ref, back, acc, send_sems, recv_sems, own_sem, back_sems, acc_sem):
+def bring_kernel(row_cap, n_dev, chunks, made_ref, back_hbm, cols_ref, out_ref, back, got, acc, send_sems, recv_sems, own_sem, back_sems):
     me = lax.axis_index("ep")
-    start, size = chunk
+    (start, size), (start1, size1) = chunks
     tok = cols_ref.shape[0]
     block = 512
 
     def send(k):
         return pltpu.make_async_remote_copy(
             src_ref=made_ref.at[partner(me, k)],
-            dst_ref=got_ref.at[me],
+            dst_ref=got.at[me],
             send_sem=send_sems.at[k],
             recv_sem=recv_sems.at[k],
             device_id=(partner(me, k),),
@@ -363,21 +337,54 @@
         at = pl.ds(pl.multiple_of(g * 2 * size, 2 * size), 2 * size)
         return pltpu.make_async_copy(back_hbm.at[at], back.at[at], back_sems.at[g])
 
+    def slots_of(chip, first, rows):
+        lane = lax.broadcasted_iota(I32, (1, 2 * rows), 1)
+        return ((2 * chip + lane // rows) * row_cap + first + lane % rows).astype(F32)
+
+    def each_block(body):
+        @pl.loop(0, tok // block)
+        def _(t):
+            body(pl.ds(pl.multiple_of(t * block, block), block))
+
+    def first_group(g):
+        fetch(g).wait()
+        rows = back[pl.ds(pl.multiple_of(g * 2 * size, 2 * size), 2 * size), :]
+        ids = slots_of(g, start, size)
+
+        def add(at):
+            acc[at, :] += gated(cols_ref[at, :], ids, rows)
+
+        each_block(add)
+
+    def arrived(k):
+        chip = partner(me, k) // 2
+        rows = got[pl.ds(2 * chip, 2)].reshape(2 * size1, got.shape[2])
+        return rows, slots_of(chip, start1, size1)
+
+    def second_group(k):
+        rows, ids = arrived(k)
+
+        def add(at):
+            acc[at, :] += gated(cols_ref[at, :], ids, rows)
+
+        each_block(add)
+
     barrier = pltpu.get_barrier_semaphore()
     for k in range(1, n_dev):
         pl.semaphore_signal(barrier, inc=1, device_id=(partner(me, k),), device_id_type=MESH)
+    groups = n_dev // 2
+
+    @pl.loop(0, groups)
+    def _(g):
+        fetch(g).start()
+
     acc[...] = jnp.zeros_like(acc)
     pl.semaphore_wait(barrier, n_dev - 1)
     send(14).start()
     send(15).start()
     send(1).start()
-    own = pltpu.make_async_copy(made_ref.at[me], got_ref.at[me], own_sem)
+    own = pltpu.make_async_copy(made_ref.at[me], got.at[me], own_sem)
     own.start()
-    groups = n_dev // 2
-
-    @pl.loop(0, groups)
-    def _(g):
-        fetch(g).start()
 
     @pl.loop(1, 7)
     def _(p):
@@ -397,72 +404,44 @@
 
         @pl.loop((groups * (p - 1)) // 6, (groups * p) // 6)
         def _(g):
-            fetch(g).wait()
-            rows = back[pl.ds(pl.multiple_of(g * 2 * size, 2 * size), 2 * size), :]
-            lane = lax.broadcasted_iota(I32, (1, 2 * size), 1)
-            ids = ((2 * g + lane // size) * row_cap + start + lane % size).astype(F32)
-
-            @pl.loop(0, tok // block)
-            def _(t):
-                at = pl.ds(pl.multiple_of(t * block, block), block)
-                acc[at, :] += gated(cols_ref[at, :], ids, rows)
-
-    out = pltpu.make_async_copy(acc, acc_ref, acc_sem)
+            first_group(g)
+
+        @pl.when((p >= 3) & (p <= 5))
+        def _():
+            base = jnp.where(p == 3, 14, jnp.where(p == 4, 6, 8))
+            send(base).wait_recv()
+            send(base + 1).wait_recv()
+            second_group(base)
+
+    own.wait()
+    send(1).wait_recv()
+
+    @pl.loop(0, 3)
+    def _(q):
+        base = jnp.where(q == 0, 0, jnp.where(q == 1, 10, 4))
+
+        @pl.when(q > 0)
+        def _():
+            send(base).wait_recv()
+            send(base + 1).wait_recv()
+
+        second_group(base)
+
+    for k in (12, 13, 2, 3):
+        send(k).wait_recv()
+    rows_a, ids_a = arrived(12)
+    rows_b, ids_b = arrived(2)
+
+    def finish(at):
+        cols = cols_ref[at, :]
+        total = acc[at, :] + gated(cols, ids_a, rows_a) + gated(cols, ids_b, rows_b)
+        out_ref[at, :] = total.astype(BF16)
+
+    each_block(finish)
     for p in (5, 6):
         for k in pair_of(p):
             send(k).wait_send()
-    out.start()
     send(1).wait_send()
-    own.wait()
-
-    @pl.loop(1, n_dev)
-    def _(k):
-        send(k).wait_recv()
-
-    out.wait()
-
-
-def combine_kernel(row_cap, start, size, n_dev, counts_ref, cols_ref, back_hbm, acc_ref, out_ref, rows_ref, sum_ref, list_ref, cnt_ref, sems):
-    group = SUM_GROUP * SLOT_TILE
-
-    def fetch(i, k):
-        src = pl.ds(pl.multiple_of(i * SLOT_TILE, SLOT_TILE), SLOT_TILE)
-        dst = pl.ds(pl.multiple_of(k * SLOT_TILE, SLOT_TILE), SLOT_TILE)
-        return pltpu.make_async_copy(back_hbm.at[src], rows_ref.at[dst], sems.at[k])
-
-    @pl.when(pl.program_id(0) == 0)
-    def _():
-        cnt = list_tiles(n_dev, size, start, counts_ref, list_ref, lambda i, k: fetch(i, k).start())
-        groups = (cnt + SUM_GROUP - 1) // SUM_GROUP
-        cnt_ref[0] = groups
-
-        @pl.loop(cnt, groups * SUM_GROUP)
-        def _(k):
-            list_ref[k] = -1
-            rows_ref[pl.ds(pl.multiple_of(k * SLOT_TILE, SLOT_TILE), SLOT_TILE), :] = jnp.zeros((SLOT_TILE, rows_ref.shape[1]), BF16)
-
-        @pl.loop(0, cnt)
-        def _(k):
-            fetch(list_ref[k], k).wait()
-
-    lane = lax.broadcasted_iota(I32, (1, group), 1)
-
-    def one(g, total):
-        ids = jnp.full((1, group), -1, I32)
-        for j in range(SUM_GROUP):
-            i = list_ref[g * SUM_GROUP + j]
-            base = jnp.where(i < 0, -1 - group, first_slot(i, size, start, row_cap))
-            ids = jnp.where(lane // SLOT_TILE == j, base + lane % SLOT_TILE, ids)
-        rows = rows_ref[pl.ds(pl.multiple_of(g * group, group), group), :]
-        return total + gated(cols_ref[...], ids.astype(F32), rows)
-
-    sum_ref[...] = acc_ref[...]
-
-    @pl.loop(0, cnt_ref[0])
-    def _(g):
-        sum_ref[...] = one(g, sum_ref[...])
-
-    out_ref[...] = sum_ref[...].astype(out_ref.dtype)
 
 
 def _params(vmem_limit_bytes=VMEM_BYTES):
@@ -488,7 +467,6 @@
             compiler_params=_params(),
             name="route",
         )(x, w_router.T, ids.T)
-        dev_counts = jnp.sum(counts[:, 0].reshape(n, local), axis=1)
         smem = pl.BlockSpec(memory_space=pltpu.SMEM)
         vmem = pl.BlockSpec(memory_space=pltpu.VMEM)
         hbm = pl.BlockSpec(memory_space=pl.ANY)
@@ -551,49 +529,26 @@
             made = made(bounds, got.reshape(rows, dim), w1, w3, w2)
             if index == 0:
                 back = lax.all_to_all(made.reshape(n, size, dim), "ep", 0, 0, tiled=True)
-        start, size = CHUNKS[1]
-        rows = n * size
-        got, acc = pl.pallas_call(
-            functools.partial(bring_kernel, cap, n, CHUNKS[0]),
+        return pl.pallas_call(
+            functools.partial(bring_kernel, cap, n, CHUNKS),
             in_specs=[hbm, hbm, vmem],
-            out_specs=[hbm, hbm],
-            out_shape=[jax.ShapeDtypeStruct((n, size, dim), BF16), jax.ShapeDtypeStruct((tok, dim), F32)],
+            out_specs=vmem,
+            out_shape=jax.ShapeDtypeStruct((tok, dim), BF16),
             scratch_shapes=[
                 pltpu.VMEM((n * CHUNKS[0][1], dim), BF16),
+                pltpu.VMEM((n, CHUNKS[1][1], dim), BF16),
                 pltpu.VMEM((tok, dim), F32),
                 pltpu.SemaphoreType.DMA((n,)),
                 pltpu.SemaphoreType.DMA((n,)),
                 pltpu.SemaphoreType.DMA,
                 pltpu.SemaphoreType.DMA((n // 2,)),
-                pltpu.SemaphoreType.DMA,
             ],
             compiler_params=pltpu.CompilerParams(
                 vmem_limit_bytes=VMEM_BYTES, collective_id=1, has_side_effects=True
             ),
             cost_estimate=pl.CostEstimate(flops=10**11, bytes_accessed=1, transcendentals=0),
             name="bring",
-        )(made.reshape(n, size, dim), back.reshape(n * CHUNKS[0][1], dim), cols)
-        tb = 512
-        tile_spec = pl.BlockSpec((tb, dim), lambda i, c: (i, 0))
-        return pl.pallas_call(
-            functools.partial(combine_kernel, cap, start, size, n),
-            grid_spec=pltpu.PrefetchScalarGridSpec(
-                num_scalar_prefetch=1,
-                grid=(tok // tb,),
-                in_specs=[pl.BlockSpec((tb, 8), lambda i, c: (i, 0)), hbm, tile_spec],
-                out_specs=tile_spec,
-                scratch_shapes=[
-                    pltpu.VMEM((rows, dim), BF16),
-                    pltpu.VMEM((tb, dim), F32),
-                    pltpu.SMEM((rows // SLOT_TILE,), I32),
-                    pltpu.SMEM((1,), I32),
-                    pltpu.SemaphoreType.DMA((rows // SLOT_TILE,)),
-                ],
-            ),
-            out_shape=jax.ShapeDtypeStruct((tok, dim), BF16),
-            compiler_params=_params(),
-            name="combine",
-        )(dev_counts, cols, got.reshape(rows, dim), acc)
+        )(made.reshape(n, CHUNKS[1][1], dim), back.reshape(n * CHUNKS[0][1], dim), cols)
 
     return jax.shard_map(
         body,

time: 348 us -> 354 us (1.017)
  Pallas kernels: 333 us -> 337 us
  local copies, waits for them, and re-layouts: 1.73 us -> 5.3 us
    pallas_call x2 -> x1, Pallas kernels: 89.7 us -> 94.1 us  [body(): pl.pallas_call(functools.partial(bring_kernel, cap, n, CHUNKS), in_specs=...]
    unnamed x2 -> x1, local copies, waits for them, and re-layouts: 0.01 us -> 3.76 us
  transfers between devices with their start and end apart: 2 -> 2, of which waited for: 0 -> 0; matrix products, arithmetic and copies ran while one was open for 1% -> 0% of each run, Pallas kernels for 47% -> 46%
where the time goes in v8:
time: 354 us; the launch traced here: 351 us
  Pallas kernels  337 us (95%)
  starting transfers between devices  8.49 us (2%)
  local copies, waits for them, and re-layouts  5.3 us (1%)
    pallas_call x2, Pallas kernels, body(): made = made(bounds, got.reshape(rows, dim), w1, w3, w2)  160 us
    pallas_call x1, Pallas kernels, body(): pl.pallas_call(functools.partial(bring_kernel, cap, n, CHUNKS), in_specs=...  94.1 us
    pallas_call x1, Pallas kernels, body(): first_rows, second_rows, every = ship(slots, counts, x)  78.3 us
  transfers between devices with their start and end apart: 2, of which 0 were waited for; matrix products, arithmetic and copies ran while one was open for 0% of the time, Pallas kernels for 46%

profile of v8, /device:TPU:11, one launch (start us, length us, event | category | flops | bytes accessed | tf_op | source)
XLA Modules:
  0.0 351.1 jit_solution(8302710298459911625)
XLA Ops:
  0.0 4.5 %route.1 = (s32[8,2048]{1,0:T(8,128)}, f32[2048,8]{1,0:T(8,128)}, s32[32,128]{1,0:T(8,128)}) custom-call(bf16[2048,768]{1,0:T(8,128)(2,1)} %x_ref.3, f32[32,768]{1,0:T(8,128)} %bitcast.10, s32[2,2048]{1,0:T(2,128)} %bitcast.11), custom_call_target="tpu_custom_call" | custom-call | tf_op jit(solution)/shard_map/route/pallas_call | solution.py:460
  4.5 78.3 %ship.1 = (bf16[16,256,768]{2,1,0:T(8,128)(2,1)}, bf16[16,256,768]{2,1,0:T(8,128)(2,1)}, s32[16,32,128]{2,1,0:T(8,128)}) custom-call(s32[8,2048]{1,0:T(8,128)} %get-tuple-element.11.slot_ref, s32[32,128]{1,0:T(8,128)} %get-tuple-element.12.cnt_ref, bf16[2048,768]{1,0:T(8,128)(2,1)} %x_ref.3), custom_call_target="tpu_custom_call" | custom-call | flops 99999997952 | bytes 1 | tf_op jit(solution)/shard_map/ship/pallas_call | solution.py:496
  82.8 5.0 %all-to-all-start = ((bf16[16,256,768]{2,1,0:T(8,128)(2,1)}), bf16[16,256,768]{2,1,0:T(8,128)(2,1)}, u32[]{:S(2)}, u32[]{:S(2)}) async-start(bf16[16,256,768]{2,1,0:T(8,128)(2,1)} %get-tuple-element.14), calls=%async_computation | async-start | bytes 12582912 | tf_op jit(solution)/shard_map/all_to_all | solution.py:505
  87.9 0.8 constant_dynamic-slice_fusion
  88.7 0.1 copy.7
  88.8 0.6 concatenate.3.bound_ref
  89.5 79.3 %shard_map.65 = bf16[4096,768]{1,0:T(8,128)(2,1)} custom-call(s32[3,16]{1,0:T(4,128)} %concatenate.3.bound_ref, bf16[4096,768]{1,0:T(8,128)(2,1)} %bitcast.14, bf16[2,768,3072]{2,1,0:T(8,128)(2,1)} %w1_hbm.3, bf16[2,768,3072]{2,1,0:T(8,128)(2,1)} %w3_hbm.3, bf16[2,3072,768]{2,1,0:T(8,128)(2,1)} %w2_hbm.3), custom_call_target="tpu_custom_call" | custom-call | flops 57982058496 | bytes 1 | tf_op jit(solution)/shard_map/pallas_call | solution.py:529
  168.7 0.0 all-to-all-done
  168.7 3.5 all-to-all-start.1
  172.2 81.0 %shard_map.64 = bf16[4096,768]{1,0:T(8,128)(2,1)} custom-call(s32[3,16]{1,0:T(4,128)} %concatenate.3.bound_ref, bf16[4096,768]{1,0:T(8,128)(2,1)} %bitcast.4.x_hbm, bf16[2,768,3072]{2,1,0:T(8,128)(2,1)} %w1_hbm.3, bf16[2,768,3072]{2,1,0:T(8,128)(2,1)} %w3_hbm.3, bf16[2,3072,768]{2,1,0:T(8,128)(2,1)} %w2_hbm.3), custom_call_target="tpu_custom_call" | custom-call | flops 57982058496 | bytes 1 | tf_op jit(solution)/shard_map/pallas_call | solution.py:529
  253.2 0.0 all-to-all-done.1
  253.3 94.1 %bring.1 = bf16[2048,768]{1,0:T(8,128)(2,1)} custom-call(bf16[16,256,768]{2,1,0:T(8,128)(2,1)} %bitcast.15, bf16[4096,768]{1,0:T(8,128)(2,1)} %bitcast.8.back_hbm, f32[2048,8]{1,0:T(8,128)} %get-tuple-element.16.cols_ref), custom_call_target="tpu_custom_call" | custom-call | flops 99999997952 | bytes 1 | tf_op jit(solution)/shard_map/bring/pallas_call | solution.py:532
  347.4 3.8 %copy.9 = bf16[2048,768]{1,0:T(8,128)(2,1)} copy(bf16[2048,768]{1,0:T(8,128)(2,1)} %bring.1) | data formatting | bytes 6291456
  (1 shorter events, 0.0 us)
Async XLA Ops:
  82.8 85.9 %all-to-all-start = ((bf16[16,256,768]{2,1,0:T(8,128)(2,1)}), bf16[16,256,768]{2,1,0:T(8,128)(2,1)}, u32[]{:S(2)}, u32[]{:S(2)}) async-start(bf16[16,256,768]{2,1,0:T(8,128)(2,1)} %get-tuple-element.14), calls=%async_computation | async-start | bytes 12582912 | tf_op jit(solution)/shard_map/all_to_all | solution.py:505
  168.7 84.5 %all-to-all-start.1 = ((bf16[16,256,768]{2,1,0:T(8,128)(2,1)}), bf16[16,256,768]{2,1,0:T(8,128)(2,1)}, u32[]{:S(2)}, u32[]{:S(2)}) async-start(bf16[16,256,768]{2,1,0:T(8,128)(2,1)} %bitcast.9), calls=%async_computation.1 | async-start | bytes 12582912 | tf_op jit(solution)/shard_map/all_to_all | solution.py:531

commit v9 on v8

--- a/solution.py
+++ b/solution.py
@@ -317,7 +317,7 @@
     return add
 
 
-def bring_kernel(row_cap, n_dev, chunks, made_ref, back_hbm, cols_ref, out_ref, back, got, acc, send_sems, recv_sems, own_sem, back_sems):
+def bring_kernel(row_cap, n_dev, chunks, made_ref, back_hbm, cols_ref, out_ref, back, got, acc, rows_ref, send_sems, recv_sems, own_sem, back_sems):
     me = lax.axis_index("ep")
     (start, size), (start1, size1) = chunks
     tok = cols_ref.shape[0]
@@ -337,38 +337,6 @@
         at = pl.ds(pl.multiple_of(g * 2 * size, 2 * size), 2 * size)
         return pltpu.make_async_copy(back_hbm.at[at], back.at[at], back_sems.at[g])
 
-    def slots_of(chip, first, rows):
-        lane = lax.broadcasted_iota(I32, (1, 2 * rows), 1)
-        return ((2 * chip + lane // rows) * row_cap + first + lane % rows).astype(F32)
-
-    def each_block(body):
-        @pl.loop(0, tok // block)
-        def _(t):
-            body(pl.ds(pl.multiple_of(t * block, block), block))
-
-    def first_group(g):
-        fetch(g).wait()
-        rows = back[pl.ds(pl.multiple_of(g * 2 * size, 2 * size), 2 * size), :]
-        ids = slots_of(g, start, size)
-
-        def add(at):
-            acc[at, :] += gated(cols_ref[at, :], ids, rows)
-
-        each_block(add)
-
-    def arrived(k):
-        chip = partner(me, k) // 2
-        rows = got[pl.ds(2 * chip, 2)].reshape(2 * size1, got.shape[2])
-        return rows, slots_of(chip, start1, size1)
-
-    def second_group(k):
-        rows, ids = arrived(k)
-
-        def add(at):
-            acc[at, :] += gated(cols_ref[at, :], ids, rows)
-
-        each_block(add)
-
     barrier = pltpu.get_barrier_semaphore()
     for k in range(1, n_dev):
         pl.semaphore_signal(barrier, inc=1, device_id=(partner(me, k),), device_id_type=MESH)
@@ -385,11 +353,10 @@
     send(1).start()
     own = pltpu.make_async_copy(made_ref.at[me], got.at[me], own_sem)
     own.start()
-
-    @pl.loop(1, 7)
+    lane = lax.broadcasted_iota(I32, (1, 2 * size), 1)
+
+    @pl.loop(1, 9)
     def _(p):
-        k0, k1 = pair_of(p)
-
         @pl.when(p <= 2)
         def _():
             send(13 + p).wait_send()
@@ -399,48 +366,48 @@
             for k in pair_of(p - 2):
                 send(k).wait_send()
 
-        send(k0).start()
-        send(k1).start()
-
-        @pl.loop((groups * (p - 1)) // 6, (groups * p) // 6)
+        @pl.when(p <= 6)
+        def _():
+            for k in pair_of(p):
+                send(k).start()
+
+        low = jnp.minimum((groups * (p - 1)) // 6, groups)
+        high = jnp.minimum((groups * p) // 6, groups)
+        near, far = pair_of(p - 2)
+        k0 = jnp.where(p == 1, 0, jnp.where(p == 2, 14, near))
+        k1 = jnp.where(p == 1, 1, jnp.where(p == 2, 15, far))
+        d0, d1 = partner(me, k0), partner(me, k1)
+
+        @pl.loop(low, high + 1)
         def _(g):
-            first_group(g)
-
-        @pl.when((p >= 3) & (p <= 5))
-        def _():
-            base = jnp.where(p == 3, 14, jnp.where(p == 4, 6, 8))
-            send(base).wait_recv()
-            send(base + 1).wait_recv()
-            second_group(base)
-
-    own.wait()
-    send(1).wait_recv()
-
-    @pl.loop(0, 3)
-    def _(q):
-        base = jnp.where(q == 0, 0, jnp.where(q == 1, 10, 4))
-
-        @pl.when(q > 0)
-        def _():
-            send(base).wait_recv()
-            send(base + 1).wait_recv()
-
-        second_group(base)
-
-    for k in (12, 13, 2, 3):
-        send(k).wait_recv()
-    rows_a, ids_a = arrived(12)
-    rows_b, ids_b = arrived(2)
-
-    def finish(at):
-        cols = cols_ref[at, :]
-        total = acc[at, :] + gated(cols, ids_a, rows_a) + gated(cols, ids_b, rows_b)
-        out_ref[at, :] = total.astype(BF16)
-
-    each_block(finish)
-    for p in (5, 6):
-        for k in pair_of(p):
-            send(k).wait_send()
+            @pl.when(g < high)
+            def _():
+                fetch(g).wait()
+                rows_ref[...] = back[pl.ds(pl.multiple_of(g * 2 * size, 2 * size), 2 * size), :]
+
+            @pl.when(g == high)
+            def _():
+                @pl.when(p == 1)
+                def _():
+                    own.wait()
+
+                @pl.when(p > 1)
+                def _():
+                    send(k0).wait_recv()
+
+                send(k1).wait_recv()
+                rows_ref[:size1, :] = got[d0]
+                rows_ref[size1:, :] = got[d1]
+
+            at0 = jnp.where(g < high, 2 * g * row_cap + start, d0 * row_cap + start1)
+            at1 = jnp.where(g < high, (2 * g + 1) * row_cap + start, d1 * row_cap + start1)
+            ids = jnp.where(lane < size, at0 + lane, at1 + lane - size).astype(F32)
+            rows = rows_ref[...]
+            for t in range(tok // block):
+                at = slice(t * block, (t + 1) * block)
+                acc[at, :] += gated(cols_ref[at, :], ids, rows)
+
+    out_ref[...] = acc[...].astype(BF16)
     send(1).wait_send()
 
 
@@ -538,6 +505,7 @@
                 pltpu.VMEM((n * CHUNKS[0][1], dim), BF16),
                 pltpu.VMEM((n, CHUNKS[1][1], dim), BF16),
                 pltpu.VMEM((tok, dim), F32),
+                pltpu.VMEM((2 * CHUNKS[0][1], dim), BF16),
                 pltpu.SemaphoreType.DMA((n,)),
                 pltpu.SemaphoreType.DMA((n,)),
                 pltpu.SemaphoreType.DMA,

time: 354 us -> 343 us (0.969)
  Pallas kernels: 337 us -> 326 us
    pallas_call x1, Pallas kernels: 94.1 us -> 82.7 us  [body(): pl.pallas_call(functools.partial(bring_kernel, cap, n, CHUNKS), in_specs=...]
  transfers between devices with their start and end apart: 2 -> 2, of which waited for: 0 -> 0; matrix products, arithmetic and copies ran while one was open for 0% -> 0% of each run, Pallas kernels for 46% -> 47%
where the time goes in v9:
time: 343 us; the launch traced here: 340 us
  Pallas kernels  326 us (95%)
  starting transfers between devices  8.49 us (2%)
  local copies, waits for them, and re-layouts  5.3 us (2%)
    pallas_call x2, Pallas kernels, body(): made = made(bounds, got.reshape(rows, dim), w1, w3, w2)  160 us
    pallas_call x1, Pallas kernels, body(): pl.pallas_call(functools.partial(bring_kernel, cap, n, CHUNKS), in_specs=...  82.7 us
    pallas_call x1, Pallas kernels, body(): first_rows, second_rows, every = ship(slots, counts, x)  78.3 us
  transfers between devices with their start and end apart: 2, of which 0 were waited for; matrix products, arithmetic and copies ran while one was open for 0% of the time, Pallas kernels for 47%

profile of v9, /device:TPU:11, one launch (start us, length us, event | category | flops | bytes accessed | tf_op | source)
XLA Modules:
  0.0 339.7 jit_solution(17889955532204676873)
XLA Ops:
  0.0 4.5 %route.1 = (s32[8,2048]{1,0:T(8,128)}, f32[2048,8]{1,0:T(8,128)}, s32[32,128]{1,0:T(8,128)}) custom-call(bf16[2048,768]{1,0:T(8,128)(2,1)} %x_ref.3, f32[32,768]{1,0:T(8,128)} %bitcast.10, s32[2,2048]{1,0:T(2,128)} %bitcast.11), custom_call_target="tpu_custom_call" | custom-call | tf_op jit(solution)/shard_map/route/pallas_call | solution.py:427
  4.5 78.3 %ship.1 = (bf16[16,256,768]{2,1,0:T(8,128)(2,1)}, bf16[16,256,768]{2,1,0:T(8,128)(2,1)}, s32[16,32,128]{2,1,0:T(8,128)}) custom-call(s32[8,2048]{1,0:T(8,128)} %get-tuple-element.11.slot_ref, s32[32,128]{1,0:T(8,128)} %get-tuple-element.12.cnt_ref, bf16[2048,768]{1,0:T(8,128)(2,1)} %x_ref.3), custom_call_target="tpu_custom_call" | custom-call | flops 99999997952 | bytes 1 | tf_op jit(solution)/shard_map/ship/pallas_call | solution.py:463
  82.8 5.0 %all-to-all-start = ((bf16[16,256,768]{2,1,0:T(8,128)(2,1)}), bf16[16,256,768]{2,1,0:T(8,128)(2,1)}, u32[]{:S(2)}, u32[]{:S(2)}) async-start(bf16[16,256,768]{2,1,0:T(8,128)(2,1)} %get-tuple-element.14), calls=%async_computation | async-start | bytes 12582912 | tf_op jit(solution)/shard_map/all_to_all | solution.py:472
  87.9 0.8 constant_dynamic-slice_fusion
  88.7 0.1 copy.7
  88.8 0.6 concatenate.3.bound_ref
  89.5 79.3 %shard_map.65 = bf16[4096,768]{1,0:T(8,128)(2,1)} custom-call(s32[3,16]{1,0:T(4,128)} %concatenate.3.bound_ref, bf16[4096,768]{1,0:T(8,128)(2,1)} %bitcast.14, bf16[2,768,3072]{2,1,0:T(8,128)(2,1)} %w1_hbm.3, bf16[2,768,3072]{2,1,0:T(8,128)(2,1)} %w3_hbm.3, bf16[2,3072,768]{2,1,0:T(8,128)(2,1)} %w2_hbm.3), custom_call_target="tpu_custom_call" | custom-call | flops 57982058496 | bytes 1 | tf_op jit(solution)/shard_map/pallas_call | solution.py:496
  168.7 0.0 all-to-all-done
  168.7 3.5 %all-to-all-start.1 = ((bf16[16,256,768]{2,1,0:T(8,128)(2,1)}), bf16[16,256,768]{2,1,0:T(8,128)(2,1)}, u32[]{:S(2)}, u32[]{:S(2)}) async-start(bf16[16,256,768]{2,1,0:T(8,128)(2,1)} %bitcast.9), calls=%async_computation.1 | async-start | bytes 12582912 | tf_op jit(solution)/shard_map/all_to_all | solution.py:498
  172.2 81.0 %shard_map.64 = bf16[4096,768]{1,0:T(8,128)(2,1)} custom-call(s32[3,16]{1,0:T(4,128)} %concatenate.3.bound_ref, bf16[4096,768]{1,0:T(8,128)(2,1)} %bitcast.4.x_hbm, bf16[2,768,3072]{2,1,0:T(8,128)(2,1)} %w1_hbm.3, bf16[2,768,3072]{2,1,0:T(8,128)(2,1)} %w3_hbm.3, bf16[2,3072,768]{2,1,0:T(8,128)(2,1)} %w2_hbm.3), custom_call_target="tpu_custom_call" | custom-call | flops 57982058496 | bytes 1 | tf_op jit(solution)/shard_map/pallas_call | solution.py:496
  253.2 0.0 all-to-all-done.1
  253.3 82.7 %bring.1 = bf16[2048,768]{1,0:T(8,128)(2,1)} custom-call(bf16[16,256,768]{2,1,0:T(8,128)(2,1)} %bitcast.15, bf16[4096,768]{1,0:T(8,128)(2,1)} %bitcast.8.back_hbm, f32[2048,8]{1,0:T(8,128)} %get-tuple-element.16.cols_ref), custom_call_target="tpu_custom_call" | custom-call | flops 99999997952 | bytes 1 | tf_op jit(solution)/shard_map/bring/pallas_call | solution.py:499
  336.0 3.8 %copy.9 = bf16[2048,768]{1,0:T(8,128)(2,1)} copy(bf16[2048,768]{1,0:T(8,128)(2,1)} %bring.1) | data formatting | bytes 6291456
  (1 shorter events, 0.0 us)
Async XLA Ops:
  82.8 85.9 %all-to-all-start = ((bf16[16,256,768]{2,1,0:T(8,128)(2,1)}), bf16[16,256,768]{2,1,0:T(8,128)(2,1)}, u32[]{:S(2)}, u32[]{:S(2)}) async-start(bf16[16,256,768]{2,1,0:T(8,128)(2,1)} %get-tuple-element.14), calls=%async_computation | async-start | bytes 12582912 | tf_op jit(solution)/shard_map/all_to_all | solution.py:472
  168.7 84.5 %all-to-all-start.1 = ((bf16[16,256,768]{2,1,0:T(8,128)(2,1)}), bf16[16,256,768]{2,1,0:T(8,128)(2,1)}, u32[]{:S(2)}, u32[]{:S(2)}) async-start(bf16[16,256,768]{2,1,0:T(8,128)(2,1)} %bitcast.9), calls=%async_computation.1 | async-start | bytes 12582912 | tf_op jit(solution)/shard_map/all_to_all | solution.py:498
